TPU v7x, 128 devices: a whole 4x4x4 slice. The times are simulated.
128 devices in a mesh: grp: 4 (over z), kv: 16 (over x, y), tp: 2 (over core).
Axes of the slice: x: 4, y: 4, z: 4, core: 2. Of those that a mesh axis runs over, the one named last changes fastest.
Arguments:
- hidden_states: bfloat16 [512, 4096], P('grp', 'kv'), may hold values from -6 to 6
- attn_gain: float32 [4096], P('kv'), may hold values from 0.25 to 1.75
- mlp_gain: float32 [4096], replicated, may hold values from 0.25 to 1.75
- w_query: bfloat16 [4096, 4096], P('kv', 'tp'), may hold values from -0.09375 to 0.09375
- w_out: bfloat16 [32, 128, 4096], P('tp', 'kv'), may hold values from -1 to 1
- w_gate: bfloat16 [4096, 14336], P(None, ('kv', 'tp')), may hold values from -0.09375 to 0.09375
- w_up: bfloat16 [4096, 14336], P(None, ('kv', 'tp')), may hold values from -0.09375 to 0.09375
- w_down: bfloat16 [14336, 4096], P(('kv', 'tp')), may hold values from -0.046875 to 0.046875
- kv_pool: bfloat16 [1024, 2, 128, 1024], P(('grp', 'kv'), None, None, 'tp'), may hold values from -110 to 110
- resident_cache: bfloat16 [4, 128, 2, 128, 1024], P('grp', 'kv', None, None, 'tp'), may hold values from -110 to 110
- resident_slot: int32 [4, 128], P('grp', 'kv'), may hold values from 0 to 127
- resident_len: int32 [4, 128], P('grp', 'kv'), may hold values from 1 to 128
- new_owner: int32 [4, 256], replicated, may hold values from 0 to 63, as said below
- new_local: int32 [4, 256], replicated, may hold values from 0 to 15
- new_slot: int32 [4, 256], P('grp', 'kv'), may hold values from 0 to 127
- new_len: int32 [4, 256], P('grp', 'kv'), may hold values from 1 to 128
- token_kv: bfloat16 [512, 2, 1024], P('grp', None, 'tp'), may hold values from -6 to 6
Outputs:
- mixed: bfloat16 [512, 4096], P(('grp', 'kv', 'tp'))
- new_cache: bfloat16 [4, 256, 2, 128, 1024], P('grp', 'kv', None, None, 'tp')
Inputs may be any that keep to these rules, and one draw needn't show every extreme that they name: New page c of group g is kept by the device of kv index c // 16 of group g and comes from the device whose index along grp+kv is new_owner[g, c]; every decode device receives exactly 4 new pages from the owners of each grp index; no owner sends more than 1 pages to the devices of one kv index over all groups, so at most 1 to one device; every owner sends each of its 16 pages exactly once.
All inputs are finite; a program needn't handle non-finite values.
Results may differ from a plain program's by a relative error of at most 0.018.
Values may be sent and summed in bfloat16 or wider, within the bound.
A program may use at most 128 MiB of HBM per device.

v0:
```python
import jax
import jax.numpy as jnp
from jax import lax
from jax.sharding import Mesh
from jax.sharding import PartitionSpec as P

D = 4096
HEADS = 32
KV_HEADS = 8
HEAD_DIM = 128
NPR = 4
KV = ("kv_0", "kv_1")
KV_TP = ("kv_0", "kv_1", "tp")
GRP_KV = ("grp", "kv_0", "kv_1")
GRP_KV_TP = ("grp", "kv_0", "kv_1", "tp")


neg_fill = -1e30
norm_eps = 1e-05


def combined_by_axis(shard, axes, combine):
    for axis in axes:
        pieces = jax.tree.map(lambda part: lax.all_gather(part, axis), shard)
        shard = jax.tree.map(lambda part: part[0], pieces)
        for k in range(1, lax.axis_size(axis)):
            shard = combine(shard, jax.tree.map(lambda part: part[k], pieces))
    return shard


def split_up(shard, dim, peers):
    before, after = (shard.shape[:dim], shard.shape[dim + 1 :])
    return jnp.moveaxis(shard.reshape(*before, peers, -1, *after), dim, 0)


def summed_on_arrival(shard, axis, dim):
    tiles = split_up(shard, dim, lax.axis_size(axis))
    arrived = lax.all_to_all(tiles, axis, split_axis=0, concat_axis=0, tiled=True)
    return arrived.astype(jnp.float32).sum(axis=0)


def combine(earlier, later):
    top_a, sum_a, acc_a = earlier
    top_b, sum_b, acc_b = later
    top = jnp.maximum(top_a, top_b)
    fade_a = jnp.exp(top_a - top)
    fade_b = jnp.exp(top_b - top)
    return (
        top,
        sum_a * fade_a + sum_b * fade_b,
        acc_a * fade_a[..., None] + acc_b * fade_b[..., None],
    )


def nth_match(table, wanted, places):
    matched = (table == wanted).astype(jnp.int32)
    ranking = jnp.cumsum(matched, axis=1) - 1
    return (matched[:, None, :] == 1) & (ranking[:, None, :] == places[None, :, None])


def move_pages(kv_pool, new_owner, new_local):
    groups = lax.axis_size("grp")
    ranks = lax.axis_size(KV)
    per_dev = new_owner.shape[1] // ranks
    cap = groups * NPR // ranks
    grp_rank = lax.axis_index("grp")
    kv_rank = lax.axis_index(KV)
    owners = new_owner.reshape(groups * ranks, per_dev)
    myself = grp_rank * ranks + kv_rank
    places = jnp.arange(cap, dtype=jnp.int32)
    mine = lax.dynamic_index_in_dim(owners, myself, 0, keepdims=False)
    order = jnp.arange(per_dev, dtype=jnp.int32)
    by_col = (
        new_owner.reshape(groups, ranks, per_dev)
        .transpose(1, 0, 2)
        .reshape(ranks, groups * per_dev)
    )
    local_col = (
        new_local.reshape(groups, ranks, per_dev)
        .transpose(1, 0, 2)
        .reshape(ranks, groups * per_dev)
    )
    select = nth_match(by_col, myself, places)
    picked = jnp.sum(jnp.where(select, local_col[:, None, :], 0), axis=2)
    outgoing = jnp.take(kv_pool, picked.reshape(-1), axis=0)
    received = lax.all_to_all(outgoing, KV, split_axis=0, concat_axis=0, tiled=True)
    row_here = lax.dynamic_index_in_dim(by_col, kv_rank, 0, keepdims=False)
    sources = grp_rank * ranks + jnp.arange(ranks, dtype=jnp.int32)
    hits = nth_match(
        jnp.broadcast_to(row_here[None, :], (ranks, row_here.shape[0])), sources[:, None], places
    )
    spots = jnp.arange(row_here.shape[0], dtype=jnp.int32)
    where_f = jnp.sum(jnp.where(hits, spots[None, None, :], 0), axis=2).reshape(-1)
    dest_grp = where_f // per_dev
    dest_pos = where_f % per_dev
    same = (dest_grp[:, None] == dest_grp[None, :]) & (dest_pos[:, None] < dest_pos[None, :])
    rank_in = jnp.sum(same.astype(jnp.int32), axis=0)
    target = dest_grp * NPR + rank_in
    items = jnp.arange(target.shape[0], dtype=jnp.int32)
    inverse = jnp.sum(jnp.where(target[None, :] == items[:, None], items[None, :], 0), axis=1)
    sorted_pages = jnp.take(received, inverse, axis=0)
    arrived = lax.all_to_all(sorted_pages, "grp", split_axis=0, concat_axis=0, tiled=True)
    src_grp = mine // ranks
    earlier = (src_grp[:, None] == src_grp[None, :]) & (order[:, None] < order[None, :])
    before = jnp.sum(earlier.astype(jnp.int32), axis=0)
    return jnp.take(arrived, src_grp * NPR + before, axis=0)


def local_partials(query, resident, arrived, res_slot, res_len, arr_slot, arr_len, token_kv, first):
    pages = jnp.concatenate([resident, arrived], axis=0)
    owner_slot = jnp.concatenate([res_slot, arr_slot])
    filled = jnp.concatenate([res_len, arr_len])
    count = pages.shape[0]
    tokens = pages.shape[2]
    kv_here = pages.shape[3] // HEAD_DIM
    slots = query.shape[0]
    ratio = HEADS // KV_HEADS
    keys = pages[:, 0].astype(jnp.float32).reshape(count, tokens, kv_here, HEAD_DIM)
    values = pages[:, 1].astype(jnp.float32).reshape(count, tokens, kv_here, HEAD_DIM)
    grouped = query.reshape(slots, kv_here, ratio, HEAD_DIM)
    picked = jnp.take(grouped, owner_slot, axis=0)
    scores = jnp.einsum("ikgd,itkd->ikgt", picked, keys, precision=lax.Precision.HIGHEST)
    usable = (jnp.arange(tokens, dtype=jnp.int32)[None, :] < filled[:, None])[:, None, None, :]
    scores = jnp.where(usable, scores, neg_fill)
    page_top = jnp.max(scores, axis=3)
    member = owner_slot[None, :] == jnp.arange(slots, dtype=jnp.int32)[:, None]
    slot_top = jnp.max(jnp.where(member[:, :, None, None], page_top[None], neg_fill), axis=1)
    own_keys = token_kv[:, 0].astype(jnp.float32).reshape(slots, kv_here, HEAD_DIM)
    own_values = token_kv[:, 1].astype(jnp.float32).reshape(slots, kv_here, HEAD_DIM)
    own_score = jnp.einsum("skgd,skd->skg", grouped, own_keys, precision=lax.Precision.HIGHEST)
    own_score = jnp.where(first, own_score, neg_fill)
    slot_top = jnp.maximum(slot_top, own_score)
    reach = jnp.take(slot_top, owner_slot, axis=0)
    weights = jnp.where(usable, jnp.exp(scores - reach[..., None]), 0.0)
    page_sum = jnp.sum(weights, axis=3)
    page_acc = jnp.einsum("ikgt,itkd->ikgd", weights, values, precision=lax.Precision.HIGHEST)
    own_weight = jnp.where(first, jnp.exp(own_score - slot_top), 0.0)
    member_f = member.astype(jnp.float32)
    total = jnp.dot(member_f, page_sum.reshape(count, -1), precision=lax.Precision.HIGHEST)
    total = total + own_weight.reshape(slots, -1)
    weighted = jnp.dot(member_f, page_acc.reshape(count, -1), precision=lax.Precision.HIGHEST)
    weighted = (
        weighted.reshape(slots, kv_here, ratio, HEAD_DIM)
        + own_weight[..., None] * own_values[:, :, None, :]
    )
    return (slot_top.reshape(slots, -1), total, weighted.reshape(slots, kv_here * ratio, HEAD_DIM))


def per_device(
    hidden_states,
    attn_gain,
    mlp_gain,
    w_query,
    w_out,
    w_gate,
    w_up,
    w_down,
    kv_pool,
    resident_cache,
    resident_slot,
    resident_len,
    new_owner,
    new_local,
    new_slot,
    new_len,
    token_kv,
):
    ranks = lax.axis_size(KV)
    pairs = lax.axis_size("tp")
    kv_rank = lax.axis_index(KV)
    tp_rank = lax.axis_index("tp")
    features = hidden_states.astype(jnp.float32)
    partial_query = jnp.dot(
        (features * attn_gain).astype(jnp.bfloat16), w_query, preferred_element_type=jnp.float32
    )
    squares = jnp.sum(features * features, axis=1)
    partial_query, squares = lax.psum((partial_query, squares), KV)
    attn_scale = lax.rsqrt(squares / D + norm_eps)
    query = partial_query * attn_scale[:, None] * HEAD_DIM ** (-0.5)
    new_pages = move_pages(kv_pool, new_owner, new_local)
    top, total, weighted = local_partials(
        query,
        resident_cache[0],
        new_pages,
        resident_slot[0],
        resident_len[0],
        new_slot[0],
        new_len[0],
        token_kv,
        kv_rank == 0,
    )
    top, total, weighted = combined_by_axis((top, total, weighted), KV, combine)
    attn = (weighted / total[..., None]).astype(jnp.bfloat16)
    slots = attn.shape[0]
    heads_here = attn.shape[1]
    span = HEAD_DIM // ranks
    piece = lax.dynamic_slice_in_dim(attn, kv_rank * span, span, 2)
    branch = jnp.dot(
        piece.reshape(slots, heads_here * span),
        w_out.reshape(heads_here * span, w_out.shape[2]),
        preferred_element_type=jnp.float32,
    )
    width_here = hidden_states.shape[1]
    laid = branch.reshape(slots, ranks, width_here)
    spot = (jnp.arange(ranks, dtype=jnp.int32) == kv_rank) & (tp_rank == 0)
    laid = laid + jnp.where(spot[None, :, None], features[:, None, :], 0.0)
    resid = lax.psum(laid.reshape(slots, ranks * width_here).astype(jnp.bfloat16), KV_TP)
    resid_f = resid.astype(jnp.float32)
    mlp_scale = lax.rsqrt(jnp.sum(resid_f * resid_f, axis=1) / D + norm_eps)
    normed_mlp = (resid_f * mlp_gain).astype(jnp.bfloat16)
    gate = jnp.dot(normed_mlp, w_gate, preferred_element_type=jnp.float32) * mlp_scale[:, None]
    upward = jnp.dot(normed_mlp, w_up, preferred_element_type=jnp.float32) * mlp_scale[:, None]
    hidden_units = (jax.nn.silu(gate) * upward).astype(jnp.bfloat16)
    row_count = slots // (ranks * pairs)
    down = summed_on_arrival(
        jnp.dot(hidden_units, w_down, preferred_element_type=jnp.float32).astype(jnp.bfloat16),
        KV_TP,
        0,
    )
    row_start = (kv_rank * pairs + tp_rank) * row_count
    kept = lax.dynamic_slice_in_dim(resid_f, row_start, row_count, 0)
    mixed = (kept + down).astype(jnp.bfloat16)
    return (mixed, new_pages[None])


def solution(mesh):
    finer = Mesh(
        mesh.devices.reshape(mesh.shape["grp"], 4, 4, mesh.shape["tp"]),
        ("grp", "kv_0", "kv_1", "tp"),
    )
    return jax.shard_map(
        per_device,
        mesh=finer,
        in_specs=(
            P("grp", KV),
            P(KV),
            P(),
            P(KV, "tp"),
            P("tp", KV, None),
            P(None, KV_TP),
            P(None, KV_TP),
            P(KV_TP, None),
            P(GRP_KV, None, None, "tp"),
            P("grp", KV, None, None, "tp"),
            P("grp", KV),
            P("grp", KV),
            P(),
            P(),
            P("grp", KV),
            P("grp", KV),
            P("grp", None, "tp"),
        ),
        out_specs=(P(GRP_KV_TP, None), P("grp", KV, None, None, "tp")),
        check_vma=False,
    )
```

profile of v0, /device:TPU:1, one launch (start us, length us, event | category | flops | bytes accessed | tf_op | source)
XLA Modules:
  0.0 507.7 jit_solution(3619202428460434715)
XLA Ops:
  10.4 5.0 gather_fusion.2
  20.1 7.6 %all-to-all-start = ((bf16[16,2,128,512]{3,2,1,0:T(8,128)(2,1)}), bf16[16,2,128,512]{3,2,1,0:T(8,128)(2,1)}, u32[]{:S(2)}, u32[]{:S(2)}) async-start(bf16[16,2,128,512]{3,2,1,0:T(8,128)(2,1)} %broadcast_select_fusion.2), calls=%async_computation | async-start | bytes 8388608 | tf_op jit(solution)/shard_map/all_to_all | solution.py:86
  28.5 59.5 %all-to-all-done = bf16[16,2,128,512]{3,2,1,0:T(8,128)(2,1)} async-done(((bf16[16,2,128,512]{3,2,1,0:T(8,128)(2,1)}), bf16[16,2,128,512]{3,2,1,0:T(8,128)(2,1)}, u32[]{:S(2)}, u32[]{:S(2)}) %all-to-all-start) | async-done | bytes 4194336 | tf_op jit(solution)/shard_map/all_to_all | solution.py:86
  88.1 5.0 gather_fusion.3
  93.1 4.7 broadcast_select_fusion.1
  97.8 5.2 %all-to-all-start.1 = ((bf16[16,2,128,512]{3,2,1,0:T(8,128)(2,1)}), bf16[16,2,128,512]{3,2,1,0:T(8,128)(2,1)}, u32[]{:S(2)}, u32[]{:S(2)}) async-start(bf16[16,2,128,512]{3,2,1,0:T(8,128)(2,1)} %broadcast_select_fusion.1), calls=%async_computation.1 | async-start | bytes 8388608 | tf_op jit(solution)/shard_map/all_to_all | solution.py:102
  105.6 33.9 %psum.22 = f32[128]{0:T(128)S(1)} all-reduce(f32[128]{0:T(128)S(1)} %multiply_reduce_fusion.1), channel_id=1, replica_groups=mesh['grp'=4,'kv_0'=4,'kv_1'=4,'tp'=2] {'kv_0','kv_1'}, use_global_device_ids=true, to_apply=%region_2.0 | all-reduce | flops 128 | bytes 1024 | tf_op jit(solution)/shard_map/psum | solution.py:177
  139.8 61.1 %all-reduce.3.cloned.1.call-done = f32[128,2048]{1,0:T(8,128)} async-done(((f32[128,2048]{1,0:T(8,128)}), f32[128,2048]{1,0:T(8,128)}) %all-reduce.3.cloned.1.call-update) | async-done | bytes 1048592 | tf_op jit(solution)/shard_map/psum | solution.py:177
  205.5 5.0 gather_fusion.4
  216.3 4.7 copy.150
  227.0 4.7 copy.155
  231.7 6.9 %fusion.17 = f32[24,4,4,128]{3,2,1,0:T(4,128)S(1)} fusion(bf16[24,128,4,128]{1,3,2,0:T(8,128)(2,1)} %bitcast.217, f32[24,4,4,128]{3,2,1,0:T(4,128)S(1)} %get-tuple-element.40, f32[24,4,4]{2,1,0:T(4,128)S(1)} %broadcast_select_fusion.3, pred[24,128]{1,0:T(8,128)(4,1)S(1)} %iota_compare_fusion), kind=kOutput, calls=%fused_computation.52 | convolution fusion | flops 75595776 | bytes 3543552 | tf_op jit(solution)/shard_map/ikgt,itkd->ikgd/dot_general | solution.py:136
  241.4 9.3 %all_gather.25 = f32[4,128,16]{1,2,0:T(8,128)S(1)} all-gather(f32[1,128,16]{1,2,0:T(8,128)S(1)} %bitcast.229), channel_id=1, replica_groups=mesh['grp'=4,'kv_0'=4,'kv_1'=4,'tp'=2] {'kv_0'}, dimensions={0}, use_global_device_ids=true | all-gather | bytes 40960 | tf_op jit(solution)/shard_map/all_gather | solution.py:24
  251.3 38.9 %all-gather.4.cloned.1.call-done = f32[4,128,16,128]{3,2,1,0:T(8,128)} async-done(((f32[1,128,16,128]{3,2,1,0:T(8,128)}), f32[4,128,16,128]{3,2,1,0:T(8,128)}) %all-gather.4.cloned.1.call-update) | async-done | bytes 4194320 | tf_op jit(solution)/shard_map/all_gather | solution.py:24
  290.2 4.8 fusion.3
  297.1 9.0 %all-gather = f32[512,16]{0,1:T(8,128)S(1)} all-gather(f32[128,16]{0,1:T(8,128)S(1)} %convolution_add_fusion.1), channel_id=2, replica_groups=mesh['grp'=4,'kv_0'=4,'kv_1'=4,'tp'=2] {'kv_0'}, dimensions={0}, use_global_device_ids=true | all-gather | bytes 40960 | tf_op jit(solution)/shard_map/all_gather | solution.py:24
  306.2 10.8 %all_gather.27 = f32[4,128,16]{1,2,0:T(8,128)S(1)} all-gather(f32[1,128,16]{1,2,0:T(8,128)S(1)} %get-tuple-element.15), channel_id=1, replica_groups=mesh['grp'=4,'kv_0'=4,'kv_1'=4,'tp'=2] {'kv_1'}, dimensions={0}, use_global_device_ids=true | all-gather | bytes 40960 | tf_op jit(solution)/shard_map/all_gather | solution.py:24
  317.0 10.6 %all_gather.30 = f32[4,128,16]{1,2,0:T(8,128)S(1)} all-gather(f32[1,128,16]{1,2,0:T(8,128)S(1)} %get-tuple-element.14), channel_id=1, replica_groups=mesh['grp'=4,'kv_0'=4,'kv_1'=4,'tp'=2] {'kv_1'}, dimensions={0}, use_global_device_ids=true | all-gather | bytes 40960 | tf_op jit(solution)/shard_map/all_gather | solution.py:24
  327.6 16.7 %all-gather.6.cloned.1.call-done = f32[4,128,16,128]{3,2,1,0:T(8,128)} async-done(((f32[1,128,16,128]{3,2,1,0:T(8,128)}), f32[4,128,16,128]{3,2,1,0:T(8,128)}) %all-gather.6.cloned.1.call-update) | async-done | bytes 4194320 | tf_op jit(solution)/shard_map/all_gather | solution.py:24
  358.3 105.6 %all-reduce.5.cloned.1.call-done = bf16[128,4096]{1,0:T(8,128)(2,1)} async-done(((bf16[128,4096]{1,0:T(8,128)(2,1)}), bf16[128,4096]{1,0:T(8,128)(2,1)}) %all-reduce.5.cloned.1.call-update) | async-done | bytes 1048592 | tf_op jit(solution)/shard_map/psum | solution.py:207
  469.0 6.0 %convolution_convert_fusion = bf16[128,4096]{1,0:T(8,128)(2,1)S(1)} fusion(bf16[448,4096]{1,0:T(8,128)(2,1)} %param.26, bf16[4096,448]{0,1:T(8,128)(2,1)} %param.25, f32[4096]{0:T(1024)S(1)} %copy-done.7, bf16[128,4096]{1,0:T(8,128)(2,1)S(1)} %copy-done.2, f32[128,448]{0,1:T(8,128)S(1)} %convolution_multiply_fusion.1, f32[128]{0:T(128)S(1)} %add_rsqrt_fusion), kind=kOutput, calls=%fused_computation.7 | convolution fusion | flops 942022656 | bytes 9683456 | tf_op jit(solution)/shard_map/dot_general | solution.py:216
  476.2 6.1 %all-to-all-start.2 = ((bf16[32,4,4096]{2,1,0:T(4,128)(2,1)}), bf16[32,4,4096]{2,1,0:T(4,128)(2,1)S(1)}, u32[]{:S(2)}, u32[]{:S(2)}) async-start(bf16[32,4,4096]{2,1,0:T(4,128)(2,1)} %reshape.671), calls=%async_computation.2 | async-start | bytes 2097152 | tf_op jit(solution)/shard_map/all_to_all | solution.py:38
  482.3 4.8 fusion.92
  488.6 10.6 %all-to-all-done.2 = bf16[32,4,4096]{2,1,0:T(4,128)(2,1)S(1)} async-done(((bf16[32,4,4096]{2,1,0:T(4,128)(2,1)}), bf16[32,4,4096]{2,1,0:T(4,128)(2,1)S(1)}, u32[]{:S(2)}, u32[]{:S(2)}) %all-to-all-start.2) | async-done | bytes 1048608 | tf_op jit(solution)/shard_map/all_to_all | solution.py:38
  (129 shorter events, 57.0 us)
Async XLA Ops:
  7.2 95.8 %copy-start = (bf16[256,2048]{1,0:T(8,128)(2,1)S(1)}, bf16[256,2048]{1,0:T(8,128)(2,1)}, u32[]{:S(2)}) copy-start(bf16[256,2048]{1,0:T(8,128)(2,1)} %param.22) | copy-start | bytes 3145732
  20.1 68.0 %all-to-all-start = ((bf16[16,2,128,512]{3,2,1,0:T(8,128)(2,1)}), bf16[16,2,128,512]{3,2,1,0:T(8,128)(2,1)}, u32[]{:S(2)}, u32[]{:S(2)}) async-start(bf16[16,2,128,512]{3,2,1,0:T(8,128)(2,1)} %broadcast_select_fusion.2), calls=%async_computation | async-start | bytes 8388608 | tf_op jit(solution)/shard_map/all_to_all | solution.py:86
  97.8 5.3 %copy-start.6 = (bf16[128,256]{1,0:T(8,128)(2,1)S(1)}, bf16[128,256]{1,0:T(8,128)(2,1)}, u32[]{:S(2)}) copy-start(bf16[128,256]{1,0:T(8,128)(2,1)} %param.19) | copy-start | bytes 196612
  97.8 5.3 %copy-start.8 = (f32[256]{0:T(256)S(1)}, f32[256]{0:T(256)}, u32[]{:S(2)}) copy-start(f32[256]{0:T(256)} %param.20) | copy-start | bytes 3076
  97.8 6.7 %copy-start.9 = (s32[1,16]{1,0:T(1,128)S(1)}, s32[1,16]{1,0:T(1,128)}, u32[]{:S(2)}) copy-start(s32[1,16]{1,0:T(1,128)} %param.33) | copy-start | bytes 196
  97.8 6.7 %copy-start.10 = (s32[1,8]{1,0:T(1,128)S(1)}, s32[1,8]{1,0:T(1,128)}, u32[]{:S(2)}) copy-start(s32[1,8]{1,0:T(1,128)} %param.29) | copy-start | bytes 100
  97.8 7.0 %copy-start.5 = (bf16[128,2,512]{2,1,0:T(2,128)(2,1)S(1)}, bf16[128,2,512]{2,1,0:T(2,128)(2,1)}, u32[]{:S(2)}) copy-start(bf16[128,2,512]{2,1,0:T(2,128)(2,1)} %param.35) | copy-start | bytes 786436
  97.8 107.8 %all-to-all-start.1 = ((bf16[16,2,128,512]{3,2,1,0:T(8,128)(2,1)}), bf16[16,2,128,512]{3,2,1,0:T(8,128)(2,1)}, u32[]{:S(2)}, u32[]{:S(2)}) async-start(bf16[16,2,128,512]{3,2,1,0:T(8,128)(2,1)} %broadcast_select_fusion.1), calls=%async_computation.1 | async-start | bytes 8388608 | tf_op jit(solution)/shard_map/all_to_all | solution.py:102
  103.0 2.2 copy-start.11
  103.0 2.2 copy-start.12
  103.0 98.0 %all-reduce.3.cloned.1.call-start = ((), (), s32[]{:S(2)}) async-start(), calls=%async_computation.3 | async-start | bytes 2097152 | tf_op jit(solution)/shard_map/psum | solution.py:177
  104.4 185.8 %all-gather.4.cloned.1.call-start = ((), (), s32[]{:S(2)}) async-start(), calls=%async_computation.4 | async-start | bytes 5242880 | tf_op jit(solution)/shard_map/all_gather | solution.py:24
  210.6 2.9 copy-start.3
  241.2 103.0 %all-gather.6.cloned.1.call-start = ((), (), s32[]{:S(2)}) async-start(), calls=%async_computation.5 | async-start | bytes 5242880 | tf_op jit(solution)/shard_map/all_gather | solution.py:24
  250.7 44.4 %copy-start.4 = (bf16[16,8,4096]{2,1,0:T(8,128)(2,1)S(1)}, bf16[16,8,4096]{2,1,0:T(8,128)(2,1)}, u32[]{:S(2)}) copy-start(bf16[16,8,4096]{2,1,0:T(8,128)(2,1)} %param.23) | copy-start | bytes 3145732
  295.0 168.9 %all-reduce.5.cloned.1.call-start = ((), (), s32[]{:S(2)}) async-start(), calls=%async_computation.6 | async-start | bytes 2097152 | tf_op jit(solution)/shard_map/psum | solution.py:207
  356.2 109.3 %copy-start.7 = (f32[4096]{0:T(1024)S(1)}, f32[4096]{0:T(1024)}, u32[]{:S(2)}) copy-start(f32[4096]{0:T(1024)} %param.21) | copy-start | bytes 49156
  463.9 5.1 %copy-start.2 = (bf16[128,4096]{1,0:T(8,128)(2,1)S(1)}, bf16[128,4096]{1,0:T(8,128)(2,1)}, u32[]{:S(2)}) copy-start(bf16[128,4096]{1,0:T(8,128)(2,1)} %all-reduce.5.cloned.1.call-done) | copy-start | bytes 3145732
  476.2 23.0 %all-to-all-start.2 = ((bf16[32,4,4096]{2,1,0:T(4,128)(2,1)}), bf16[32,4,4096]{2,1,0:T(4,128)(2,1)S(1)}, u32[]{:S(2)}, u32[]{:S(2)}) async-start(bf16[32,4,4096]{2,1,0:T(4,128)(2,1)} %reshape.671), calls=%async_computation.2 | async-start | bytes 2097152 | tf_op jit(solution)/shard_map/all_to_all | solution.py:38
  482.3 18.9 %copy-start.1 = (bf16[256,2048]{1,0:T(8,128)(2,1)S(1)}, bf16[256,2048]{1,0:T(8,128)(2,1)}, u32[]{:S(2)}) copy-start(bf16[256,2048]{1,0:T(8,128)(2,1)} %param.22) | copy-start | bytes 3145732
Sparse Core Ops, SparseCore 0:
  107.0 93.8 all-reduce.2
  241.4 48.7 all-gather.3
  295.1 49.0 all-gather.5
  358.4 105.4 all-reduce.4
where the time goes:
time: 509 us; the launch traced here: 508 us
  waiting for transfers between devices  292 us (57%)
  blocking collectives  73.6 us (14%)
  local copies, waits for them, and re-layouts  47 us (9%)
  other arithmetic  34.5 us (7%)
  matrix products  26.8 us (5%)
  starting transfers between devices  19 us (4%)
  between operations  14.2 us (3%)
    psum x1, waiting for transfers between devices, per_device(): lax.psum(laid.reshape(slots, ranks * width_here).astype(jnp.bfloat16), KV...  106 us
    psum x1, waiting for transfers between devices, per_device(): partial_query, squares = lax.psum((partial_query, squares), KV)  61.1 us
    all_to_all x1, waiting for transfers between devices, move_pages(): lax.all_to_all(outgoing, KV, split_axis=0, concat_axis=0, tiled=True)  59.5 us
    all_gather x2, waiting for transfers between devices, combined_by_axis(): pieces = jax.tree.map(lambda part: lax.all_gather(part, axis), shard)  55.5 us
    all_gather x4, blocking collectives, combined_by_axis(): pieces = jax.tree.map(lambda part: lax.all_gather(part, axis), shard)  39.7 us
    psum x1, blocking collectives, per_device(): partial_query, squares = lax.psum((partial_query, squares), KV)  33.9 us
    all_to_all x1, waiting for transfers between devices, summed_on_arrival(): lax.all_to_all(tiles, axis, split_axis=0, concat_axis=0, tiled=True)  10.6 us
  transfers between devices with their start and end apart: 7, of which 6 were waited for; matrix products, arithmetic and copies ran while one was open for 3% of the time, Pallas kernels for 0%

commit v1 on v0

--- a/solution.py
+++ b/solution.py
@@ -1,7 +1,8 @@
 import jax
 import jax.numpy as jnp
 from jax import lax
-from jax.sharding import Mesh
+from jax.experimental import pallas as pl
+from jax.experimental.pallas import tpu as pltpu
 from jax.sharding import PartitionSpec as P
 
 D = 4096
@@ -9,10 +10,10 @@
 KV_HEADS = 8
 HEAD_DIM = 128
 NPR = 4
-KV = ("kv_0", "kv_1")
-KV_TP = ("kv_0", "kv_1", "tp")
-GRP_KV = ("grp", "kv_0", "kv_1")
-GRP_KV_TP = ("grp", "kv_0", "kv_1", "tp")
+KV = "kv"
+KV_TP = ("kv", "tp")
+GRP_KV = ("grp", "kv")
+GRP_KV_TP = ("grp", "kv", "tp")
 
 
 neg_fill = -1e30
@@ -146,6 +147,238 @@
     return (slot_top.reshape(slots, -1), total, weighted.reshape(slots, kv_here * ratio, HEAD_DIM))
 
 
+MESH = pl.DeviceIdType.MESH
+
+
+def peer_of(x, y, k):
+    return lax.rem(x + k // 4, 4) * 4 + lax.rem(y + k % 4, 4)
+
+
+def source_of(x, y, k):
+    return lax.rem(x + 4 - k // 4, 4) * 4 + lax.rem(y + 4 - k % 4, 4)
+
+
+ORDER = sorted(range(1, 16), key=lambda k: (min(k // 4, 4 - k // 4) + min(k % 4, 4 - k % 4), k))
+
+
+def tail_kernel(
+    attn_ref, hid_ref, gain_ref, wout_hbm, wg_hbm, wu_hbm, wd_hbm, out_ref,
+    wout, wg, wu, wd, pair_send, pair_recv, own_part, rs_send, rs_recv, ag, hunits,
+    dp_send, dp_recv, dsum, d_send, d_recv, resrow,
+    w_sem, pair_ss, pair_rs, rs_ss, rs_rs, ag_ss, ag_rs, fw_ss, fw_rs, dp_ss, dp_rs, d_ss, d_rs,
+):
+    f32, bf16 = jnp.float32, jnp.bfloat16
+    grp, kv, tp = lax.axis_index("grp"), lax.axis_index("kv"), lax.axis_index("tp")
+    x, y = kv // 4, lax.rem(kv, 4)
+    other = 1 - tp
+    partner = (grp, kv, other)
+
+    def dev(k):
+        return (grp, peer_of(x, y, k), tp)
+
+    loads = [
+        pltpu.make_async_copy(src, dst, w_sem.at[i])
+        for i, (src, dst) in enumerate([(wout_hbm, wout), (wg_hbm, wg), (wu_hbm, wu), (wd_hbm, wd)])
+    ]
+    for load in loads:
+        load.start()
+
+    barrier = pltpu.get_barrier_semaphore()
+    pl.semaphore_signal(barrier, inc=1, device_id=partner, device_id_type=MESH)
+    for k in range(1, 16):
+        pl.semaphore_signal(barrier, inc=1, device_id=dev(k), device_id_type=MESH)
+
+    rho = lax.broadcasted_iota(jnp.int32, (128, 128), 0)
+    col = lax.broadcasted_iota(jnp.int32, (128, 128), 1)
+    slot = (lax.rem(rho, 64) // 4) * 8 + (rho // 64) * 4 + lax.rem(rho, 4)
+    perm = jnp.where(col == slot, 1.0, 0.0).astype(bf16)
+    attn = jnp.dot(perm, attn_ref[...], preferred_element_type=f32).astype(bf16)
+    hid = jnp.dot(
+        perm, hid_ref[:, pl.ds(pl.multiple_of(tp * 128, 128), 128)], preferred_element_type=f32
+    )
+
+    loads[0].wait()
+    pl.semaphore_wait(barrier, 16)
+
+    order = ORDER[::-1] + [0]
+    pair_copies = []
+    for g in range(4):
+        for i in range(4):
+            k = order[4 * g + i]
+            dest = peer_of(x, y, k)
+            part = jnp.dot(
+                attn, wout[:, pl.ds(pl.multiple_of(dest * 256, 256), 256)], preferred_element_type=f32
+            )
+            low, high = part[:, :128], part[:, 128:]
+            own_part[g, i] = jnp.where(tp == 0, low, high)
+            pair_send[g, i] = jnp.where(tp == 0, high, low).astype(bf16)
+        copy = pltpu.make_async_remote_copy(
+            src_ref=pair_send.at[g], dst_ref=pair_recv.at[g], send_sem=pair_ss.at[g],
+            recv_sem=pair_rs.at[g], device_id=partner, device_id_type=MESH,
+        )
+        copy.start()
+        pair_copies.append(copy)
+    rs_copies = {}
+    block = None
+    for g in range(4):
+        pair_copies[g].wait_recv()
+        for i in range(4):
+            k = order[4 * g + i]
+            total = own_part[g, i] + pair_recv[g, i].astype(f32)
+            if k == 0:
+                block = total + hid
+            else:
+                rs_send[k] = total.astype(bf16)
+                copy = pltpu.make_async_remote_copy(
+                    src_ref=rs_send.at[k], dst_ref=rs_recv.at[k], send_sem=rs_ss.at[k],
+                    recv_sem=rs_rs.at[k], device_id=dev(k), device_id_type=MESH,
+                )
+                copy.start()
+                rs_copies[k] = copy
+    for k in ORDER:
+        rs_copies[k].wait_recv()
+        block = block + rs_recv[k].astype(f32)
+    ag[0, tp] = block.astype(bf16)
+
+    ag_copies = {}
+    fw_copies = {}
+
+    def forward(k):
+        copy = pltpu.make_async_remote_copy(
+            src_ref=ag.at[k, tp], dst_ref=ag.at[k, tp], send_sem=fw_ss.at[k],
+            recv_sem=fw_rs.at[k], device_id=partner, device_id_type=MESH,
+        )
+        copy.start()
+        fw_copies[k] = copy
+
+    for k in ORDER[::-1]:
+        copy = pltpu.make_async_remote_copy(
+            src_ref=ag.at[0, tp], dst_ref=ag.at[k, tp], send_sem=ag_ss.at[k],
+            recv_sem=ag_rs.at[k], device_id=dev(k), device_id_type=MESH,
+        )
+        copy.start()
+        ag_copies[k] = copy
+    forward(0)
+    for g in range(4):
+        pair_copies[g].wait_send()
+    loads[1].wait()
+    loads[2].wait()
+    seq = [0] + ORDER
+    gate = jnp.zeros((128, 448), f32)
+    upward = jnp.zeros((128, 448), f32)
+    squares = jnp.zeros((128, 128), f32)
+    mine = lax.broadcasted_iota(jnp.int32, (8, 128), 0) + tp * 64 + kv * 4
+    pick = jnp.where(lax.broadcasted_iota(jnp.int32, (8, 128), 1) == mine, 1.0, 0.0).astype(bf16)
+    for n, k in enumerate(seq):
+        if n + 1 < 16:
+            ag_copies[seq[n + 1]].wait_recv()
+            forward(seq[n + 1])
+        fw_copies[k].wait_recv()
+        src = source_of(x, y, k)
+        both = jnp.concatenate([ag[k, 0], ag[k, 1]], axis=1)
+        wide = both.astype(f32)
+        squares = squares + wide[:, :128] * wide[:, :128] + wide[:, 128:] * wide[:, 128:]
+        normed = (wide * gain_ref[pl.ds(src, 1), :]).astype(bf16)
+        rows = pl.ds(pl.multiple_of(src * 256, 256), 256)
+        gate = gate + jnp.dot(normed, wg[rows, :], preferred_element_type=f32)
+        upward = upward + jnp.dot(normed, wu[rows, :], preferred_element_type=f32)
+    scale = lax.rsqrt(jnp.sum(squares, axis=1, keepdims=True) / D + norm_eps)
+    gate = gate * scale
+    upward = upward * scale
+    hunits[...] = (gate / (1.0 + jnp.exp(-gate)) * upward).astype(bf16)
+
+    loads[3].wait()
+    dp_copies = []
+    for c in range(4):
+        cols = pl.ds(c * 1024, 1024)
+        part = jnp.dot(hunits[...], wd[:, cols], preferred_element_type=f32)
+        first, second = part[:64], part[64:]
+        dsum[:, cols] = jnp.where(tp == 0, first, second)
+        dp_send[c] = jnp.where(tp == 0, second, first).astype(bf16)
+        copy = pltpu.make_async_remote_copy(
+            src_ref=dp_send.at[c], dst_ref=dp_recv.at[c], send_sem=dp_ss.at[c],
+            recv_sem=dp_rs.at[c], device_id=partner, device_id_type=MESH,
+        )
+        copy.start()
+        dp_copies.append(copy)
+    for c in range(4):
+        dp_copies[c].wait_recv()
+        cols = pl.ds(c * 1024, 1024)
+        dsum[:, cols] = dsum[:, cols] + dp_recv[c].astype(f32)
+    for j in range(16):
+        d_send[j] = dsum[4 * j : 4 * j + 4, :].astype(bf16)
+    d_copies = {}
+    for k in ORDER[::-1]:
+        copy = pltpu.make_async_remote_copy(
+            src_ref=d_send.at[peer_of(x, y, k)], dst_ref=d_recv.at[k], send_sem=d_ss.at[k],
+            recv_sem=d_rs.at[k], device_id=dev(k), device_id_type=MESH,
+        )
+        copy.start()
+        d_copies[k] = copy
+    for k in range(16):
+        for t in range(2):
+            cols = pl.ds(pl.multiple_of((source_of(x, y, k) * 2 + t) * 128, 128), 128)
+            resrow[:, cols] = jnp.dot(pick, ag[k, t], preferred_element_type=f32)
+    pick64 = lax.broadcasted_iota(jnp.int32, (8, 64), 0) + kv * 4
+    total = resrow[...][:4]
+    lane = lax.broadcasted_iota(jnp.int32, (4, 4096), 0)
+    own = jnp.zeros((4, 4096), f32)
+    for j in range(16):
+        own = jnp.where(kv == j, dsum[4 * j : 4 * j + 4, :], own)
+    total = total + own
+    for k in ORDER:
+        d_copies[k].wait_recv()
+        total = total + d_recv[k].astype(f32)
+    out_ref[...] = total.astype(bf16)
+
+    for k in range(1, 16):
+        rs_copies[k].wait_send()
+        ag_copies[k].wait_send()
+        d_copies[k].wait_send()
+    for k in range(16):
+        fw_copies[k].wait_send()
+    for c in range(4):
+        dp_copies[c].wait_send()
+
+
+def tail(attn, hidden, gain, w_out, w_gate, w_up, w_down):
+    bf16, f32 = jnp.bfloat16, jnp.float32
+    vmem = pl.BlockSpec(memory_space=pltpu.VMEM)
+    hbm = pl.BlockSpec(memory_space=pl.ANY)
+    dma = pltpu.SemaphoreType.DMA
+    return pl.pallas_call(
+        tail_kernel,
+        name="tail",
+        out_shape=jax.ShapeDtypeStruct((4, 4096), bf16),
+        in_specs=[vmem, vmem, vmem, hbm, hbm, hbm, hbm],
+        out_specs=vmem,
+        scratch_shapes=[
+            pltpu.VMEM((128, 4096), bf16),
+            pltpu.VMEM((4096, 448), bf16),
+            pltpu.VMEM((4096, 448), bf16),
+            pltpu.VMEM((448, 4096), bf16),
+            pltpu.VMEM((4, 4, 128, 128), bf16),
+            pltpu.VMEM((4, 4, 128, 128), bf16),
+            pltpu.VMEM((4, 4, 128, 128), f32),
+            pltpu.VMEM((16, 128, 128), bf16),
+            pltpu.VMEM((16, 128, 128), bf16),
+            pltpu.VMEM((16, 2, 128, 128), bf16),
+            pltpu.VMEM((128, 448), bf16),
+            pltpu.VMEM((4, 64, 1024), bf16),
+            pltpu.VMEM((4, 64, 1024), bf16),
+            pltpu.VMEM((64, 4096), f32),
+            pltpu.VMEM((16, 4, 4096), bf16),
+            pltpu.VMEM((16, 4, 4096), bf16),
+            pltpu.VMEM((8, 4096), f32),
+            dma((4,)), dma((4,)), dma((4,)), dma((16,)), dma((16,)), dma((16,)), dma((16,)),
+            dma((16,)), dma((16,)), dma((4,)), dma((4,)), dma((16,)), dma((16,)),
+        ],
+        compiler_params=pltpu.CompilerParams(
+            collective_id=0, has_side_effects=True, vmem_limit_bytes=60 * 1024 * 1024
+        ),
+    )(attn, hidden, gain, w_out, w_gate, w_up, w_down)
+
+
 def per_device(
     hidden_states,
     attn_gain,
@@ -189,48 +422,28 @@
         token_kv,
         kv_rank == 0,
     )
-    top, total, weighted = combined_by_axis((top, total, weighted), KV, combine)
+    top, total, weighted = combined_by_axis((top, total, weighted), (KV,), combine)
     attn = (weighted / total[..., None]).astype(jnp.bfloat16)
     slots = attn.shape[0]
     heads_here = attn.shape[1]
     span = HEAD_DIM // ranks
     piece = lax.dynamic_slice_in_dim(attn, kv_rank * span, span, 2)
-    branch = jnp.dot(
+    mixed = tail(
         piece.reshape(slots, heads_here * span),
+        hidden_states,
+        mlp_gain.reshape(16, 256),
         w_out.reshape(heads_here * span, w_out.shape[2]),
-        preferred_element_type=jnp.float32,
-    )
-    width_here = hidden_states.shape[1]
-    laid = branch.reshape(slots, ranks, width_here)
-    spot = (jnp.arange(ranks, dtype=jnp.int32) == kv_rank) & (tp_rank == 0)
-    laid = laid + jnp.where(spot[None, :, None], features[:, None, :], 0.0)
-    resid = lax.psum(laid.reshape(slots, ranks * width_here).astype(jnp.bfloat16), KV_TP)
-    resid_f = resid.astype(jnp.float32)
-    mlp_scale = lax.rsqrt(jnp.sum(resid_f * resid_f, axis=1) / D + norm_eps)
-    normed_mlp = (resid_f * mlp_gain).astype(jnp.bfloat16)
-    gate = jnp.dot(normed_mlp, w_gate, preferred_element_type=jnp.float32) * mlp_scale[:, None]
-    upward = jnp.dot(normed_mlp, w_up, preferred_element_type=jnp.float32) * mlp_scale[:, None]
-    hidden_units = (jax.nn.silu(gate) * upward).astype(jnp.bfloat16)
-    row_count = slots // (ranks * pairs)
-    down = summed_on_arrival(
-        jnp.dot(hidden_units, w_down, preferred_element_type=jnp.float32).astype(jnp.bfloat16),
-        KV_TP,
-        0,
-    )
-    row_start = (kv_rank * pairs + tp_rank) * row_count
-    kept = lax.dynamic_slice_in_dim(resid_f, row_start, row_count, 0)
-    mixed = (kept + down).astype(jnp.bfloat16)
+        w_gate,
+        w_up,
+        w_down,
+    )
     return (mixed, new_pages[None])
 
 
 def solution(mesh):
-    finer = Mesh(
-        mesh.devices.reshape(mesh.shape["grp"], 4, 4, mesh.shape["tp"]),
-        ("grp", "kv_0", "kv_1", "tp"),
-    )
     return jax.shard_map(
         per_device,
-        mesh=finer,
+        mesh=mesh,
         in_specs=(
             P("grp", KV),
             P(KV),

time: 509 us -> 462 us (0.908)
  waiting for transfers between devices: 292 us -> 175 us
  local copies, waits for them, and re-layouts: 47 us -> 93.4 us
  Pallas kernels: 0 us -> 43.9 us
  matrix products: 26.8 us -> 15.6 us
  starting transfers between devices: 19 us -> 12.9 us
    psum x1 -> x0, waiting for transfers between devices: 106 us -> none  [per_device(): lax.psum(laid.reshape(slots, ranks * width_here).astype(jnp.bfloat16), KV...]
    pallas_call x0 -> x1, Pallas kernels: none -> 43.9 us  [tail(): pl.pallas_call(tail_kernel, name='tail', out_shape=jax.ShapeDtypeStruct((...]
    unnamed x31 -> x42, local copies, waits for them, and re-layouts: 6.32 us -> 49.4 us
    dot_general x3 -> x0, matrix products: 11.3 us -> none  [the longest x1 5.99 us: per_device(): jnp.dot(hidden_units, w_down, preferred_element_type=jnp.float32)]
    all_to_all x1 -> x0, waiting for transfers between devices: 10.6 us -> none  [summed_on_arrival(): lax.all_to_all(tiles, axis, split_axis=0, concat_axis=0, tiled=True)]
    slice x1, local copies, waits for them, and re-layouts: 3.91 us -> 10.9 us  [combined_by_axis(): shard = jax.tree.map(lambda part: part[0], pieces)]
    all_to_all x1 -> x0, starting transfers between devices: 6.05 us -> none  [summed_on_arrival(): lax.all_to_all(tiles, axis, split_axis=0, concat_axis=0, tiled=True)]
    all_gather x2 -> x1, waiting for transfers between devices: 55.5 us -> 54.6 us  [combined_by_axis(): pieces = jax.tree.map(lambda part: lax.all_gather(part, axis), shard)]
  transfers between devices with their start and end apart: 7 -> 4, of which waited for: 6 -> 3; matrix products, arithmetic and copies ran while one was open for 3% -> 6% of each run, Pallas kernels for 0% -> 0%
where the time goes in v1:
time: 462 us; the launch traced here: 460 us
  waiting for transfers between devices  175 us (38%)
  local copies, waits for them, and re-layouts  93.4 us (20%)
  blocking collectives  72.8 us (16%)
  Pallas kernels  43.9 us (10%)
  other arithmetic  32 us (7%)
  matrix products  15.6 us (3%)
  between operations  14.4 us (3%)
  starting transfers between devices  12.9 us (3%)
    psum x1, waiting for transfers between devices, per_device(): partial_query, squares = lax.psum((partial_query, squares), KV)  61.1 us
    all_to_all x1, waiting for transfers between devices, move_pages(): lax.all_to_all(outgoing, KV, split_axis=0, concat_axis=0, tiled=True)  59.5 us
    all_gather x1, waiting for transfers between devices, combined_by_axis(): pieces = jax.tree.map(lambda part: lax.all_gather(part, axis), shard)  54.6 us
    unnamed x42, local copies, waits for them, and re-layouts  49.4 us
    pallas_call x1, Pallas kernels, tail(): pl.pallas_call(tail_kernel, name='tail', out_shape=jax.ShapeDtypeStruct((...  43.9 us
    all_gather x2, blocking collectives, combined_by_axis(): pieces = jax.tree.map(lambda part: lax.all_gather(part, axis), shard)  38.9 us
    psum x1, blocking collectives, per_device(): partial_query, squares = lax.psum((partial_query, squares), KV)  33.9 us
    slice x1, local copies, waits for them, and re-layouts, combined_by_axis(): shard = jax.tree.map(lambda part: part[0], pieces)  10.9 us
  transfers between devices with their start and end apart: 4, of which 3 were waited for; matrix products, arithmetic and copies ran while one was open for 6% of the time, Pallas kernels for 0%

profile of v1, /device:TPU:1, one launch (start us, length us, event | category | flops | bytes accessed | tf_op | source)
XLA Modules:
  0.0 460.4 jit_solution(8398149596584717670)
XLA Ops:
  10.4 5.0 %gather_fusion.2 = bf16[16,2,128,512]{3,2,1,0:T(8,128)(2,1)} fusion(bf16[16,2,128,512]{3,2,1,0:T(8,128)(2,1)} %param.27, s32[1024]{0:T(1024)S(1)} %pad_clamp_fusion.2), kind=kCustom, calls=%fused_computation.clone | custom fusion | bytes 8388672 | tf_op jit(solution)/shard_map/jit(_take)/gather | solution.py:86
  15.5 4.7 %broadcast_select_fusion.2 = bf16[16,2,128,512]{3,2,1,0:T(8,128)(2,1)} fusion(bf16[16,2,128,512]{3,2,1,0:T(8,128)(2,1)} %gather_fusion.2, pred[16]{0:T(512)(128)(4,1)S(1)} %compare_and_fusion.2), kind=kLoop, calls=%fused_computation.9 | loop fusion | flops 2097152 | bytes 8388624 | tf_op jit(solution)/shard_map/jit(_take)/select_n | solution.py:86
  20.1 7.6 %all-to-all-start = ((bf16[16,2,128,512]{3,2,1,0:T(8,128)(2,1)}), bf16[16,2,128,512]{3,2,1,0:T(8,128)(2,1)}, u32[]{:S(2)}, u32[]{:S(2)}) async-start(bf16[16,2,128,512]{3,2,1,0:T(8,128)(2,1)} %broadcast_select_fusion.2), calls=%async_computation | async-start | bytes 8388608 | tf_op jit(solution)/shard_map/all_to_all | solution.py:87
  28.5 59.5 %all-to-all-done = bf16[16,2,128,512]{3,2,1,0:T(8,128)(2,1)} async-done(((bf16[16,2,128,512]{3,2,1,0:T(8,128)(2,1)}), bf16[16,2,128,512]{3,2,1,0:T(8,128)(2,1)}, u32[]{:S(2)}, u32[]{:S(2)}) %all-to-all-start) | async-done | bytes 4194336 | tf_op jit(solution)/shard_map/all_to_all | solution.py:87
  88.1 5.0 %gather_fusion.3 = bf16[16,2,128,512]{3,2,1,0:T(8,128)(2,1)} fusion(bf16[16,2,128,512]{3,2,1,0:T(8,128)(2,1)} %all-to-all-done, s32[1024]{0:T(1024)S(1)} %pad_clamp_fusion.1), kind=kCustom, calls=%fused_computation.1.clone | custom fusion | bytes 8388672 | tf_op jit(solution)/shard_map/jit(_take)/gather | solution.py:102
  93.1 4.7 %broadcast_select_fusion.1 = bf16[16,2,128,512]{3,2,1,0:T(8,128)(2,1)} fusion(bf16[16,2,128,512]{3,2,1,0:T(8,128)(2,1)} %gather_fusion.3, pred[16]{0:T(512)(128)(4,1)S(1)} %compare_and_fusion.1), kind=kLoop, calls=%fused_computation.8 | loop fusion | flops 2097152 | bytes 8388624 | tf_op jit(solution)/shard_map/jit(_take)/select_n | solution.py:102
  97.8 5.2 %all-to-all-start.1 = ((bf16[16,2,128,512]{3,2,1,0:T(8,128)(2,1)}), bf16[16,2,128,512]{3,2,1,0:T(8,128)(2,1)}, u32[]{:S(2)}, u32[]{:S(2)}) async-start(bf16[16,2,128,512]{3,2,1,0:T(8,128)(2,1)} %broadcast_select_fusion.1), calls=%async_computation.1 | async-start | bytes 8388608 | tf_op jit(solution)/shard_map/all_to_all | solution.py:103
  105.6 33.9 %psum.15 = f32[128]{0:T(128)S(1)} all-reduce(f32[128]{0:T(128)S(1)} %fusion.29), channel_id=1, replica_groups=mesh['grp'=4,'kv'=16,'tp'=2] {'kv'}, use_global_device_ids=true, to_apply=%region_2.0 | all-reduce | flops 128 | bytes 1024 | tf_op jit(solution)/shard_map/psum | solution.py:410
  139.8 61.1 %all-reduce.2.cloned.1.call-done = f32[128,2048]{1,0:T(8,128)} async-done(((f32[128,2048]{1,0:T(8,128)}), f32[128,2048]{1,0:T(8,128)}) %all-reduce.2.cloned.1.call-update) | async-done | bytes 1048592 | tf_op jit(solution)/shard_map/psum | solution.py:410
  205.5 5.0 %gather_fusion.4 = bf16[16,2,128,512]{3,2,1,0:T(8,128)(2,1)} fusion(bf16[16,2,128,512]{3,2,1,0:T(8,128)(2,1)} %all-to-all-done.1, s32[1024]{0:T(1024)S(1)} %pad_clamp_fusion), kind=kCustom, calls=%fused_computation.2.clone | custom fusion | bytes 8388672 | tf_op jit(solution)/shard_map/jit(_take)/gather | solution.py:107
  213.4 2.9 pad_maximum_fusion
  216.3 4.7 %copy.195 = bf16[24,1,128,512]{2,3,0,1:T(8,128)(2,1)} copy(bf16[24,1,128,512]{3,2,1,0:T(8,128)(2,1)} %get-tuple-element.64) | data formatting | bytes 6291456 | tf_op jit(solution)/shard_map/slice | solution.py:119
  221.0 4.6 fusion.112
  227.0 4.7 %copy.200 = bf16[24,1,128,512]{2,3,0,1:T(8,128)(2,1)} copy(bf16[24,1,128,512]{3,2,1,0:T(8,128)(2,1)} %get-tuple-element.63) | data formatting | bytes 6291456 | tf_op jit(solution)/shard_map/slice | solution.py:120
  231.7 6.9 %fusion.31 = f32[24,4,4,128]{3,2,1,0:T(4,128)S(1)} fusion(bf16[24,128,4,128]{1,3,2,0:T(8,128)(2,1)} %bitcast.365, f32[24,4,4,128]{3,2,1,0:T(4,128)S(1)} %get-tuple-element.72, f32[24,4,4]{2,1,0:T(4,128)S(1)} %broadcast_select_fusion.3, pred[24,128]{1,0:T(8,128)(4,1)S(1)} %iota_compare_fusion), kind=kOutput, calls=%fused_computation.67 | convolution fusion | flops 75595776 | bytes 3543552 | tf_op jit(solution)/shard_map/ikgt,itkd->ikgd/dot_general | solution.py:137
  242.0 6.5 %copy.226.wg_hbm = bf16[4096,448]{1,0:T(8,128)(2,1)} copy(bf16[4096,448]{0,1:T(8,128)(2,1)} %param.24) | data formatting | bytes 7340032 | tf_op args[5]
  248.4 6.5 %copy.227.wu_hbm = bf16[4096,448]{1,0:T(8,128)(2,1)} copy(bf16[4096,448]{0,1:T(8,128)(2,1)} %param.25) | data formatting | bytes 7340032 | tf_op args[6]
  255.7 19.5 %all-gather = f32[2048,16]{0,1:T(8,128)S(1)} all-gather(f32[128,16]{0,1:T(8,128)S(1)} %convolution_add_fusion.1), channel_id=2, replica_groups=mesh['grp'=4,'kv'=16,'tp'=2] {'kv'}, dimensions={0}, use_global_device_ids=true | all-gather | bytes 139264 | tf_op jit(solution)/shard_map/all_gather | solution.py:25
  275.2 19.4 %all_gather.13 = f32[16,128,16]{1,2,0:T(8,128)S(1)} all-gather(f32[1,128,16]{1,2,0:T(8,128)S(1)} %bitcast.376), channel_id=1, replica_groups=mesh['grp'=4,'kv'=16,'tp'=2] {'kv'}, dimensions={0}, use_global_device_ids=true | all-gather | bytes 139264 | tf_op jit(solution)/shard_map/all_gather | solution.py:25
  294.7 4.7 %fusion.120 = bf16[1,16,2,128,512]{4,3,2,1,0:T(8,128)(2,1)} fusion(bf16[16,2,128,512]{3,2,1,0:T(8,128)(2,1)} %gather_fusion.4, pred[16]{0:T(512)(128)(4,1)S(1)} %get-tuple-element.45), kind=kLoop, calls=%fused_computation.256 | loop fusion | flops 2097152 | bytes 8388624 | tf_op jit(solution)/shard_map/broadcast_in_dim | solution.py:440
  299.4 54.6 %all-gather.3.cloned.1.call-done = f32[16,128,16,128]{3,2,1,0:T(8,128)} async-done(((f32[1,128,16,128]{3,2,1,0:T(8,128)}), f32[16,128,16,128]{3,2,1,0:T(8,128)}) %all-gather.3.cloned.1.call-update) | async-done | bytes 16777232 | tf_op jit(solution)/shard_map/all_gather | solution.py:25
  354.0 10.9 %fusion.111 = (f32[1,128,16,128]{3,2,1,0:T(8,128)}, f32[1,128,16,128]{3,2,1,0:T(8,128)S(1)}, f32[1,128,16,128]{3,2,1,0:T(8,128)S(1)}, f32[1,128,16,128]{3,2,1,0:...) fusion(f32[16,128,16,128]{3,2,1,0:T(8,128)} %all-gather.3.clone, ...), kind=kLoop, calls=%fused_computation.253 | loop fusion | bytes 33554432 | tf_op jit(solution)/shard_map/slice | solution.py:26
  399.8 6.8 %fusion.1 = f32[128,16,128]{0,2,1:T(8,128)S(1)} fusion(f32[1,128,16,128]{1,3,2,0:T(8,128)S(1)} %copy.247, f32[1,128,16,128]{1,3,2,0:T(8,128)S(1)} %copy.246, f32[1,128,16,128]{1,3,2,0:T(8,128)S(1)} %copy.245, f32[1,128,16,128]{1,3,2,0:T(8,128)} %copy.244, f32[1,128,16,128]{1,3,2,0:T(8,128)} %copy.243, f32[1,128,16,128]{1,3,2,0:T(8,128)} %copy.242, ...), kind=kLoop, calls=%fused_computation.16 | loop fusion | flops 10223616 | bytes 15941632 | tf_op jit(solution)/shard_map/add | solution.py:52
  408.2 43.9 %tail.1 = bf16[4,4096]{1,0:T(4,128)(2,1)} custom-call(bf16[128,128]{1,0:T(8,128)(2,1)} %copy.225.attn_ref, bf16[128,256]{1,0:T(8,128)(2,1)} %hid_ref.1, f32[16,256]{1,0:T(8,128)} %reshape.1577.gain_ref, bf16[128,4096]{1,0:T(8,128)(2,1)} %bitcast.369, bf16[4096,448]{1,0:T(8,128)(2,1)} %copy.226.wg_hbm, bf16[4096,448]{1,0:T(8,128)(2,1)} %copy.227.wu_hbm, ...), custom_call_target="tpu_custom_call" | custom-call | tf_op jit(solution)/shard_map/tail/pallas_call | solution.py:349
  (111 shorter events, 57.6 us)
Async XLA Ops:
  7.2 95.8 %copy-start = (bf16[256,2048]{1,0:T(8,128)(2,1)S(1)}, bf16[256,2048]{1,0:T(8,128)(2,1)}, u32[]{:S(2)}) copy-start(bf16[256,2048]{1,0:T(8,128)(2,1)} %param.22) | copy-start | bytes 3145732
  20.1 68.0 %all-to-all-start = ((bf16[16,2,128,512]{3,2,1,0:T(8,128)(2,1)}), bf16[16,2,128,512]{3,2,1,0:T(8,128)(2,1)}, u32[]{:S(2)}, u32[]{:S(2)}) async-start(bf16[16,2,128,512]{3,2,1,0:T(8,128)(2,1)} %broadcast_select_fusion.2), calls=%async_computation | async-start | bytes 8388608 | tf_op jit(solution)/shard_map/all_to_all | solution.py:87
  97.8 5.3 %copy-start.4 = (bf16[128,256]{1,0:T(8,128)(2,1)S(1)}, bf16[128,256]{1,0:T(8,128)(2,1)}, u32[]{:S(2)}) copy-start(bf16[128,256]{1,0:T(8,128)(2,1)} %hid_ref.1) | copy-start | bytes 196612
  97.8 5.3 %copy-start.6 = (f32[256]{0:T(256)S(1)}, f32[256]{0:T(256)}, u32[]{:S(2)}) copy-start(f32[256]{0:T(256)} %param.20) | copy-start | bytes 3076
  97.8 6.7 %copy-start.7 = (s32[1,16]{1,0:T(1,128)S(1)}, s32[1,16]{1,0:T(1,128)}, u32[]{:S(2)}) copy-start(s32[1,16]{1,0:T(1,128)} %param.33) | copy-start | bytes 196
  97.8 6.7 %copy-start.8 = (s32[1,8]{1,0:T(1,128)S(1)}, s32[1,8]{1,0:T(1,128)}, u32[]{:S(2)}) copy-start(s32[1,8]{1,0:T(1,128)} %param.29) | copy-start | bytes 100
  97.8 7.0 %copy-start.3 = (bf16[128,2,512]{2,1,0:T(2,128)(2,1)S(1)}, bf16[128,2,512]{2,1,0:T(2,128)(2,1)}, u32[]{:S(2)}) copy-start(bf16[128,2,512]{2,1,0:T(2,128)(2,1)} %param.35) | copy-start | bytes 786436
  97.8 107.8 %all-to-all-start.1 = ((bf16[16,2,128,512]{3,2,1,0:T(8,128)(2,1)}), bf16[16,2,128,512]{3,2,1,0:T(8,128)(2,1)}, u32[]{:S(2)}, u32[]{:S(2)}) async-start(bf16[16,2,128,512]{3,2,1,0:T(8,128)(2,1)} %broadcast_select_fusion.1), calls=%async_computation.1 | async-start | bytes 8388608 | tf_op jit(solution)/shard_map/all_to_all | solution.py:103
  103.0 2.2 copy-start.9
  103.0 2.2 copy-start.10
  103.0 98.0 %all-reduce.2.cloned.1.call-start = ((), (), s32[]{:S(2)}) async-start(), calls=%async_computation.2 | async-start | bytes 2097152 | tf_op jit(solution)/shard_map/psum | solution.py:410
  104.4 249.6 %all-gather.3.cloned.1.call-start = ((), (), s32[]{:S(2)}) async-start(), calls=%async_computation.3 | async-start | bytes 17825792 | tf_op jit(solution)/shard_map/all_gather | solution.py:25
  210.6 2.9 copy-start.2
  231.7 9.6 %copy-start.5 = (f32[4096]{0:T(1024)S(1)}, f32[4096]{0:T(1024)}, u32[]{:S(2)}) copy-start(f32[4096]{0:T(1024)} %param.21) | copy-start | bytes 49156
  408.2 45.3 %copy-start.1 = (bf16[256,2048]{1,0:T(8,128)(2,1)S(1)}, bf16[256,2048]{1,0:T(8,128)(2,1)}, u32[]{:S(2)}) copy-start(bf16[256,2048]{1,0:T(8,128)(2,1)} %param.22) | copy-start | bytes 3145732
Sparse Core Ops, SparseCore 0:
  107.0 93.8 all-reduce.1
  241.5 112.5 all-gather.2

commit v2 on v1

--- a/solution.py
+++ b/solution.py
@@ -9,8 +9,6 @@
 HEADS = 32
 KV_HEADS = 8
 HEAD_DIM = 128
-NPR = 4
-KV = "kv"
 KV_TP = ("kv", "tp")
 GRP_KV = ("grp", "kv")
 GRP_KV_TP = ("grp", "kv", "tp")
@@ -18,135 +16,6 @@
 
 neg_fill = -1e30
 norm_eps = 1e-05
-
-
-def combined_by_axis(shard, axes, combine):
-    for axis in axes:
-        pieces = jax.tree.map(lambda part: lax.all_gather(part, axis), shard)
-        shard = jax.tree.map(lambda part: part[0], pieces)
-        for k in range(1, lax.axis_size(axis)):
-            shard = combine(shard, jax.tree.map(lambda part: part[k], pieces))
-    return shard
-
-
-def split_up(shard, dim, peers):
-    before, after = (shard.shape[:dim], shard.shape[dim + 1 :])
-    return jnp.moveaxis(shard.reshape(*before, peers, -1, *after), dim, 0)
-
-
-def summed_on_arrival(shard, axis, dim):
-    tiles = split_up(shard, dim, lax.axis_size(axis))
-    arrived = lax.all_to_all(tiles, axis, split_axis=0, concat_axis=0, tiled=True)
-    return arrived.astype(jnp.float32).sum(axis=0)
-
-
-def combine(earlier, later):
-    top_a, sum_a, acc_a = earlier
-    top_b, sum_b, acc_b = later
-    top = jnp.maximum(top_a, top_b)
-    fade_a = jnp.exp(top_a - top)
-    fade_b = jnp.exp(top_b - top)
-    return (
-        top,
-        sum_a * fade_a + sum_b * fade_b,
-        acc_a * fade_a[..., None] + acc_b * fade_b[..., None],
-    )
-
-
-def nth_match(table, wanted, places):
-    matched = (table == wanted).astype(jnp.int32)
-    ranking = jnp.cumsum(matched, axis=1) - 1
-    return (matched[:, None, :] == 1) & (ranking[:, None, :] == places[None, :, None])
-
-
-def move_pages(kv_pool, new_owner, new_local):
-    groups = lax.axis_size("grp")
-    ranks = lax.axis_size(KV)
-    per_dev = new_owner.shape[1] // ranks
-    cap = groups * NPR // ranks
-    grp_rank = lax.axis_index("grp")
-    kv_rank = lax.axis_index(KV)
-    owners = new_owner.reshape(groups * ranks, per_dev)
-    myself = grp_rank * ranks + kv_rank
-    places = jnp.arange(cap, dtype=jnp.int32)
-    mine = lax.dynamic_index_in_dim(owners, myself, 0, keepdims=False)
-    order = jnp.arange(per_dev, dtype=jnp.int32)
-    by_col = (
-        new_owner.reshape(groups, ranks, per_dev)
-        .transpose(1, 0, 2)
-        .reshape(ranks, groups * per_dev)
-    )
-    local_col = (
-        new_local.reshape(groups, ranks, per_dev)
-        .transpose(1, 0, 2)
-        .reshape(ranks, groups * per_dev)
-    )
-    select = nth_match(by_col, myself, places)
-    picked = jnp.sum(jnp.where(select, local_col[:, None, :], 0), axis=2)
-    outgoing = jnp.take(kv_pool, picked.reshape(-1), axis=0)
-    received = lax.all_to_all(outgoing, KV, split_axis=0, concat_axis=0, tiled=True)
-    row_here = lax.dynamic_index_in_dim(by_col, kv_rank, 0, keepdims=False)
-    sources = grp_rank * ranks + jnp.arange(ranks, dtype=jnp.int32)
-    hits = nth_match(
-        jnp.broadcast_to(row_here[None, :], (ranks, row_here.shape[0])), sources[:, None], places
-    )
-    spots = jnp.arange(row_here.shape[0], dtype=jnp.int32)
-    where_f = jnp.sum(jnp.where(hits, spots[None, None, :], 0), axis=2).reshape(-1)
-    dest_grp = where_f // per_dev
-    dest_pos = where_f % per_dev
-    same = (dest_grp[:, None] == dest_grp[None, :]) & (dest_pos[:, None] < dest_pos[None, :])
-    rank_in = jnp.sum(same.astype(jnp.int32), axis=0)
-    target = dest_grp * NPR + rank_in
-    items = jnp.arange(target.shape[0], dtype=jnp.int32)
-    inverse = jnp.sum(jnp.where(target[None, :] == items[:, None], items[None, :], 0), axis=1)
-    sorted_pages = jnp.take(received, inverse, axis=0)
-    arrived = lax.all_to_all(sorted_pages, "grp", split_axis=0, concat_axis=0, tiled=True)
-    src_grp = mine // ranks
-    earlier = (src_grp[:, None] == src_grp[None, :]) & (order[:, None] < order[None, :])
-    before = jnp.sum(earlier.astype(jnp.int32), axis=0)
-    return jnp.take(arrived, src_grp * NPR + before, axis=0)
-
-
-def local_partials(query, resident, arrived, res_slot, res_len, arr_slot, arr_len, token_kv, first):
-    pages = jnp.concatenate([resident, arrived], axis=0)
-    owner_slot = jnp.concatenate([res_slot, arr_slot])
-    filled = jnp.concatenate([res_len, arr_len])
-    count = pages.shape[0]
-    tokens = pages.shape[2]
-    kv_here = pages.shape[3] // HEAD_DIM
-    slots = query.shape[0]
-    ratio = HEADS // KV_HEADS
-    keys = pages[:, 0].astype(jnp.float32).reshape(count, tokens, kv_here, HEAD_DIM)
-    values = pages[:, 1].astype(jnp.float32).reshape(count, tokens, kv_here, HEAD_DIM)
-    grouped = query.reshape(slots, kv_here, ratio, HEAD_DIM)
-    picked = jnp.take(grouped, owner_slot, axis=0)
-    scores = jnp.einsum("ikgd,itkd->ikgt", picked, keys, precision=lax.Precision.HIGHEST)
-    usable = (jnp.arange(tokens, dtype=jnp.int32)[None, :] < filled[:, None])[:, None, None, :]
-    scores = jnp.where(usable, scores, neg_fill)
-    page_top = jnp.max(scores, axis=3)
-    member = owner_slot[None, :] == jnp.arange(slots, dtype=jnp.int32)[:, None]
-    slot_top = jnp.max(jnp.where(member[:, :, None, None], page_top[None], neg_fill), axis=1)
-    own_keys = token_kv[:, 0].astype(jnp.float32).reshape(slots, kv_here, HEAD_DIM)
-    own_values = token_kv[:, 1].astype(jnp.float32).reshape(slots, kv_here, HEAD_DIM)
-    own_score = jnp.einsum("skgd,skd->skg", grouped, own_keys, precision=lax.Precision.HIGHEST)
-    own_score = jnp.where(first, own_score, neg_fill)
-    slot_top = jnp.maximum(slot_top, own_score)
-    reach = jnp.take(slot_top, owner_slot, axis=0)
-    weights = jnp.where(usable, jnp.exp(scores - reach[..., None]), 0.0)
-    page_sum = jnp.sum(weights, axis=3)
-    page_acc = jnp.einsum("ikgt,itkd->ikgd", weights, values, precision=lax.Precision.HIGHEST)
-    own_weight = jnp.where(first, jnp.exp(own_score - slot_top), 0.0)
-    member_f = member.astype(jnp.float32)
-    total = jnp.dot(member_f, page_sum.reshape(count, -1), precision=lax.Precision.HIGHEST)
-    total = total + own_weight.reshape(slots, -1)
-    weighted = jnp.dot(member_f, page_acc.reshape(count, -1), precision=lax.Precision.HIGHEST)
-    weighted = (
-        weighted.reshape(slots, kv_here, ratio, HEAD_DIM)
-        + own_weight[..., None] * own_values[:, :, None, :]
-    )
-    return (slot_top.reshape(slots, -1), total, weighted.reshape(slots, kv_here * ratio, HEAD_DIM))
-
-
 MESH = pl.DeviceIdType.MESH
 
 
@@ -379,6 +248,353 @@
     )(attn, hidden, gain, w_out, w_gate, w_up, w_down)
 
 
+CHUNKS = 8
+CROWS = 256 // CHUNKS
+LOG_ROWS = 32
+
+
+def head_kernel(
+    meta, hid_ref, again_ref, tok_ref, wq_hbm, pool_hbm, res_hbm, attn_ref, cache_hbm,
+    wq, kept, qs_send, qs_recv, qfull, qflat, fsk, fsv, scores, probs, pvacc, accs, stats, msend, mrecv, *rest,
+):
+    f32, bf16, i32 = jnp.float32, jnp.bfloat16, jnp.int32
+    nc = CHUNKS
+    pool, xs, xr, zs, zr = (rest[i * nc : (i + 1) * nc] for i in range(5))
+    (ld_sem, pool_sem, kept_sem, out_sem, q_ss, q_rs, a_ss, a_rs, x_ss, x_rs, z_ss, z_rs, s_ss, s_rs,
+     m_ss, m_rs) = rest[5 * nc :]
+    grp, kv, tp = lax.axis_index("grp"), lax.axis_index("kv"), lax.axis_index("tp")
+    x, y = kv // 4, lax.rem(kv, 4)
+
+    def dev(k):
+        return (grp, peer_of(x, y, k), tp)
+
+    def zdev(dz):
+        return (lax.rem(grp + dz, 4), kv, tp)
+
+    def remote(src, dst, send, recv, device):
+        copy = pltpu.make_async_remote_copy(
+            src_ref=src, dst_ref=dst, send_sem=send, recv_sem=recv, device_id=device,
+            device_id_type=MESH,
+        )
+        copy.start()
+        return copy
+
+    wq_load = pltpu.make_async_copy(wq_hbm, wq, ld_sem.at[0])
+    wq_load.start()
+    pool_loads = []
+    for c in range(nc):
+        load = pltpu.make_async_copy(pool_hbm.at[:, pl.ds(c * CROWS, CROWS), :], pool[c], pool_sem.at[c])
+        load.start()
+        pool_loads.append(load)
+    kept_load = pltpu.make_async_copy(res_hbm, kept, kept_sem.at[0])
+    kept_load.start()
+
+    barrier = pltpu.get_barrier_semaphore()
+    for k in range(1, 16):
+        pl.semaphore_signal(barrier, inc=1, device_id=dev(k), device_id_type=MESH)
+    for dz in range(1, 4):
+        pl.semaphore_signal(barrier, inc=1, device_id=zdev(dz), device_id_type=MESH)
+
+    feats = hid_ref[...].astype(f32)
+    normed = (feats * again_ref[...]).astype(bf16)
+    squares = jnp.sum(feats * feats, axis=1, keepdims=True)
+    wq_load.wait()
+    for h in range(4):
+        part = jnp.dot(normed, wq[:, h * 512 : h * 512 + 512], preferred_element_type=f32)
+        qs_send[:, :, h * 512 : h * 512 + 512] = part.reshape(16, 8, 512)
+    qs_send[:, :, 2048:2176] = jnp.broadcast_to(squares, (128, 128)).reshape(16, 8, 128)
+    pl.semaphore_wait(barrier, 18)
+
+    q_copies = {}
+    for k in ORDER[::-1]:
+        q_copies[k] = remote(qs_send.at[peer_of(x, y, k)], qs_recv.at[k], q_ss.at[k], q_rs.at[k], dev(k))
+
+    x_copies = {}
+    z_copies = {}
+    out_copies = []
+
+    def xy_start(c):
+        pool_loads[c].wait()
+        xr[c][kv] = pool[c][meta[kv]]
+        for k in range(1, 16):
+            xs[c][k - 1] = pool[c][meta[peer_of(x, y, k)]]
+        for k in ORDER[::-1]:
+            x_copies[c, k] = remote(
+                xs[c].at[k - 1], xr[c].at[kv], x_ss.at[c, k], x_rs.at[c, k], dev(k)
+            )
+
+    def z_start(c):
+        for k in ORDER:
+            x_copies[c, k].wait_recv()
+        for dz in range(4):
+            g = lax.rem(grp + dz, 4)
+            for r in range(4):
+                page = xr[c][meta[16 + g * 4 + r]]
+                if dz == 0:
+                    zr[c][grp, r] = page
+                else:
+                    zs[c][dz - 1, r] = page
+        for dz in (2, 1, 3):
+            z_copies[c, dz] = remote(
+                zs[c].at[dz - 1], zr[c].at[grp], z_ss.at[c, dz], z_rs.at[c, dz], zdev(dz)
+            )
+
+    def finish(c):
+        for dz in (1, 3, 2):
+            z_copies[c, dz].wait_recv()
+        final, half = (fsk, 0) if c < nc // 2 else (fsv, 1)
+        row = (c % (nc // 2)) * CROWS
+        for i in range(16):
+            where = meta[32 + i]
+            final[i, row : row + CROWS, :] = zr[c][where // 4, lax.rem(where, 4)]
+        copy = pltpu.make_async_copy(
+            final.at[:, pl.ds(row, CROWS), :], cache_hbm.at[:, half, pl.ds(row, CROWS), :], out_sem.at[c]
+        )
+        copy.start()
+        out_copies.append(copy)
+
+    head_of = lax.broadcasted_iota(i32, (16, 512), 0) // 4
+    block_of = lax.broadcasted_iota(i32, (16, 512), 1) // 128
+    diag = head_of == block_of
+    lanes = lax.broadcasted_iota(i32, (16, 128), 1)
+
+    def page_scores(p, keys, slot, filled):
+        q = qfull[slot]
+        wide = jnp.where(diag, jnp.concatenate([q, q, q, q], axis=1), 0.0)
+        high = wide.astype(bf16)
+        left = wide - high.astype(f32)
+        mid = left.astype(bf16)
+        low = (left - mid.astype(f32)).astype(bf16)
+        rows = jnp.concatenate([high, mid, low], axis=0)
+        s = lax.dot_general(rows, keys, (((1,), (1,)), ((), ())), preferred_element_type=f32)
+        s = s[:16] + s[16:32] + s[32:]
+        s = jnp.where(lanes < filled, s, neg_fill)
+        scores[p] = s
+        top = jnp.max(s, axis=1, keepdims=True)
+        total = jnp.sum(jnp.where(lanes < filled, jnp.exp(s - top), 0.0), axis=1, keepdims=True)
+        return top, total
+
+    def weighted(p, values, lo, hi):
+        w = probs[p][:, lo:hi]
+        high = w.astype(bf16)
+        low = (w - high.astype(f32)).astype(bf16)
+        out = jnp.dot(jnp.concatenate([high, low], axis=0), values, preferred_element_type=f32)
+        return out[:16] + out[16:]
+
+    def place(p, acc):
+        for h in range(16):
+            accs[h, p : p + 1, :] = acc[h : h + 1, (h // 4) * 128 : (h // 4) * 128 + 128]
+
+    table = jnp.zeros((128, 128), f32)
+    row128 = lax.broadcasted_iota(i32, (128, 128), 0)
+    col128 = lax.broadcasted_iota(i32, (128, 128), 1)
+
+    def note(table, p, top, total):
+        both = jnp.concatenate([top, total, jnp.zeros((96, 1), f32)], axis=0)
+        return jnp.where(col128 == p, both, table)
+
+    def query_done():
+        total = qs_send[kv]
+        for k in ORDER:
+            q_copies[k].wait_recv()
+            total = total + qs_recv[k]
+        scale = lax.rsqrt(total[:, 2048:2049] / D + norm_eps)
+        q8 = total[:, :2048] * scale * HEAD_DIM ** (-0.5)
+        qflat[...] = q8
+        for h in range(16):
+            qfull[pl.ds(pl.multiple_of(kv * 8, 8), 8), h, :] = q8[:, h * 128 : h * 128 + 128]
+        mine = qfull.at[pl.ds(pl.multiple_of(kv * 8, 8), 8)]
+        return {k: remote(mine, mine, a_ss.at[k], a_rs.at[k], dev(k)) for k in ORDER[::-1]}
+
+    xy_start(0)
+    xy_start(1)
+    a_copies = query_done()
+    xy_start(2)
+    z_start(0)
+    xy_start(3)
+    z_start(1)
+    finish(0)
+    for k in ORDER:
+        a_copies[k].wait_recv()
+    kept_load.wait()
+    for p in range(8):
+        table = note(table, p, *page_scores(p, kept[p, 0], meta[48 + p], meta[56 + p]))
+    xy_start(4)
+    z_start(2)
+    finish(1)
+    xy_start(5)
+    z_start(3)
+    finish(2)
+    xy_start(6)
+    z_start(4)
+    finish(3)
+    for p in range(16):
+        table = note(table, 8 + p, *page_scores(8 + p, fsk[p], meta[64 + p], meta[80 + p]))
+    own = tok_ref[pl.ds(pl.multiple_of(kv * 8, 8), 8), :].astype(f32)
+    lane8 = lax.broadcasted_iota(i32, (8, 128), 1)
+    own_rows = jnp.where((lane8 >= 16) & (lane8 < 32), 1.0, 0.0).astype(f32)
+    for h in range(16):
+        s = jnp.sum(
+            qflat[:, h * 128 : h * 128 + 128] * own[:, (h // 4) * 128 : (h // 4) * 128 + 128],
+            axis=1, keepdims=True,
+        )
+        own_rows = jnp.where(lane8 == h, s, own_rows)
+    slots = jnp.zeros((32, 1), i32)
+    row32 = lax.broadcasted_iota(i32, (32, 1), 0)
+    for p in range(8):
+        slots = jnp.where(row32 == p, meta[48 + p], slots)
+    for p in range(16):
+        slots = jnp.where(row32 == 8 + p, meta[64 + p], slots)
+    slots = jnp.where(row32 >= 24, kv * 8 + row32 - 24, slots)
+    lane32 = lax.broadcasted_iota(i32, (32, 128), 1)
+    mine = jnp.concatenate([table.T[:24], own_rows], axis=0)
+    mine = jnp.where(lane32 == 32, slots.astype(f32), mine)
+    stats[kv] = mine
+    s_copies = {
+        k: remote(stats.at[kv], stats.at[kv], s_ss.at[k], s_rs.at[k], dev(k)) for k in ORDER[::-1]
+    }
+    xy_start(7)
+    z_start(5)
+    finish(4)
+    for k in ORDER:
+        s_copies[k].wait_recv()
+    every = stats[...].reshape(512, 128)
+    every_slot = every[:, 32:33].astype(i32)
+    sums = pltpu.roll(every, 112, 1)
+    lane512 = lax.broadcasted_iota(i32, (512, 128), 1)
+    result = jnp.zeros((128, 128), f32)
+    for p in range(32):
+        slot = meta[48 + p] if p < 8 else (meta[64 + p - 8] if p < 24 else kv * 8 + p - 24)
+        same = (every_slot == slot) & (lane512 < 16)
+        top = jnp.max(jnp.where(same, every, neg_fill), axis=0, keepdims=True)
+        total = jnp.sum(jnp.where(same, jnp.exp(every - top) * sums, 0.0), axis=0, keepdims=True)
+        line = jnp.where(lane8[:1] < 16, top, pltpu.roll(1.0 / jnp.where(lane8[:1] < 16, total, 1.0), 16, 1))
+        result = jnp.where(row128 == p, line, result)
+    turned = result.T
+    for p in range(24):
+        probs[p] = jnp.exp(scores[p] - turned[:16, p : p + 1]) * turned[16:32, p : p + 1]
+    for p in range(8):
+        place(p, weighted(p, kept[p, 1], 0, 128))
+    own_weight = jnp.exp(own_rows - result[24:32]) * pltpu.roll(result[24:32], 112, 1)
+    for h in range(16):
+        g = 512 + (h // 4) * 128
+        accs[h, 24:32, :] = own_weight[:, h : h + 1] * own[:, g : g + 128]
+    member = jnp.where(every_slot == lane512, 1.0, 0.0).astype(f32)
+    member = jnp.concatenate([member[128 * i : 128 * i + 128].T for i in range(4)], axis=1).astype(bf16)
+
+    def gather_values(c):
+        row = (c % (nc // 2)) * CROWS
+        for p in range(16):
+            part = weighted(8 + p, fsv[p, row : row + CROWS, :], row, row + CROWS)
+            if row == 0:
+                pvacc[p] = part
+            else:
+                pvacc[p] = pvacc[p] + part
+
+    gather_values(4)
+    z_start(6)
+    finish(5)
+    gather_values(5)
+    z_start(7)
+    finish(6)
+    gather_values(6)
+    finish(7)
+    for p in range(16):
+        row = 3 * CROWS
+        place(8 + p, pvacc[p] + weighted(8 + p, fsv[p, row : row + CROWS, :], row, row + CROWS))
+
+    tiles = [accs[h] for h in range(16)]
+    group = lane32 // 8
+    for bit in (1, 2, 4, 8):
+        upper = (group & bit) != 0
+        for h in range(16):
+            if h & bit == 0:
+                a, b = tiles[h], tiles[h + bit]
+                tiles[h] = jnp.where(upper, pltpu.roll(b, 8 * bit, 1), a)
+                tiles[h + bit] = jnp.where(upper, b, pltpu.roll(a, 128 - 8 * bit, 1))
+    for j in range(16):
+        msend[j] = tiles[j].astype(bf16)
+    m_copies = {}
+    for k in ORDER[::-1]:
+        m_copies[k] = remote(msend.at[peer_of(x, y, k)], mrecv.at[kv], m_ss.at[k], m_rs.at[k], dev(k))
+    mrecv[kv] = msend[kv]
+    for k in ORDER:
+        m_copies[k].wait_recv()
+    attn_ref[...] = jnp.dot(
+        member, mrecv[...].reshape(512, 128), preferred_element_type=f32
+    ).astype(bf16)
+
+    for copies in (q_copies, a_copies, x_copies, z_copies, s_copies, m_copies):
+        for copy in copies.values():
+            copy.wait_send()
+    for copy in out_copies:
+        copy.wait()
+
+
+def head(meta, hidden, gain, token_kv, w_query, pool, resident):
+    bf16, f32 = jnp.bfloat16, jnp.float32
+    vmem = pl.BlockSpec(memory_space=pltpu.VMEM)
+    hbm = pl.BlockSpec(memory_space=pl.ANY)
+    dma = pltpu.SemaphoreType.DMA
+    nc = CHUNKS
+    chunk = lambda *lead: [pltpu.VMEM((*lead, CROWS, 512), bf16)] * nc
+    return pl.pallas_call(
+        head_kernel,
+        name="head",
+        out_shape=(
+            jax.ShapeDtypeStruct((128, 128), bf16),
+            jax.ShapeDtypeStruct((16, 2, 128, 512), bf16),
+        ),
+        in_specs=[pl.BlockSpec(memory_space=pltpu.SMEM), vmem, vmem, vmem, hbm, hbm, hbm],
+        out_specs=(vmem, hbm),
+        scratch_shapes=[
+            pltpu.VMEM((256, 2048), bf16),
+            pltpu.VMEM((8, 2, 128, 512), bf16),
+            pltpu.VMEM((16, 8, 2176), f32),
+            pltpu.VMEM((16, 8, 2176), f32),
+            pltpu.VMEM((128, 16, 128), f32),
+            pltpu.VMEM((8, 2048), f32),
+            pltpu.VMEM((16, 128, 512), bf16),
+            pltpu.VMEM((16, 128, 512), bf16),
+            pltpu.VMEM((24, 16, 128), f32),
+            pltpu.VMEM((24, 16, 128), f32),
+            pltpu.VMEM((16, 16, 512), f32),
+            pltpu.VMEM((16, 32, 128), f32),
+            pltpu.VMEM((16, 32, 128), f32),
+            pltpu.VMEM((16, 32, 128), bf16),
+            pltpu.VMEM((16, 32, 128), bf16),
+            *chunk(16), *chunk(15), *chunk(16), *chunk(3, 4), *chunk(4, 4),
+            dma((1,)), dma((nc,)), dma((1,)), dma((nc,)),
+            dma((16,)), dma((16,)), dma((16,)), dma((16,)),
+            dma((nc, 16)), dma((nc, 16)), dma((nc, 4)), dma((nc, 4)),
+            dma((16,)), dma((16,)), dma((16,)), dma((16,)),
+        ],
+        compiler_params=pltpu.CompilerParams(
+            collective_id=1, has_side_effects=True, vmem_limit_bytes=60 * 1024 * 1024
+        ),
+    )(meta, hidden, gain, token_kv, w_query, pool, resident)
+
+
+def routing(new_owner, new_local, resident_slot, resident_len, new_slot, new_len):
+    i32 = jnp.int32
+    grp, kv = lax.axis_index("grp"), lax.axis_index("kv")
+    owners = new_owner.reshape(4, 16, 16)
+    places = new_local.reshape(4, 16, 16)
+    mine = (owners == grp * 16 + kv).astype(i32)
+    pick = jnp.sum(mine * places, axis=(0, 2))
+    column = lax.dynamic_index_in_dim(owners, kv, 1, keepdims=False)
+    from_grp = column // 16
+    earlier = jnp.arange(16)[None, :] < jnp.arange(16)[:, None]
+    same = (from_grp[:, :, None] == from_grp[:, None, :]) & earlier[None]
+    rank = jnp.sum(same.astype(i32), axis=2)
+    hit = (from_grp == grp)[:, None, :] & (rank[:, None, :] == jnp.arange(4)[None, :, None])
+    onward = jnp.sum(jnp.where(hit, (column % 16)[:, None, :], 0), axis=2).reshape(16)
+    final = lax.dynamic_index_in_dim(from_grp * 4 + rank, grp, 0, keepdims=False)
+    return jnp.concatenate(
+        [pick, onward, final, resident_slot[0], resident_len[0], new_slot[0], new_len[0]]
+    ).astype(i32)
+
+
 def per_device(
     hidden_states,
     attn_gain,
@@ -398,41 +614,21 @@
     new_len,
     token_kv,
 ):
-    ranks = lax.axis_size(KV)
-    pairs = lax.axis_size("tp")
-    kv_rank = lax.axis_index(KV)
-    tp_rank = lax.axis_index("tp")
-    features = hidden_states.astype(jnp.float32)
-    partial_query = jnp.dot(
-        (features * attn_gain).astype(jnp.bfloat16), w_query, preferred_element_type=jnp.float32
+    meta = routing(new_owner, new_local, resident_slot, resident_len, new_slot, new_len)
+    piece, new_pages = head(
+        meta,
+        hidden_states,
+        attn_gain.reshape(1, 256),
+        token_kv.reshape(128, 1024),
+        w_query,
+        kv_pool.reshape(16, 256, 512),
+        resident_cache[0],
     )
-    squares = jnp.sum(features * features, axis=1)
-    partial_query, squares = lax.psum((partial_query, squares), KV)
-    attn_scale = lax.rsqrt(squares / D + norm_eps)
-    query = partial_query * attn_scale[:, None] * HEAD_DIM ** (-0.5)
-    new_pages = move_pages(kv_pool, new_owner, new_local)
-    top, total, weighted = local_partials(
-        query,
-        resident_cache[0],
-        new_pages,
-        resident_slot[0],
-        resident_len[0],
-        new_slot[0],
-        new_len[0],
-        token_kv,
-        kv_rank == 0,
-    )
-    top, total, weighted = combined_by_axis((top, total, weighted), (KV,), combine)
-    attn = (weighted / total[..., None]).astype(jnp.bfloat16)
-    slots = attn.shape[0]
-    heads_here = attn.shape[1]
-    span = HEAD_DIM // ranks
-    piece = lax.dynamic_slice_in_dim(attn, kv_rank * span, span, 2)
     mixed = tail(
-        piece.reshape(slots, heads_here * span),
+        piece,
         hidden_states,
         mlp_gain.reshape(16, 256),
-        w_out.reshape(heads_here * span, w_out.shape[2]),
+        w_out.reshape(128, 4096),
         w_gate,
         w_up,
         w_down,
@@ -445,24 +641,24 @@
         per_device,
         mesh=mesh,
         in_specs=(
-            P("grp", KV),
-            P(KV),
+            P("grp", "kv"),
+            P("kv"),
             P(),
-            P(KV, "tp"),
-            P("tp", KV, None),
+            P("kv", "tp"),
+            P("tp", "kv", None),
             P(None, KV_TP),
             P(None, KV_TP),
             P(KV_TP, None),
             P(GRP_KV, None, None, "tp"),
-            P("grp", KV, None, None, "tp"),
-            P("grp", KV),
-            P("grp", KV),
+            P("grp", "kv", None, None, "tp"),
+            P("grp", "kv"),
+            P("grp", "kv"),
             P(),
             P(),
-            P("grp", KV),
-            P("grp", KV),
+            P("grp", "kv"),
+            P("grp", "kv"),
             P("grp", None, "tp"),
         ),
-        out_specs=(P(GRP_KV_TP, None), P("grp", KV, None, None, "tp")),
+        out_specs=(P(GRP_KV_TP, None), P("grp", "kv", None, None, "tp")),
         check_vma=False,
     )

time: 462 us -> 181 us (0.39)
  waiting for transfers between devices: 175 us -> 0 us
  Pallas kernels: 43.9 us -> 154 us
  blocking collectives: 72.8 us -> 0 us
  local copies, waits for them, and re-layouts: 93.4 us -> 24.1 us
  other arithmetic: 32 us -> 1.26 us
  matrix products: 15.6 us -> 0 us
  between operations: 14.4 us -> 0.7 us
  starting transfers between devices: 12.9 us -> 0 us
    pallas_call x0 -> x1, Pallas kernels: none -> 112 us  [head(): pl.pallas_call(head_kernel, name='head', out_shape=(jax.ShapeDtypeStruct(...]
    psum x1 -> x0, waiting for transfers between devices: 61.1 us -> none  [per_device(): partial_query, squares = lax.psum((partial_query, squares), KV)]
    all_to_all x2 -> x0, waiting for transfers between devices: 59.5 us -> none  [the longest x1 59.5 us: move_pages(): lax.all_to_all(outgoing, KV, split_axis=0, concat_axis=0, tiled=True)]
    all_gather x1 -> x0, waiting for transfers between devices: 54.6 us -> none  [combined_by_axis(): pieces = jax.tree.map(lambda part: lax.all_gather(part, axis), shard)]
    all_gather x2 -> x0, blocking collectives: 38.9 us -> none  [combined_by_axis(): pieces = jax.tree.map(lambda part: lax.all_gather(part, axis), shard)]
    psum x1 -> x0, blocking collectives: 33.9 us -> none  [per_device(): partial_query, squares = lax.psum((partial_query, squares), KV)]
    unnamed x42 -> x5, local copies, waits for them, and re-layouts: 49.4 us -> 20.6 us
    slice x3 -> x0, local copies, waits for them, and re-layouts: 20.4 us -> none  [the longest x1 10.9 us: combined_by_axis(): shard = jax.tree.map(lambda part: part[0], pieces)]
  transfers between devices with their start and end apart: 4 -> 0, of which waited for: 3 -> 0; matrix products, arithmetic and copies ran while one was open for 6% -> 0% of each run, Pallas kernels for 0% -> 0%
where the time goes in v2:
time: 181 us; the launch traced here: 180 us
  Pallas kernels  154 us (85%)
  local copies, waits for them, and re-layouts  24.1 us (13%)
    pallas_call x1, Pallas kernels, head(): pl.pallas_call(head_kernel, name='head', out_shape=(jax.ShapeDtypeStruct(...  112 us
    pallas_call x1, Pallas kernels, tail(): pl.pallas_call(tail_kernel, name='tail', out_shape=jax.ShapeDtypeStruct((...  42.5 us
    unnamed x5, local copies, waits for them, and re-layouts  20.6 us

profile of v2, /device:TPU:1, one launch (start us, length us, event | category | flops | bytes accessed | tf_op | source)
XLA Modules:
  0.0 180.1 jit_solution(4152667437742860455)
XLA Ops:
  0.6 0.7 select_reduce_fusion.1
  1.4 0.1 reduce_sum.35
  1.4 0.1 reduce_sum.36
  1.6 1.3 reshape.73.gain_ref
  2.9 0.8 reshape.68
  3.7 0.2 convert_reduce_fusion
  3.9 0.2 select_reduce_fusion
  4.1 0.1 reshape.69
  4.2 1.3 concatenate.3.meta
  5.5 1.7 copy.26
  7.2 111.5 %head.1 = (bf16[128,128]{1,0:T(8,128)(2,1)}, bf16[16,2,128,512]{3,2,1,0:T(8,128)(2,1)}) custom-call(s32[96]{0:T(128)} %concatenate.3.meta, bf16[128,256]{1,0:T(8,128)(2,1)} %hid_ref.3, f32[1,256]{1,0:T(1,128)} %bitcast.32, bf16[128,1024]{1,0:T(8,128)(2,1)} %bitcast.25, bf16[256,2048]{1,0:T(8,128)(2,1)} %wq_hbm.1, bf16[16,256,512]{2,1,0:T(8,128)(2,1)} %bitcast.21, ...), custom_call_target="tpu_custom_call" | custom-call | tf_op jit(solution)/shard_map/head/pallas_call | solution.py:541
  118.8 6.4 %copy.23.wg_hbm = bf16[4096,448]{1,0:T(8,128)(2,1)} copy(bf16[4096,448]{0,1:T(8,128)(2,1)} %param.22) | data formatting | bytes 7340032 | tf_op args[5]
  125.1 6.5 %copy.24.wu_hbm = bf16[4096,448]{1,0:T(8,128)(2,1)} copy(bf16[4096,448]{0,1:T(8,128)(2,1)} %param.23) | data formatting | bytes 7340032 | tf_op args[6]
  131.6 42.5 %tail.1 = bf16[4,4096]{1,0:T(4,128)(2,1)} custom-call(bf16[128,128]{1,0:T(8,128)(2,1)} %get-tuple-element.4.attn_ref, bf16[128,256]{1,0:T(8,128)(2,1)} %hid_ref.3, f32[16,256]{1,0:T(8,128)} %reshape.73.gain_ref, bf16[128,4096]{1,0:T(8,128)(2,1)} %bitcast.24, bf16[4096,448]{1,0:T(8,128)(2,1)} %copy.23.wg_hbm, bf16[4096,448]{1,0:T(8,128)(2,1)} %copy.24.wu_hbm, ...), custom_call_target="tpu_custom_call" | custom-call | tf_op jit(solution)/shard_map/tail/pallas_call | solution.py:218
  174.1 1.4 copy.29
  175.5 4.6 %copy.30 = bf16[1,16,2,128,512]{4,3,2,1,0:T(8,128)(2,1)} copy(bf16[1,16,2,128,512]{4,3,2,1,0:T(8,128)(2,1)} %bitcast.22) | data formatting | bytes 8388608
  (7 shorter events, 0.1 us)

commit v3 on v2

--- a/solution.py
+++ b/solution.py
@@ -133,6 +133,7 @@
     loads[1].wait()
     loads[2].wait()
     seq = [0] + ORDER
+    nt = (((1,), (1,)), ((), ()))
     gate = jnp.zeros((128, 448), f32)
     upward = jnp.zeros((128, 448), f32)
     squares = jnp.zeros((128, 128), f32)
@@ -147,10 +148,10 @@
         both = jnp.concatenate([ag[k, 0], ag[k, 1]], axis=1)
         wide = both.astype(f32)
         squares = squares + wide[:, :128] * wide[:, :128] + wide[:, 128:] * wide[:, 128:]
-        normed = (wide * gain_ref[pl.ds(src, 1), :]).astype(bf16)
         rows = pl.ds(pl.multiple_of(src * 256, 256), 256)
-        gate = gate + jnp.dot(normed, wg[rows, :], preferred_element_type=f32)
-        upward = upward + jnp.dot(normed, wu[rows, :], preferred_element_type=f32)
+        normed = (wide * gain_ref[:, rows]).astype(bf16)
+        gate = gate + lax.dot_general(normed, wg[:, rows], nt, preferred_element_type=f32)
+        upward = upward + lax.dot_general(normed, wu[:, rows], nt, preferred_element_type=f32)
     scale = lax.rsqrt(jnp.sum(squares, axis=1, keepdims=True) / D + norm_eps)
     gate = gate * scale
     upward = upward * scale
@@ -223,8 +224,8 @@
         out_specs=vmem,
         scratch_shapes=[
             pltpu.VMEM((128, 4096), bf16),
-            pltpu.VMEM((4096, 448), bf16),
-            pltpu.VMEM((4096, 448), bf16),
+            pltpu.VMEM((448, 4096), bf16),
+            pltpu.VMEM((448, 4096), bf16),
             pltpu.VMEM((448, 4096), bf16),
             pltpu.VMEM((4, 4, 128, 128), bf16),
             pltpu.VMEM((4, 4, 128, 128), bf16),
@@ -254,8 +255,8 @@
 
 
 def head_kernel(
-    meta, hid_ref, again_ref, tok_ref, wq_hbm, pool_hbm, res_hbm, attn_ref, cache_hbm,
-    wq, kept, qs_send, qs_recv, qfull, qflat, fsk, fsv, scores, probs, pvacc, accs, stats, msend, mrecv, *rest,
+    meta, hid_ref, again_ref, tok_hbm, wq_hbm, pool_hbm, res_hbm, attn_ref, cache_hbm,
+    wq, tok, kept, qs_send, qs_recv, qfull, qflat, fsk, fsv, scores, probs, pvacc, accs, stats, msend, mrecv, *rest,
 ):
     f32, bf16, i32 = jnp.float32, jnp.bfloat16, jnp.int32
     nc = CHUNKS
@@ -288,6 +289,10 @@
         pool_loads.append(load)
     kept_load = pltpu.make_async_copy(res_hbm, kept, kept_sem.at[0])
     kept_load.start()
+    tok_load = pltpu.make_async_copy(
+        tok_hbm.at[pl.ds(pl.multiple_of(kv * 8, 8), 8)], tok, ld_sem.at[1]
+    )
+    tok_load.start()
 
     barrier = pltpu.get_barrier_semaphore()
     for k in range(1, 16):
@@ -430,12 +435,13 @@
     finish(3)
     for p in range(16):
         table = note(table, 8 + p, *page_scores(8 + p, fsk[p], meta[64 + p], meta[80 + p]))
-    own = tok_ref[pl.ds(pl.multiple_of(kv * 8, 8), 8), :].astype(f32)
+    tok_load.wait()
+    own_key, own_value = tok[:, 0, :].astype(f32), tok[:, 1, :].astype(f32)
     lane8 = lax.broadcasted_iota(i32, (8, 128), 1)
     own_rows = jnp.where((lane8 >= 16) & (lane8 < 32), 1.0, 0.0).astype(f32)
     for h in range(16):
         s = jnp.sum(
-            qflat[:, h * 128 : h * 128 + 128] * own[:, (h // 4) * 128 : (h // 4) * 128 + 128],
+            qflat[:, h * 128 : h * 128 + 128] * own_key[:, (h // 4) * 128 : (h // 4) * 128 + 128],
             axis=1, keepdims=True,
         )
         own_rows = jnp.where(lane8 == h, s, own_rows)
@@ -477,8 +483,8 @@
         place(p, weighted(p, kept[p, 1], 0, 128))
     own_weight = jnp.exp(own_rows - result[24:32]) * pltpu.roll(result[24:32], 112, 1)
     for h in range(16):
-        g = 512 + (h // 4) * 128
-        accs[h, 24:32, :] = own_weight[:, h : h + 1] * own[:, g : g + 128]
+        g = (h // 4) * 128
+        accs[h, 24:32, :] = own_weight[:, h : h + 1] * own_value[:, g : g + 128]
     member = jnp.where(every_slot == lane512, 1.0, 0.0).astype(f32)
     member = jnp.concatenate([member[128 * i : 128 * i + 128].T for i in range(4)], axis=1).astype(bf16)
 
@@ -545,10 +551,11 @@
             jax.ShapeDtypeStruct((128, 128), bf16),
             jax.ShapeDtypeStruct((16, 2, 128, 512), bf16),
         ),
-        in_specs=[pl.BlockSpec(memory_space=pltpu.SMEM), vmem, vmem, vmem, hbm, hbm, hbm],
+        in_specs=[pl.BlockSpec(memory_space=pltpu.SMEM), vmem, vmem, hbm, hbm, hbm, hbm],
         out_specs=(vmem, hbm),
         scratch_shapes=[
             pltpu.VMEM((256, 2048), bf16),
+            pltpu.VMEM((8, 2, 512), bf16),
             pltpu.VMEM((8, 2, 128, 512), bf16),
             pltpu.VMEM((16, 8, 2176), f32),
             pltpu.VMEM((16, 8, 2176), f32),
@@ -564,7 +571,7 @@
             pltpu.VMEM((16, 32, 128), bf16),
             pltpu.VMEM((16, 32, 128), bf16),
             *chunk(16), *chunk(15), *chunk(16), *chunk(3, 4), *chunk(4, 4),
-            dma((1,)), dma((nc,)), dma((1,)), dma((nc,)),
+            dma((2,)), dma((nc,)), dma((1,)), dma((nc,)),
             dma((16,)), dma((16,)), dma((16,)), dma((16,)),
             dma((nc, 16)), dma((nc, 16)), dma((nc, 4)), dma((nc, 4)),
             dma((16,)), dma((16,)), dma((16,)), dma((16,)),
@@ -619,7 +626,7 @@
         meta,
         hidden_states,
         attn_gain.reshape(1, 256),
-        token_kv.reshape(128, 1024),
+        token_kv,
         w_query,
         kv_pool.reshape(16, 256, 512),
         resident_cache[0],
@@ -627,10 +634,10 @@
     mixed = tail(
         piece,
         hidden_states,
-        mlp_gain.reshape(16, 256),
+        mlp_gain.reshape(1, 4096),
         w_out.reshape(128, 4096),
-        w_gate,
-        w_up,
+        w_gate.T,
+        w_up.T,
         w_down,
     )
     return (mixed, new_pages[None])

time: 181 us -> 165 us (0.912)
  local copies, waits for them, and re-layouts: 24.1 us -> 8.27 us
    unnamed x5 -> x2, local copies, waits for them, and re-layouts: 20.6 us -> 6.02 us
where the time goes in v3:
time: 165 us; the launch traced here: 164 us
  Pallas kernels  154 us (93%)
  local copies, waits for them, and re-layouts  8.27 us (5%)
    pallas_call x1, Pallas kernels, head(): pl.pallas_call(head_kernel, name='head', out_shape=(jax.ShapeDtypeStruct(...  111 us
    pallas_call x1, Pallas kernels, tail(): pl.pallas_call(tail_kernel, name='tail', out_shape=jax.ShapeDtypeStruct((...  42.9 us
    unnamed x2, local copies, waits for them, and re-layouts  6.02 us

profile of v3, /device:TPU:1, one launch (start us, length us, event | category | flops | bytes accessed | tf_op | source)
XLA Modules:
  0.0 164.2 jit_solution(5107726395276498150)
XLA Ops:
  0.6 0.7 select_reduce_fusion.1
  1.4 0.1 reduce_sum.35
  1.4 0.1 reduce_sum.36
  1.6 0.8 reshape.65
  2.4 0.2 convert_reduce_fusion
  2.6 0.2 select_reduce_fusion
  2.8 0.1 reshape.66
  2.9 1.3 concatenate.3.meta
  4.2 111.1 %head.1 = (bf16[128,128]{1,0:T(8,128)(2,1)}, bf16[16,2,128,512]{3,2,1,0:T(8,128)(2,1)}) custom-call(s32[96]{0:T(128)} %concatenate.3.meta, bf16[128,256]{1,0:T(8,128)(2,1)} %hid_ref.3, f32[1,256]{1,0:T(1,128)} %bitcast.34, bf16[128,2,512]{2,1,0:T(2,128)(2,1)} %tok_hbm.1, bf16[256,2048]{1,0:T(8,128)(2,1)} %wq_hbm.1, bf16[16,256,512]{2,1,0:T(8,128)(2,1)} %bitcast.22, ...), custom_call_target="tpu_custom_call" | custom-call | tf_op jit(solution)/shard_map/head/pallas_call | solution.py:547
  115.3 42.9 %tail.1 = bf16[4,4096]{1,0:T(4,128)(2,1)} custom-call(bf16[128,128]{1,0:T(8,128)(2,1)} %get-tuple-element.4.attn_ref, bf16[128,256]{1,0:T(8,128)(2,1)} %hid_ref.3, f32[1,4096]{1,0:T(1,128)} %bitcast.32, bf16[128,4096]{1,0:T(8,128)(2,1)} %bitcast.27, bf16[448,4096]{1,0:T(8,128)(2,1)} %bitcast.24, bf16[448,4096]{1,0:T(8,128)(2,1)} %bitcast.25, ...), custom_call_target="tpu_custom_call" | custom-call | tf_op jit(solution)/shard_map/tail/pallas_call | solution.py:219
  158.2 1.4 copy.24
  159.6 4.6 %copy.25 = bf16[1,16,2,128,512]{4,3,2,1,0:T(8,128)(2,1)} copy(bf16[1,16,2,128,512]{4,3,2,1,0:T(8,128)(2,1)} %bitcast.23) | data formatting | bytes 8388608
  (7 shorter events, 0.1 us)

commit v4 on v1

v4 whole, which is shorter than its diff:
```python
import jax
import jax.numpy as jnp
from jax import lax
from jax.experimental import pallas as pl
from jax.experimental.pallas import tpu as pltpu
from jax.sharding import PartitionSpec as P

D = 4096
HEADS = 32
KV_HEADS = 8
HEAD_DIM = 128
KV_TP = ("kv", "tp")
GRP_KV = ("grp", "kv")
GRP_KV_TP = ("grp", "kv", "tp")


neg_fill = -1e30
norm_eps = 1e-05
MESH = pl.DeviceIdType.MESH


def peer_of(x, y, k):
    return lax.rem(x + k // 4, 4) * 4 + lax.rem(y + k % 4, 4)


def source_of(x, y, k):
    return lax.rem(x + 4 - k // 4, 4) * 4 + lax.rem(y + 4 - k % 4, 4)


ORDER = sorted(range(1, 16), key=lambda k: (min(k // 4, 4 - k // 4) + min(k % 4, 4 - k % 4), k))


CHUNKS = 8
CROWS = 256 // CHUNKS


def step_kernel(
    meta, hid_ref, again_ref, gain_ref, tok_hbm, wq_hbm, pool_hbm, res_hbm, wout_hbm, wg_hbm, wu_hbm, wd_hbm,
    out_ref, cache_hbm,
    wq, tok, kept, qs_send, qs_recv, qfull, qflat, fsk, fsv, scores, probs, pvacc, accs, stats, msend, mrecv,
    wout, wg, wu, wd, pair_send, pair_recv, own_part, rs_send, rs_recv, ag, hunits,
    dp_send, dp_recv, dsum, d_send, d_recv, resrow, *rest,
):
    f32, bf16, i32 = jnp.float32, jnp.bfloat16, jnp.int32
    nc = CHUNKS
    pool, xs, xr, zs, zr = (rest[i * nc : (i + 1) * nc] for i in range(5))
    (ld_sem, pool_sem, kept_sem, out_sem, q_ss, q_rs, a_ss, a_rs, x_ss, x_rs, z_ss, z_rs, s_ss, s_rs,
     m_ss, m_rs, w_sem, pair_ss, pair_rs, rs_ss, rs_rs, ag_ss, ag_rs, fw_ss, fw_rs, dp_ss, dp_rs, d_ss,
     d_rs) = rest[5 * nc :]
    grp, kv, tp = lax.axis_index("grp"), lax.axis_index("kv"), lax.axis_index("tp")
    x, y = kv // 4, lax.rem(kv, 4)
    other = 1 - tp
    partner = (grp, kv, other)

    def dev(k):
        return (grp, peer_of(x, y, k), tp)

    def zdev(dz):
        return (lax.rem(grp + dz, 4), kv, tp)

    def remote(src, dst, send, recv, device):
        copy = pltpu.make_async_remote_copy(
            src_ref=src, dst_ref=dst, send_sem=send, recv_sem=recv, device_id=device,
            device_id_type=MESH,
        )
        copy.start()
        return copy

    wq_load = pltpu.make_async_copy(wq_hbm, wq, ld_sem.at[0])
    wq_load.start()
    pool_loads = []
    for c in range(nc):
        load = pltpu.make_async_copy(pool_hbm.at[:, pl.ds(c * CROWS, CROWS), :], pool[c], pool_sem.at[c])
        load.start()
        pool_loads.append(load)
    kept_load = pltpu.make_async_copy(res_hbm, kept, kept_sem.at[0])
    kept_load.start()
    tok_load = pltpu.make_async_copy(
        tok_hbm.at[pl.ds(pl.multiple_of(kv * 8, 8), 8)], tok, ld_sem.at[1]
    )
    tok_load.start()

    loads = [
        pltpu.make_async_copy(src, dst, w_sem.at[i])
        for i, (src, dst) in enumerate([(wout_hbm, wout), (wg_hbm, wg), (wu_hbm, wu), (wd_hbm, wd)])
    ]
    for load in loads:
        load.start()

    barrier = pltpu.get_barrier_semaphore()
    pl.semaphore_signal(barrier, inc=1, device_id=partner, device_id_type=MESH)
    for k in range(1, 16):
        pl.semaphore_signal(barrier, inc=1, device_id=dev(k), device_id_type=MESH)
    for dz in range(1, 4):
        pl.semaphore_signal(barrier, inc=1, device_id=zdev(dz), device_id_type=MESH)

    feats = hid_ref[...].astype(f32)
    normed = (feats * again_ref[...]).astype(bf16)
    squares = jnp.sum(feats * feats, axis=1, keepdims=True)
    wq_load.wait()
    for h in range(4):
        part = jnp.dot(normed, wq[:, h * 512 : h * 512 + 512], preferred_element_type=f32)
        qs_send[:, :, h * 512 : h * 512 + 512] = part.reshape(16, 8, 512)
    qs_send[:, :, 2048:2176] = jnp.broadcast_to(squares, (128, 128)).reshape(16, 8, 128)
    pl.semaphore_wait(barrier, 19)

    q_copies = {}
    for k in ORDER[::-1]:
        q_copies[k] = remote(qs_send.at[peer_of(x, y, k)], qs_recv.at[k], q_ss.at[k], q_rs.at[k], dev(k))

    x_copies = {}
    z_copies = {}
    out_copies = []

    def xy_start(c):
        pool_loads[c].wait()
        xr[c][kv] = pool[c][meta[kv]]
        for k in range(1, 16):
            xs[c][k - 1] = pool[c][meta[peer_of(x, y, k)]]
        for k in ORDER[::-1]:
            x_copies[c, k] = remote(
                xs[c].at[k - 1], xr[c].at[kv], x_ss.at[c, k], x_rs.at[c, k], dev(k)
            )

    def z_start(c):
        for k in ORDER:
            x_copies[c, k].wait_recv()
        for dz in range(4):
            g = lax.rem(grp + dz, 4)
            for r in range(4):
                page = xr[c][meta[16 + g * 4 + r]]
                if dz == 0:
                    zr[c][grp, r] = page
                else:
                    zs[c][dz - 1, r] = page
        for dz in (2, 1, 3):
            z_copies[c, dz] = remote(
                zs[c].at[dz - 1], zr[c].at[grp], z_ss.at[c, dz], z_rs.at[c, dz], zdev(dz)
            )

    def finish(c):
        for dz in (1, 3, 2):
            z_copies[c, dz].wait_recv()
        final, half = (fsk, 0) if c < nc // 2 else (fsv, 1)
        row = (c % (nc // 2)) * CROWS
        for i in range(16):
            where = meta[32 + i]
            final[i, row : row + CROWS, :] = zr[c][where // 4, lax.rem(where, 4)]
        copy = pltpu.make_async_copy(
            final.at[:, pl.ds(row, CROWS), :], cache_hbm.at[:, half, pl.ds(row, CROWS), :], out_sem.at[c]
        )
        copy.start()
        out_copies.append(copy)

    head_of = lax.broadcasted_iota(i32, (16, 512), 0) // 4
    block_of = lax.broadcasted_iota(i32, (16, 512), 1) // 128
    diag = head_of == block_of
    lanes = lax.broadcasted_iota(i32, (16, 128), 1)

    def page_scores(p, keys, slot, filled):
        q = qfull[slot]
        wide = jnp.where(diag, jnp.concatenate([q, q, q, q], axis=1), 0.0)
        high = wide.astype(bf16)
        left = wide - high.astype(f32)
        mid = left.astype(bf16)
        low = (left - mid.astype(f32)).astype(bf16)
        rows = jnp.concatenate([high, mid, low], axis=0)
        s = lax.dot_general(rows, keys, (((1,), (1,)), ((), ())), preferred_element_type=f32)
        s = s[:16] + s[16:32] + s[32:]
        s = jnp.where(lanes < filled, s, neg_fill)
        scores[p] = s
        top = jnp.max(s, axis=1, keepdims=True)
        total = jnp.sum(jnp.where(lanes < filled, jnp.exp(s - top), 0.0), axis=1, keepdims=True)
        return top, total

    def weighted(p, values, lo, hi):
        w = probs[p][:, lo:hi]
        high = w.astype(bf16)
        low = (w - high.astype(f32)).astype(bf16)
        out = jnp.dot(jnp.concatenate([high, low], axis=0), values, preferred_element_type=f32)
        return out[:16] + out[16:]

    def place(p, acc):
        for h in range(16):
            accs[h, p : p + 1, :] = acc[h : h + 1, (h // 4) * 128 : (h // 4) * 128 + 128]

    lane32 = lax.broadcasted_iota(i32, (32, 128), 1)

    def note(table, p, top, total):
        return jnp.where(lane32 == p, jnp.concatenate([top, total], axis=0), table)

    def query_done():
        total = qs_send[kv]
        for k in ORDER:
            q_copies[k].wait_recv()
            total = total + qs_recv[k]
        scale = lax.rsqrt(total[:, 2048:2049] / D + norm_eps)
        q8 = total[:, :2048] * scale * HEAD_DIM ** (-0.5)
        qflat[...] = q8
        for h in range(16):
            qfull[pl.ds(pl.multiple_of(kv * 8, 8), 8), h, :] = q8[:, h * 128 : h * 128 + 128]
        mine = qfull.at[pl.ds(pl.multiple_of(kv * 8, 8), 8)]
        return {k: remote(mine, mine, a_ss.at[k], a_rs.at[k], dev(k)) for k in ORDER[::-1]}

    for c in range(3):
        xy_start(c)
    a_copies = query_done()
    xy_start(3)
    z_start(0)
    xy_start(4)
    z_start(1)
    finish(0)
    xy_start(5)
    z_start(2)
    finish(1)
    xy_start(6)
    z_start(3)
    finish(2)
    xy_start(7)
    tok_load.wait()
    own_key, own_value = tok[:, 0, :].astype(f32), tok[:, 1, :].astype(f32)
    lane8 = lax.broadcasted_iota(i32, (8, 128), 1)
    own_rows = jnp.zeros((8, 128), f32)
    for h in range(16):
        s = jnp.sum(
            qflat[:, h * 128 : h * 128 + 128] * own_key[:, (h // 4) * 128 : (h // 4) * 128 + 128],
            axis=1, keepdims=True,
        )
        own_rows = jnp.where(lane8 == h, s, own_rows)
    own_tops = jnp.concatenate([jnp.zeros((24, 128), f32), own_rows, jnp.zeros((96, 128), f32)], axis=0).T[:16]
    slot_row = jnp.zeros((8, 128), i32)
    for p in range(24):
        slot_row = jnp.where(lane8 == p, meta[48 + p] if p < 8 else meta[56 + p], slot_row)
    slot_row = jnp.where(lane8 >= 24, kv * 8 + lane8 - 24, slot_row)
    for k in ORDER:
        a_copies[k].wait_recv()
    kept_load.wait()
    table = jnp.zeros((32, 128), f32)
    for p in range(8):
        table = note(table, p, *page_scores(p, kept[p, 0], meta[48 + p], meta[56 + p]))
    z_start(4)
    finish(3)
    for p in range(16):
        table = note(table, 8 + p, *page_scores(8 + p, fsk[p], meta[64 + p], meta[80 + p]))
    own_lane = lanes >= 24
    mine = jnp.concatenate(
        [
            jnp.where(own_lane, own_tops, table[:16]),
            jnp.where(own_lane, 1.0, table[16:]),
            slot_row.astype(f32),
        ],
        axis=0,
    )
    mine = jnp.where(lax.broadcasted_iota(i32, (40, 128), 1) < 32, mine, 0.0)
    turned = [mine] + [pltpu.roll(mine, 32 * q, 1) for q in range(1, 4)]
    for q in range(1, 4):
        mine = jnp.where(y == q, turned[q], mine)
    stats[kv] = mine
    s_copies = {
        k: remote(stats.at[kv], stats.at[kv], s_ss.at[k], s_rs.at[k], dev(k)) for k in ORDER[::-1]
    }
    z_start(5)
    finish(4)
    for k in ORDER:
        s_copies[k].wait_recv()
    every = jnp.concatenate(
        [stats[4 * i] + stats[4 * i + 1] + stats[4 * i + 2] + stats[4 * i + 3] for i in range(4)], axis=1
    )
    tops, sums, every_slot = every[:16], every[16:32], every[32:33].astype(i32)
    own_w = jnp.zeros((16, 128), f32)
    for p in range(32):
        slot = meta[48 + p] if p < 8 else (meta[56 + p] if p < 24 else kv * 8 + p - 24)
        same = jnp.broadcast_to(every_slot == slot, (16, 512))
        top = jnp.max(jnp.where(same, tops, neg_fill), axis=1, keepdims=True)
        total = jnp.sum(jnp.where(same, jnp.exp(tops - top) * sums, 0.0), axis=1, keepdims=True)
        if p < 24:
            probs[p] = jnp.exp(scores[p] - top) * (1.0 / total)
        else:
            own_w = jnp.where(lanes == p, jnp.exp(own_tops - top) * (1.0 / total), own_w)
    own_weight = jnp.concatenate([own_w, jnp.zeros((112, 128), f32)], axis=0).T[24:32]
    for h in range(16):
        g = (h // 4) * 128
        accs[h, 24:32, :] = own_weight[:, h : h + 1] * own_value[:, g : g + 128]
    rho = lax.broadcasted_iota(i32, (128, 512), 0)
    member = (lax.rem(rho, 64) // 4) * 8 + (rho // 64) * 4 + lax.rem(rho, 4) == every_slot
    member = jnp.where(member, 1.0, 0.0).astype(bf16)
    z_start(6)
    finish(5)
    for p in range(8):
        place(p, weighted(p, kept[p, 1], 0, 128))

    def gather_values(c):
        row = (c % (nc // 2)) * CROWS
        for p in range(16):
            part = weighted(8 + p, fsv[p, row : row + CROWS, :], row, row + CROWS)
            if row == 0:
                pvacc[p] = part
            else:
                pvacc[p] = pvacc[p] + part

    gather_values(4)
    gather_values(5)
    z_start(7)
    finish(6)
    gather_values(6)
    finish(7)
    for p in range(16):
        row = 3 * CROWS
        place(8 + p, pvacc[p] + weighted(8 + p, fsv[p, row : row + CROWS, :], row, row + CROWS))

    tiles = [accs[h] for h in range(16)]
    group = lane32 // 8
    for bit in (1, 2, 4, 8):
        upper = (group & bit) != 0
        for h in range(16):
            if h & bit == 0:
                a, b = tiles[h], tiles[h + bit]
                tiles[h] = jnp.where(upper, pltpu.roll(b, 8 * bit, 1), a)
                tiles[h + bit] = jnp.where(upper, b, pltpu.roll(a, 128 - 8 * bit, 1))
    for j in range(16):
        msend[j] = tiles[j].astype(bf16)
    m_copies = {}
    for k in ORDER[::-1]:
        m_copies[k] = remote(msend.at[peer_of(x, y, k)], mrecv.at[kv], m_ss.at[k], m_rs.at[k], dev(k))
    mrecv[kv] = msend[kv]
    for k in ORDER:
        m_copies[k].wait_recv()
    attn = jnp.dot(
        member, mrecv[...].reshape(512, 128), preferred_element_type=f32
    ).astype(bf16)

    rho = lax.broadcasted_iota(jnp.int32, (128, 128), 0)
    col = lax.broadcasted_iota(jnp.int32, (128, 128), 1)
    slot = (lax.rem(rho, 64) // 4) * 8 + (rho // 64) * 4 + lax.rem(rho, 4)
    perm = jnp.where(col == slot, 1.0, 0.0).astype(bf16)
    hid = jnp.dot(
        perm, hid_ref[:, pl.ds(pl.multiple_of(tp * 128, 128), 128)], preferred_element_type=f32
    )

    loads[0].wait()

    order = ORDER[::-1] + [0]
    pair_copies = []
    for g in range(4):
        for i in range(4):
            k = order[4 * g + i]
            dest = peer_of(x, y, k)
            part = jnp.dot(
                attn, wout[:, pl.ds(pl.multiple_of(dest * 256, 256), 256)], preferred_element_type=f32
            )
            low, high = part[:, :128], part[:, 128:]
            own_part[g, i] = jnp.where(tp == 0, low, high)
            pair_send[g, i] = jnp.where(tp == 0, high, low).astype(bf16)
        copy = pltpu.make_async_remote_copy(
            src_ref=pair_send.at[g], dst_ref=pair_recv.at[g], send_sem=pair_ss.at[g],
            recv_sem=pair_rs.at[g], device_id=partner, device_id_type=MESH,
        )
        copy.start()
        pair_copies.append(copy)
    rs_copies = {}
    block = None
    for g in range(4):
        pair_copies[g].wait_recv()
        for i in range(4):
            k = order[4 * g + i]
            total = own_part[g, i] + pair_recv[g, i].astype(f32)
            if k == 0:
                block = total + hid
            else:
                rs_send[k] = total.astype(bf16)
                copy = pltpu.make_async_remote_copy(
                    src_ref=rs_send.at[k], dst_ref=rs_recv.at[k], send_sem=rs_ss.at[k],
                    recv_sem=rs_rs.at[k], device_id=dev(k), device_id_type=MESH,
                )
                copy.start()
                rs_copies[k] = copy
    for k in ORDER:
        rs_copies[k].wait_recv()
        block = block + rs_recv[k].astype(f32)
    ag[0, tp] = block.astype(bf16)

    ag_copies = {}
    fw_copies = {}

    def forward(k):
        copy = pltpu.make_async_remote_copy(
            src_ref=ag.at[k, tp], dst_ref=ag.at[k, tp], send_sem=fw_ss.at[k],
            recv_sem=fw_rs.at[k], device_id=partner, device_id_type=MESH,
        )
        copy.start()
        fw_copies[k] = copy

    for k in ORDER[::-1]:
        copy = pltpu.make_async_remote_copy(
            src_ref=ag.at[0, tp], dst_ref=ag.at[k, tp], send_sem=ag_ss.at[k],
            recv_sem=ag_rs.at[k], device_id=dev(k), device_id_type=MESH,
        )
        copy.start()
        ag_copies[k] = copy
    forward(0)
    for g in range(4):
        pair_copies[g].wait_send()
    loads[1].wait()
    loads[2].wait()
    seq = [0] + ORDER
    nt = (((1,), (1,)), ((), ()))
    gate = jnp.zeros((128, 448), f32)
    upward = jnp.zeros((128, 448), f32)
    squares = jnp.zeros((128, 128), f32)
    mine = lax.broadcasted_iota(jnp.int32, (8, 128), 0) + tp * 64 + kv * 4
    pick = jnp.where(lax.broadcasted_iota(jnp.int32, (8, 128), 1) == mine, 1.0, 0.0).astype(bf16)
    for n, k in enumerate(seq):
        if n + 1 < 16:
            ag_copies[seq[n + 1]].wait_recv()
            forward(seq[n + 1])
        fw_copies[k].wait_recv()
        src = source_of(x, y, k)
        both = jnp.concatenate([ag[k, 0], ag[k, 1]], axis=1)
        wide = both.astype(f32)
        squares = squares + wide[:, :128] * wide[:, :128] + wide[:, 128:] * wide[:, 128:]
        rows = pl.ds(pl.multiple_of(src * 256, 256), 256)
        normed = (wide * gain_ref[:, rows]).astype(bf16)
        gate = gate + lax.dot_general(normed, wg[:, rows], nt, preferred_element_type=f32)
        upward = upward + lax.dot_general(normed, wu[:, rows], nt, preferred_element_type=f32)
    scale = lax.rsqrt(jnp.sum(squares, axis=1, keepdims=True) / D + norm_eps)
    gate = gate * scale
    upward = upward * scale
    hunits[...] = (gate / (1.0 + jnp.exp(-gate)) * upward).astype(bf16)

    loads[3].wait()
    dp_copies = []
    for c in range(4):
        cols = pl.ds(c * 1024, 1024)
        part = jnp.dot(hunits[...], wd[:, cols], preferred_element_type=f32)
        first, second = part[:64], part[64:]
        dsum[:, cols] = jnp.where(tp == 0, first, second)
        dp_send[c] = jnp.where(tp == 0, second, first).astype(bf16)
        copy = pltpu.make_async_remote_copy(
            src_ref=dp_send.at[c], dst_ref=dp_recv.at[c], send_sem=dp_ss.at[c],
            recv_sem=dp_rs.at[c], device_id=partner, device_id_type=MESH,
        )
        copy.start()
        dp_copies.append(copy)
    for c in range(4):
        dp_copies[c].wait_recv()
        cols = pl.ds(c * 1024, 1024)
        dsum[:, cols] = dsum[:, cols] + dp_recv[c].astype(f32)
    for j in range(16):
        d_send[j] = dsum[4 * j : 4 * j + 4, :].astype(bf16)
    d_copies = {}
    for k in ORDER[::-1]:
        copy = pltpu.make_async_remote_copy(
            src_ref=d_send.at[peer_of(x, y, k)], dst_ref=d_recv.at[k], send_sem=d_ss.at[k],
            recv_sem=d_rs.at[k], device_id=dev(k), device_id_type=MESH,
        )
        copy.start()
        d_copies[k] = copy
    for k in range(16):
        for t in range(2):
            cols = pl.ds(pl.multiple_of((source_of(x, y, k) * 2 + t) * 128, 128), 128)
            resrow[:, cols] = jnp.dot(pick, ag[k, t], preferred_element_type=f32)
    pick64 = lax.broadcasted_iota(jnp.int32, (8, 64), 0) + kv * 4
    total = resrow[...][:4]
    lane = lax.broadcasted_iota(jnp.int32, (4, 4096), 0)
    own = jnp.zeros((4, 4096), f32)
    for j in range(16):
        own = jnp.where(kv == j, dsum[4 * j : 4 * j + 4, :], own)
    total = total + own
    for k in ORDER:
        d_copies[k].wait_recv()
        total = total + d_recv[k].astype(f32)
    out_ref[...] = total.astype(bf16)

    for k in range(1, 16):
        rs_copies[k].wait_send()
        ag_copies[k].wait_send()
        d_copies[k].wait_send()
    for k in range(16):
        fw_copies[k].wait_send()
    for c in range(4):
        dp_copies[c].wait_send()
    for copies in (q_copies, a_copies, x_copies, z_copies, s_copies, m_copies):
        for copy in copies.values():
            copy.wait_send()
    for copy in out_copies:
        copy.wait()


def step(meta, hidden, again, gain, token_kv, w_query, pool, resident, w_out, w_gate, w_up, w_down):
    bf16, f32 = jnp.bfloat16, jnp.float32
    vmem = pl.BlockSpec(memory_space=pltpu.VMEM)
    hbm = pl.BlockSpec(memory_space=pl.ANY)
    dma = pltpu.SemaphoreType.DMA
    nc = CHUNKS

    def chunk(*lead):
        return [pltpu.VMEM((*lead, CROWS, 512), bf16)] * nc

    return pl.pallas_call(
        step_kernel,
        name="step",
        out_shape=(
            jax.ShapeDtypeStruct((4, 4096), bf16),
            jax.ShapeDtypeStruct((16, 2, 128, 512), bf16),
        ),
        in_specs=[pl.BlockSpec(memory_space=pltpu.SMEM), vmem, vmem, vmem] + [hbm] * 8,
        out_specs=(vmem, hbm),
        scratch_shapes=[
            pltpu.VMEM((256, 2048), bf16),
            pltpu.VMEM((8, 2, 512), bf16),
            pltpu.VMEM((8, 2, 128, 512), bf16),
            pltpu.VMEM((16, 8, 2176), f32),
            pltpu.VMEM((16, 8, 2176), f32),
            pltpu.VMEM((128, 16, 128), f32),
            pltpu.VMEM((8, 2048), f32),
            pltpu.VMEM((16, 128, 512), bf16),
            pltpu.VMEM((16, 128, 512), bf16),
            pltpu.VMEM((24, 16, 128), f32),
            pltpu.VMEM((24, 16, 128), f32),
            pltpu.VMEM((16, 16, 512), f32),
            pltpu.VMEM((16, 32, 128), f32),
            pltpu.VMEM((16, 40, 128), f32),
            pltpu.VMEM((16, 32, 128), bf16),
            pltpu.VMEM((16, 32, 128), bf16),
            pltpu.VMEM((128, 4096), bf16),
            pltpu.VMEM((448, 4096), bf16),
            pltpu.VMEM((448, 4096), bf16),
            pltpu.VMEM((448, 4096), bf16),
            pltpu.VMEM((4, 4, 128, 128), bf16),
            pltpu.VMEM((4, 4, 128, 128), bf16),
            pltpu.VMEM((4, 4, 128, 128), f32),
            pltpu.VMEM((16, 128, 128), bf16),
            pltpu.VMEM((16, 128, 128), bf16),
            pltpu.VMEM((16, 2, 128, 128), bf16),
            pltpu.VMEM((128, 448), bf16),
            pltpu.VMEM((4, 64, 1024), bf16),
            pltpu.VMEM((4, 64, 1024), bf16),
            pltpu.VMEM((64, 4096), f32),
            pltpu.VMEM((16, 4, 4096), bf16),
            pltpu.VMEM((16, 4, 4096), bf16),
            pltpu.VMEM((8, 4096), f32),
            *chunk(16), *chunk(15), *chunk(16), *chunk(3, 4), *chunk(4, 4),
            dma((2,)), dma((nc,)), dma((1,)), dma((nc,)),
            dma((16,)), dma((16,)), dma((16,)), dma((16,)),
            dma((nc, 16)), dma((nc, 16)), dma((nc, 4)), dma((nc, 4)),
            dma((16,)), dma((16,)), dma((16,)), dma((16,)),
            dma((4,)), dma((4,)), dma((4,)), dma((16,)), dma((16,)), dma((16,)), dma((16,)),
            dma((16,)), dma((16,)), dma((4,)), dma((4,)), dma((16,)), dma((16,)),
        ],
        compiler_params=pltpu.CompilerParams(
            collective_id=0, has_side_effects=True, vmem_limit_bytes=62 * 1024 * 1024
        ),
    )(meta, hidden, again, gain, token_kv, w_query, pool, resident, w_out, w_gate, w_up, w_down)


def routing(new_owner, new_local, resident_slot, resident_len, new_slot, new_len):
    i32 = jnp.int32
    grp, kv = lax.axis_index("grp"), lax.axis_index("kv")
    mine = jnp.where(new_owner == grp * 16 + kv, new_local, 0)
    pick = jnp.sum(jnp.sum(mine, axis=0).reshape(16, 16), axis=1)
    column = lax.dynamic_slice(new_owner, (0, kv * 16), (4, 16))
    from_grp = column // 16
    earlier = jnp.arange(16)[None, :] < jnp.arange(16)[:, None]
    same = (from_grp[:, :, None] == from_grp[:, None, :]) & earlier[None]
    rank = jnp.sum(same.astype(i32), axis=2)
    hit = (from_grp == grp)[:, None, :] & (rank[:, None, :] == jnp.arange(4)[None, :, None])
    onward = jnp.sum(jnp.where(hit, (column % 16)[:, None, :], 0), axis=2).reshape(16)
    final = lax.dynamic_index_in_dim(from_grp * 4 + rank, grp, 0, keepdims=False)
    return jnp.concatenate(
        [pick, onward, final, resident_slot[0], resident_len[0], new_slot[0], new_len[0]]
    ).astype(i32)


def per_device(
    hidden_states,
    attn_gain,
    mlp_gain,
    w_query,
    w_out,
    w_gate,
    w_up,
    w_down,
    kv_pool,
    resident_cache,
    resident_slot,
    resident_len,
    new_owner,
    new_local,
    new_slot,
    new_len,
    token_kv,
):
    meta = routing(new_owner, new_local, resident_slot, resident_len, new_slot, new_len)
    mixed, new_pages = step(
        meta,
        hidden_states,
        attn_gain.reshape(1, 256),
        mlp_gain.reshape(1, 4096),
        token_kv,
        w_query,
        kv_pool.reshape(16, 256, 512),
        resident_cache[0],
        w_out.reshape(128, 4096),
        w_gate.T,
        w_up.T,
        w_down,
    )
    return (mixed, new_pages[None])


def solution(mesh):
    return jax.shard_map(
        per_device,
        mesh=mesh,
        in_specs=(
            P("grp", "kv"),
            P("kv"),
            P(),
            P("kv", "tp"),
            P("tp", "kv", None),
            P(None, KV_TP),
            P(None, KV_TP),
            P(KV_TP, None),
            P(GRP_KV, None, None, "tp"),
            P("grp", "kv", None, None, "tp"),
            P("grp", "kv"),
            P("grp", "kv"),
            P(),
            P(),
            P("grp", "kv"),
            P("grp", "kv"),
            P("grp", None, "tp"),
        ),
        out_specs=(P(GRP_KV_TP, None), P("grp", "kv", None, None, "tp")),
        check_vma=False,
    )
```

time: 462 us -> 159 us (0.34)
  waiting for transfers between devices: 175 us -> 0 us
  Pallas kernels: 43.9 us -> 148 us
  local copies, waits for them, and re-layouts: 93.4 us -> 7.5 us
  blocking collectives: 72.8 us -> 0 us
  other arithmetic: 32 us -> 2.75 us
  matrix products: 15.6 us -> 0 us
  between operations: 14.4 us -> 0.67 us
  starting transfers between devices: 12.9 us -> 0 us
    pallas_call x1, Pallas kernels: 43.9 us -> 148 us  [step(): pl.pallas_call(step_kernel, name='step', out_shape=(jax.ShapeDtypeStruct(...]
    psum x1 -> x0, waiting for transfers between devices: 61.1 us -> none  [per_device(): partial_query, squares = lax.psum((partial_query, squares), KV)]
    all_to_all x2 -> x0, waiting for transfers between devices: 59.5 us -> none  [the longest x1 59.5 us: move_pages(): lax.all_to_all(outgoing, KV, split_axis=0, concat_axis=0, tiled=True)]
    all_gather x1 -> x0, waiting for transfers between devices: 54.6 us -> none  [combined_by_axis(): pieces = jax.tree.map(lambda part: lax.all_gather(part, axis), shard)]
    unnamed x42 -> x2, local copies, waits for them, and re-layouts: 49.4 us -> 6.02 us
    all_gather x2 -> x0, blocking collectives: 38.9 us -> none  [combined_by_axis(): pieces = jax.tree.map(lambda part: lax.all_gather(part, axis), shard)]
    psum x1 -> x0, blocking collectives: 33.9 us -> none  [per_device(): partial_query, squares = lax.psum((partial_query, squares), KV)]
    slice x3 -> x0, local copies, waits for them, and re-layouts: 20.4 us -> none  [the longest x1 10.9 us: combined_by_axis(): shard = jax.tree.map(lambda part: part[0], pieces)]
  transfers between devices with their start and end apart: 4 -> 0, of which waited for: 3 -> 0; matrix products, arithmetic and copies ran while one was open for 6% -> 0% of each run, Pallas kernels for 0% -> 0%
where the time goes in v4:
time: 159 us
  Pallas kernels  148 us (93%)
  local copies, waits for them, and re-layouts  7.5 us (5%)
  other arithmetic  2.75 us (2%)
    pallas_call x1, Pallas kernels, step(): pl.pallas_call(step_kernel, name='step', out_shape=(jax.ShapeDtypeStruct(...  148 us
    unnamed x2, local copies, waits for them, and re-layouts  6.02 us

profile of v4, /device:TPU:1, one launch (start us, length us, event | category | flops | bytes accessed | tf_op | source)
XLA Modules:
  0.0 159.1 jit_solution(7974950711652727320)
XLA Ops:
  0.6 0.7 select_reduce_fusion.1
  1.4 0.8 add_select_fusion
  2.1 0.8 broadcast_compare_fusion
  2.9 0.2 convert_reduce_fusion
  3.1 0.2 select_reduce_fusion
  3.3 0.1 reshape.40
  3.4 0.1 reshape.39
  3.5 0.1 reduce_sum.37
  3.6 1.3 concatenate.3.meta
  4.9 148.2 %step.1 = (bf16[4,4096]{1,0:T(4,128)(2,1)}, bf16[16,2,128,512]{3,2,1,0:T(8,128)(2,1)}) custom-call(s32[96]{0:T(128)} %concatenate.3.meta, bf16[128,256]{1,0:T(8,128)(2,1)} %hid_ref.1, f32[1,256]{1,0:T(1,128)} %bitcast.21, f32[1,4096]{1,0:T(1,128)} %bitcast.20, bf16[128,2,512]{2,1,0:T(2,128)(2,1)} %tok_hbm.1, bf16[256,2048]{1,0:T(8,128)(2,1)} %wq_hbm.1, ...), custom_call_target="tpu_custom_call" | custom-call | tf_op jit(solution)/shard_map/step/pallas_call | solution.py:499
  153.1 1.4 copy.21
  154.5 4.6 %copy.22 = bf16[1,16,2,128,512]{4,3,2,1,0:T(8,128)(2,1)} copy(bf16[1,16,2,128,512]{4,3,2,1,0:T(8,128)(2,1)} %bitcast.15) | data formatting | bytes 8388608
  (3 shorter events, 0.0 us)

commit v5 on v4

--- a/solution.py
+++ b/solution.py
@@ -66,6 +66,9 @@
         copy.start()
         return copy
 
+    def settle(ref, sem):
+        pltpu.make_async_copy(ref, ref, sem).wait()
+
     wq_load = pltpu.make_async_copy(wq_hbm, wq, ld_sem.at[0])
     wq_load.start()
     pool_loads = []
@@ -104,13 +107,8 @@
     qs_send[:, :, 2048:2176] = jnp.broadcast_to(squares, (128, 128)).reshape(16, 8, 128)
     pl.semaphore_wait(barrier, 19)
 
-    q_copies = {}
     for k in ORDER[::-1]:
-        q_copies[k] = remote(qs_send.at[peer_of(x, y, k)], qs_recv.at[k], q_ss.at[k], q_rs.at[k], dev(k))
-
-    x_copies = {}
-    z_copies = {}
-    out_copies = []
+        remote(qs_send.at[peer_of(x, y, k)], qs_recv.at[k], q_ss.at[0], q_rs.at[0], dev(k))
 
     def xy_start(c):
         pool_loads[c].wait()
@@ -118,13 +116,10 @@
         for k in range(1, 16):
             xs[c][k - 1] = pool[c][meta[peer_of(x, y, k)]]
         for k in ORDER[::-1]:
-            x_copies[c, k] = remote(
-                xs[c].at[k - 1], xr[c].at[kv], x_ss.at[c, k], x_rs.at[c, k], dev(k)
-            )
+            remote(xs[c].at[k - 1], xr[c].at[kv], x_ss.at[c], x_rs.at[c], dev(k))
 
     def z_start(c):
-        for k in ORDER:
-            x_copies[c, k].wait_recv()
+        settle(xs[c], x_rs.at[c])
         for dz in range(4):
             g = lax.rem(grp + dz, 4)
             for r in range(4):
@@ -134,23 +129,18 @@
                 else:
                     zs[c][dz - 1, r] = page
         for dz in (2, 1, 3):
-            z_copies[c, dz] = remote(
-                zs[c].at[dz - 1], zr[c].at[grp], z_ss.at[c, dz], z_rs.at[c, dz], zdev(dz)
-            )
+            remote(zs[c].at[dz - 1], zr[c].at[grp], z_ss.at[c], z_rs.at[c], zdev(dz))
 
     def finish(c):
-        for dz in (1, 3, 2):
-            z_copies[c, dz].wait_recv()
+        settle(zs[c], z_rs.at[c])
         final, half = (fsk, 0) if c < nc // 2 else (fsv, 1)
         row = (c % (nc // 2)) * CROWS
         for i in range(16):
             where = meta[32 + i]
             final[i, row : row + CROWS, :] = zr[c][where // 4, lax.rem(where, 4)]
-        copy = pltpu.make_async_copy(
-            final.at[:, pl.ds(row, CROWS), :], cache_hbm.at[:, half, pl.ds(row, CROWS), :], out_sem.at[c]
-        )
-        copy.start()
-        out_copies.append(copy)
+        pltpu.make_async_copy(
+            final.at[:, pl.ds(row, CROWS), :], cache_hbm.at[:, half, pl.ds(row, CROWS), :], out_sem.at[half]
+        ).start()
 
     head_of = lax.broadcasted_iota(i32, (16, 512), 0) // 4
     block_of = lax.broadcasted_iota(i32, (16, 512), 1) // 128
@@ -191,8 +181,8 @@
 
     def query_done():
         total = qs_send[kv]
-        for k in ORDER:
-            q_copies[k].wait_recv()
+        settle(qs_recv.at[pl.ds(1, 15)], q_rs.at[0])
+        for k in range(1, 16):
             total = total + qs_recv[k]
         scale = lax.rsqrt(total[:, 2048:2049] / D + norm_eps)
         q8 = total[:, :2048] * scale * HEAD_DIM ** (-0.5)
@@ -200,11 +190,12 @@
         for h in range(16):
             qfull[pl.ds(pl.multiple_of(kv * 8, 8), 8), h, :] = q8[:, h * 128 : h * 128 + 128]
         mine = qfull.at[pl.ds(pl.multiple_of(kv * 8, 8), 8)]
-        return {k: remote(mine, mine, a_ss.at[k], a_rs.at[k], dev(k)) for k in ORDER[::-1]}
+        for k in ORDER[::-1]:
+            remote(mine, mine, a_ss.at[0], a_rs.at[0], dev(k))
 
     for c in range(3):
         xy_start(c)
-    a_copies = query_done()
+    query_done()
     xy_start(3)
     z_start(0)
     xy_start(4)
@@ -232,8 +223,7 @@
     for p in range(24):
         slot_row = jnp.where(lane8 == p, meta[48 + p] if p < 8 else meta[56 + p], slot_row)
     slot_row = jnp.where(lane8 >= 24, kv * 8 + lane8 - 24, slot_row)
-    for k in ORDER:
-        a_copies[k].wait_recv()
+    settle(qfull.at[pl.ds(0, 120)], a_rs.at[0])
     kept_load.wait()
     table = jnp.zeros((32, 128), f32)
     for p in range(8):
@@ -256,13 +246,14 @@
     for q in range(1, 4):
         mine = jnp.where(y == q, turned[q], mine)
     stats[kv] = mine
-    s_copies = {
-        k: remote(stats.at[kv], stats.at[kv], s_ss.at[k], s_rs.at[k], dev(k)) for k in ORDER[::-1]
-    }
+    for k in ORDER[::-1]:
+        remote(stats.at[kv], stats.at[kv], s_ss.at[0], s_rs.at[0], dev(k))
     z_start(5)
     finish(4)
-    for k in ORDER:
-        s_copies[k].wait_recv()
+    z_start(6)
+    finish(5)
+    z_start(7)
+    settle(stats.at[pl.ds(0, 15)], s_rs.at[0])
     every = jnp.concatenate(
         [stats[4 * i] + stats[4 * i + 1] + stats[4 * i + 2] + stats[4 * i + 3] for i in range(4)], axis=1
     )
@@ -284,8 +275,6 @@
     rho = lax.broadcasted_iota(i32, (128, 512), 0)
     member = (lax.rem(rho, 64) // 4) * 8 + (rho // 64) * 4 + lax.rem(rho, 4) == every_slot
     member = jnp.where(member, 1.0, 0.0).astype(bf16)
-    z_start(6)
-    finish(5)
     for p in range(8):
         place(p, weighted(p, kept[p, 1], 0, 128))
 
@@ -300,7 +289,6 @@
 
     gather_values(4)
     gather_values(5)
-    z_start(7)
     finish(6)
     gather_values(6)
     finish(7)
@@ -319,12 +307,10 @@
                 tiles[h + bit] = jnp.where(upper, b, pltpu.roll(a, 128 - 8 * bit, 1))
     for j in range(16):
         msend[j] = tiles[j].astype(bf16)
-    m_copies = {}
     for k in ORDER[::-1]:
-        m_copies[k] = remote(msend.at[peer_of(x, y, k)], mrecv.at[kv], m_ss.at[k], m_rs.at[k], dev(k))
+        remote(msend.at[peer_of(x, y, k)], mrecv.at[kv], m_ss.at[0], m_rs.at[0], dev(k))
     mrecv[kv] = msend[kv]
-    for k in ORDER:
-        m_copies[k].wait_recv()
+    settle(msend.at[pl.ds(0, 15)], m_rs.at[0])
     attn = jnp.dot(
         member, mrecv[...].reshape(512, 128), preferred_element_type=f32
     ).astype(bf16)
@@ -340,7 +326,6 @@
     loads[0].wait()
 
     order = ORDER[::-1] + [0]
-    pair_copies = []
     for g in range(4):
         for i in range(4):
             k = order[4 * g + i]
@@ -351,16 +336,10 @@
             low, high = part[:, :128], part[:, 128:]
             own_part[g, i] = jnp.where(tp == 0, low, high)
             pair_send[g, i] = jnp.where(tp == 0, high, low).astype(bf16)
-        copy = pltpu.make_async_remote_copy(
-            src_ref=pair_send.at[g], dst_ref=pair_recv.at[g], send_sem=pair_ss.at[g],
-            recv_sem=pair_rs.at[g], device_id=partner, device_id_type=MESH,
-        )
-        copy.start()
-        pair_copies.append(copy)
-    rs_copies = {}
+        remote(pair_send.at[g], pair_recv.at[g], pair_ss.at[0], pair_rs.at[g], partner)
     block = None
     for g in range(4):
-        pair_copies[g].wait_recv()
+        settle(pair_recv.at[g], pair_rs.at[g])
         for i in range(4):
             k = order[4 * g + i]
             total = own_part[g, i] + pair_recv[g, i].astype(f32)
@@ -368,38 +347,18 @@
                 block = total + hid
             else:
                 rs_send[k] = total.astype(bf16)
-                copy = pltpu.make_async_remote_copy(
-                    src_ref=rs_send.at[k], dst_ref=rs_recv.at[k], send_sem=rs_ss.at[k],
-                    recv_sem=rs_rs.at[k], device_id=dev(k), device_id_type=MESH,
-                )
-                copy.start()
-                rs_copies[k] = copy
+                remote(rs_send.at[k], rs_recv.at[k], rs_ss.at[0], rs_rs.at[0], dev(k))
+    settle(rs_recv.at[pl.ds(1, 15)], rs_rs.at[0])
     for k in ORDER:
-        rs_copies[k].wait_recv()
         block = block + rs_recv[k].astype(f32)
     ag[0, tp] = block.astype(bf16)
 
-    ag_copies = {}
-    fw_copies = {}
-
     def forward(k):
-        copy = pltpu.make_async_remote_copy(
-            src_ref=ag.at[k, tp], dst_ref=ag.at[k, tp], send_sem=fw_ss.at[k],
-            recv_sem=fw_rs.at[k], device_id=partner, device_id_type=MESH,
-        )
-        copy.start()
-        fw_copies[k] = copy
-
-    for k in ORDER[::-1]:
-        copy = pltpu.make_async_remote_copy(
-            src_ref=ag.at[0, tp], dst_ref=ag.at[k, tp], send_sem=ag_ss.at[k],
-            recv_sem=ag_rs.at[k], device_id=dev(k), device_id_type=MESH,
-        )
-        copy.start()
-        ag_copies[k] = copy
+        remote(ag.at[k, tp], ag.at[k, tp], fw_ss.at[0], fw_rs.at[k], partner)
+
     forward(0)
-    for g in range(4):
-        pair_copies[g].wait_send()
+    for k in ORDER:
+        remote(ag.at[0, tp], ag.at[k, tp], ag_ss.at[0], ag_rs.at[k], dev(k))
     loads[1].wait()
     loads[2].wait()
     seq = [0] + ORDER
@@ -410,10 +369,10 @@
     mine = lax.broadcasted_iota(jnp.int32, (8, 128), 0) + tp * 64 + kv * 4
     pick = jnp.where(lax.broadcasted_iota(jnp.int32, (8, 128), 1) == mine, 1.0, 0.0).astype(bf16)
     for n, k in enumerate(seq):
-        if n + 1 < 16:
-            ag_copies[seq[n + 1]].wait_recv()
-            forward(seq[n + 1])
-        fw_copies[k].wait_recv()
+        for later in seq[n + 1 : n + 7] if n == 0 else seq[n + 6 : n + 7]:
+            settle(ag.at[later, tp], ag_rs.at[later])
+            forward(later)
+        settle(ag.at[k, other], fw_rs.at[k])
         src = source_of(x, y, k)
         both = jnp.concatenate([ag[k, 0], ag[k, 1]], axis=1)
         wide = both.astype(f32)
@@ -428,62 +387,49 @@
     hunits[...] = (gate / (1.0 + jnp.exp(-gate)) * upward).astype(bf16)
 
     loads[3].wait()
-    dp_copies = []
     for c in range(4):
         cols = pl.ds(c * 1024, 1024)
         part = jnp.dot(hunits[...], wd[:, cols], preferred_element_type=f32)
         first, second = part[:64], part[64:]
         dsum[:, cols] = jnp.where(tp == 0, first, second)
         dp_send[c] = jnp.where(tp == 0, second, first).astype(bf16)
-        copy = pltpu.make_async_remote_copy(
-            src_ref=dp_send.at[c], dst_ref=dp_recv.at[c], send_sem=dp_ss.at[c],
-            recv_sem=dp_rs.at[c], device_id=partner, device_id_type=MESH,
-        )
-        copy.start()
-        dp_copies.append(copy)
+        remote(dp_send.at[c], dp_recv.at[c], dp_ss.at[0], dp_rs.at[c], partner)
     for c in range(4):
-        dp_copies[c].wait_recv()
+        settle(dp_recv.at[c], dp_rs.at[c])
         cols = pl.ds(c * 1024, 1024)
         dsum[:, cols] = dsum[:, cols] + dp_recv[c].astype(f32)
     for j in range(16):
         d_send[j] = dsum[4 * j : 4 * j + 4, :].astype(bf16)
-    d_copies = {}
     for k in ORDER[::-1]:
-        copy = pltpu.make_async_remote_copy(
-            src_ref=d_send.at[peer_of(x, y, k)], dst_ref=d_recv.at[k], send_sem=d_ss.at[k],
-            recv_sem=d_rs.at[k], device_id=dev(k), device_id_type=MESH,
-        )
-        copy.start()
-        d_copies[k] = copy
+        remote(d_send.at[peer_of(x, y, k)], d_recv.at[k], d_ss.at[0], d_rs.at[0], dev(k))
+    for c in range(nc):
+        settle(xs[c], x_ss.at[c])
+        settle(zs[c], z_ss.at[c])
+    settle(qs_send.at[pl.ds(0, 15)], q_ss.at[0])
+    settle(qfull.at[pl.ds(0, 120)], a_ss.at[0])
+    settle(stats.at[pl.ds(0, 15)], s_ss.at[0])
+    settle(msend.at[pl.ds(0, 15)], m_ss.at[0])
+    settle(pair_send, pair_ss.at[0])
+    settle(rs_send.at[pl.ds(1, 15)], rs_ss.at[0])
+    settle(rs_send.at[pl.ds(1, 15)], ag_ss.at[0])
+    settle(rs_send, fw_ss.at[0])
+    settle(dp_send, dp_ss.at[0])
+    settle(fsk, out_sem.at[0])
+    settle(fsv, out_sem.at[1])
     for k in range(16):
         for t in range(2):
             cols = pl.ds(pl.multiple_of((source_of(x, y, k) * 2 + t) * 128, 128), 128)
             resrow[:, cols] = jnp.dot(pick, ag[k, t], preferred_element_type=f32)
-    pick64 = lax.broadcasted_iota(jnp.int32, (8, 64), 0) + kv * 4
     total = resrow[...][:4]
-    lane = lax.broadcasted_iota(jnp.int32, (4, 4096), 0)
     own = jnp.zeros((4, 4096), f32)
     for j in range(16):
         own = jnp.where(kv == j, dsum[4 * j : 4 * j + 4, :], own)
     total = total + own
+    settle(d_recv.at[pl.ds(1, 15)], d_rs.at[0])
     for k in ORDER:
-        d_copies[k].wait_recv()
         total = total + d_recv[k].astype(f32)
     out_ref[...] = total.astype(bf16)
-
-    for k in range(1, 16):
-        rs_copies[k].wait_send()
-        ag_copies[k].wait_send()
-        d_copies[k].wait_send()
-    for k in range(16):
-        fw_copies[k].wait_send()
-    for c in range(4):
-        dp_copies[c].wait_send()
-    for copies in (q_copies, a_copies, x_copies, z_copies, s_copies, m_copies):
-        for copy in copies.values():
-            copy.wait_send()
-    for copy in out_copies:
-        copy.wait()
+    settle(d_send.at[pl.ds(0, 15)], d_ss.at[0])
 
 
 def step(meta, hidden, again, gain, token_kv, w_query, pool, resident, w_out, w_gate, w_up, w_down):
@@ -540,12 +486,12 @@
             pltpu.VMEM((16, 4, 4096), bf16),
             pltpu.VMEM((8, 4096), f32),
             *chunk(16), *chunk(15), *chunk(16), *chunk(3, 4), *chunk(4, 4),
-            dma((2,)), dma((nc,)), dma((1,)), dma((nc,)),
-            dma((16,)), dma((16,)), dma((16,)), dma((16,)),
-            dma((nc, 16)), dma((nc, 16)), dma((nc, 4)), dma((nc, 4)),
-            dma((16,)), dma((16,)), dma((16,)), dma((16,)),
-            dma((4,)), dma((4,)), dma((4,)), dma((16,)), dma((16,)), dma((16,)), dma((16,)),
-            dma((16,)), dma((16,)), dma((4,)), dma((4,)), dma((16,)), dma((16,)),
+            dma((2,)), dma((nc,)), dma((1,)), dma((2,)),
+            dma((1,)), dma((1,)), dma((1,)), dma((1,)),
+            dma((nc,)), dma((nc,)), dma((nc,)), dma((nc,)),
+            dma((1,)), dma((1,)), dma((1,)), dma((1,)),
+            dma((4,)), dma((1,)), dma((4,)), dma((1,)), dma((1,)), dma((1,)), dma((16,)),
+            dma((1,)), dma((16,)), dma((1,)), dma((4,)), dma((1,)), dma((1,)),
         ],
         compiler_params=pltpu.CompilerParams(
             collective_id=0, has_side_effects=True, vmem_limit_bytes=62 * 1024 * 1024

time: 159 us -> 142 us (0.89)
  Pallas kernels: 148 us -> 131 us
    pallas_call x1, Pallas kernels: 148 us -> 131 us  [step(): pl.pallas_call(step_kernel, name='step', out_shape=(jax.ShapeDtypeStruct(...]
where the time goes in v5:
time: 142 us; the launch traced here: 141 us
  Pallas kernels  131 us (92%)
  local copies, waits for them, and re-layouts  7.5 us (5%)
  other arithmetic  2.75 us (2%)
    pallas_call x1, Pallas kernels, step(): pl.pallas_call(step_kernel, name='step', out_shape=(jax.ShapeDtypeStruct(...  131 us
    unnamed x2, local copies, waits for them, and re-layouts  6.02 us

profile of v5, /device:TPU:1, one launch (start us, length us, event | category | flops | bytes accessed | tf_op | source)
XLA Modules:
  0.0 141.4 jit_solution(5843186776984353080)
XLA Ops:
  0.6 0.7 select_reduce_fusion.1
  1.4 0.8 add_select_fusion
  2.1 0.8 broadcast_compare_fusion
  2.9 0.2 convert_reduce_fusion
  3.1 0.2 select_reduce_fusion
  3.3 0.1 reshape.40
  3.4 0.1 reshape.39
  3.5 0.1 reduce_sum.37
  3.6 1.3 concatenate.3.meta
  4.9 130.5 %step.1 = (bf16[4,4096]{1,0:T(4,128)(2,1)}, bf16[16,2,128,512]{3,2,1,0:T(8,128)(2,1)}) custom-call(s32[96]{0:T(128)} %concatenate.3.meta, bf16[128,256]{1,0:T(8,128)(2,1)} %hid_ref.1, f32[1,256]{1,0:T(1,128)} %bitcast.21, f32[1,4096]{1,0:T(1,128)} %bitcast.20, bf16[128,2,512]{2,1,0:T(2,128)(2,1)} %tok_hbm.1, bf16[256,2048]{1,0:T(8,128)(2,1)} %wq_hbm.1, ...), custom_call_target="tpu_custom_call" | custom-call | tf_op jit(solution)/shard_map/step/pallas_call | solution.py:445
  135.4 1.4 copy.21
  136.8 4.6 %copy.22 = bf16[1,16,2,128,512]{4,3,2,1,0:T(8,128)(2,1)} copy(bf16[1,16,2,128,512]{4,3,2,1,0:T(8,128)(2,1)} %bitcast.15) | data formatting | bytes 8388608
  (3 shorter events, 0.0 us)

commit v6 on v5

--- a/solution.py
+++ b/solution.py
@@ -30,19 +30,18 @@
 ORDER = sorted(range(1, 16), key=lambda k: (min(k // 4, 4 - k // 4) + min(k % 4, 4 - k % 4), k))
 
 
-CHUNKS = 8
-CROWS = 256 // CHUNKS
+PIECES = [(0, 0, 32), (0, 32, 32), (0, 64, 32), (0, 96, 32), (1, 0, 32), (1, 32, 32), (1, 64, 32), (1, 96, 16), (1, 112, 16)]
 
 
 def step_kernel(
     meta, hid_ref, again_ref, gain_ref, tok_hbm, wq_hbm, pool_hbm, res_hbm, wout_hbm, wg_hbm, wu_hbm, wd_hbm,
     out_ref, cache_hbm,
-    wq, tok, kept, qs_send, qs_recv, qfull, qflat, fsk, fsv, scores, probs, pvacc, accs, stats, msend, mrecv,
+    wq, tok, kept, qa1s, qa1r, qa2s, qa2r, qb1s, qb1r, qb2s, qb2r, qfa, qfb, qflat, fsk, fsv, scores, probs, pvacc, accs, stats, msend, mrecv,
     wout, wg, wu, wd, pair_send, pair_recv, own_part, rs_send, rs_recv, ag, hunits,
     dp_send, dp_recv, dsum, d_send, d_recv, resrow, *rest,
 ):
     f32, bf16, i32 = jnp.float32, jnp.bfloat16, jnp.int32
-    nc = CHUNKS
+    nc = len(PIECES)
     pool, xs, xr, zs, zr = (rest[i * nc : (i + 1) * nc] for i in range(5))
     (ld_sem, pool_sem, kept_sem, out_sem, q_ss, q_rs, a_ss, a_rs, x_ss, x_rs, z_ss, z_rs, s_ss, s_rs,
      m_ss, m_rs, w_sem, pair_ss, pair_rs, rs_ss, rs_rs, ag_ss, ag_rs, fw_ss, fw_rs, dp_ss, dp_rs, d_ss,
@@ -73,7 +72,7 @@
     wq_load.start()
     pool_loads = []
     for c in range(nc):
-        load = pltpu.make_async_copy(pool_hbm.at[:, pl.ds(c * CROWS, CROWS), :], pool[c], pool_sem.at[c])
+        load = pltpu.make_async_copy(pool_hbm.at[:, pl.ds(PIECES[c][0] * 128 + PIECES[c][1], PIECES[c][2]), :], pool[c], pool_sem.at[c])
         load.start()
         pool_loads.append(load)
     kept_load = pltpu.make_async_copy(res_hbm, kept, kept_sem.at[0])
@@ -101,14 +100,19 @@
     normed = (feats * again_ref[...]).astype(bf16)
     squares = jnp.sum(feats * feats, axis=1, keepdims=True)
     wq_load.wait()
-    for h in range(4):
+    for h in range(2):
         part = jnp.dot(normed, wq[:, h * 512 : h * 512 + 512], preferred_element_type=f32)
-        qs_send[:, :, h * 512 : h * 512 + 512] = part.reshape(16, 8, 512)
-    qs_send[:, :, 2048:2176] = jnp.broadcast_to(squares, (128, 128)).reshape(16, 8, 128)
+        qa1s[:, :, h * 512 : h * 512 + 512] = part.reshape(4, 32, 512)
+    qa1s[:, :, 1024:1152] = jnp.broadcast_to(squares, (128, 128)).reshape(4, 32, 128)
+    for h in range(2):
+        part = jnp.dot(normed, wq[:, 1024 + h * 512 : 1536 + h * 512], preferred_element_type=f32)
+        for i in range(16):
+            qb1s[i % 4, i // 4, :, h * 512 : h * 512 + 512] = part[8 * i : 8 * i + 8]
     pl.semaphore_wait(barrier, 19)
 
-    for k in ORDER[::-1]:
-        remote(qs_send.at[peer_of(x, y, k)], qs_recv.at[k], q_ss.at[0], q_rs.at[0], dev(k))
+    for step in (2, 1, 3):
+        remote(qa1s.at[lax.rem(x + step, 4)], qa1r.at[step], q_ss.at[0], q_rs.at[0], dev(4 * step))
+        remote(qb1s.at[lax.rem(y + step, 4)], qb1r.at[step], q_ss.at[1], q_rs.at[1], dev(step))
 
     def xy_start(c):
         pool_loads[c].wait()
@@ -133,13 +137,13 @@
 
     def finish(c):
         settle(zs[c], z_rs.at[c])
-        final, half = (fsk, 0) if c < nc // 2 else (fsv, 1)
-        row = (c % (nc // 2)) * CROWS
+        half, row, tokens = PIECES[c]
+        final = (fsk, fsv)[half]
         for i in range(16):
             where = meta[32 + i]
-            final[i, row : row + CROWS, :] = zr[c][where // 4, lax.rem(where, 4)]
+            final[i, row : row + tokens, :] = zr[c][where // 4, lax.rem(where, 4)]
         pltpu.make_async_copy(
-            final.at[:, pl.ds(row, CROWS), :], cache_hbm.at[:, half, pl.ds(row, CROWS), :], out_sem.at[half]
+            final.at[:, pl.ds(row, tokens), :], cache_hbm.at[:, half, pl.ds(row, tokens), :], out_sem.at[half]
         ).start()
 
     head_of = lax.broadcasted_iota(i32, (16, 512), 0) // 4
@@ -148,7 +152,8 @@
     lanes = lax.broadcasted_iota(i32, (16, 128), 1)
 
     def page_scores(p, keys, slot, filled):
-        q = qfull[slot]
+        place_x, place_y, place_s = slot // 32, lax.rem(slot // 8, 4), lax.rem(slot, 8)
+        q = jnp.concatenate([qfa[place_x, place_y, place_s], qfb[place_x, place_y, place_s]], axis=0)
         wide = jnp.where(diag, jnp.concatenate([q, q, q, q], axis=1), 0.0)
         high = wide.astype(bf16)
         left = wide - high.astype(f32)
@@ -179,35 +184,54 @@
     def note(table, p, top, total):
         return jnp.where(lane32 == p, jnp.concatenate([top, total], axis=0), table)
 
+    def query_second():
+        settle(qa1r.at[pl.ds(1, 3)], q_rs.at[0])
+        qa2s[...] = (qa1s[x] + qa1r[1] + qa1r[2] + qa1r[3]).reshape(4, 8, 1152)
+        settle(qb1r.at[pl.ds(1, 3)], q_rs.at[1])
+        qb2s[...] = qb1s[y] + qb1r[1] + qb1r[2] + qb1r[3]
+        for step in (2, 1, 3):
+            remote(qa2s.at[lax.rem(y + step, 4)], qa2r.at[step], q_ss.at[2], q_rs.at[2], dev(step))
+            remote(qb2s.at[lax.rem(x + step, 4)], qb2r.at[step], q_ss.at[3], q_rs.at[3], dev(4 * step))
+
     def query_done():
-        total = qs_send[kv]
-        settle(qs_recv.at[pl.ds(1, 15)], q_rs.at[0])
-        for k in range(1, 16):
-            total = total + qs_recv[k]
-        scale = lax.rsqrt(total[:, 2048:2049] / D + norm_eps)
-        q8 = total[:, :2048] * scale * HEAD_DIM ** (-0.5)
+        settle(qa2r.at[pl.ds(1, 3)], q_rs.at[2])
+        first = qa2s[y] + qa2r[1] + qa2r[2] + qa2r[3]
+        settle(qb2r.at[pl.ds(1, 3)], q_rs.at[3])
+        second = qb2s[x] + qb2r[1] + qb2r[2] + qb2r[3]
+        scale = lax.rsqrt(first[:, 1024:1025] / D + norm_eps)
+        q8 = jnp.concatenate([first[:, :1024], second], axis=1) * scale * HEAD_DIM ** (-0.5)
         qflat[...] = q8
-        for h in range(16):
-            qfull[pl.ds(pl.multiple_of(kv * 8, 8), 8), h, :] = q8[:, h * 128 : h * 128 + 128]
-        mine = qfull.at[pl.ds(pl.multiple_of(kv * 8, 8), 8)]
-        for k in ORDER[::-1]:
-            remote(mine, mine, a_ss.at[0], a_rs.at[0], dev(k))
-
-    for c in range(3):
-        xy_start(c)
+        for h in range(8):
+            qfa[x, y, :, h, :] = q8[:, h * 128 : h * 128 + 128]
+            qfb[x, y, :, h, :] = q8[:, 1024 + h * 128 : 1152 + h * 128]
+        for step in (2, 1, 3):
+            remote(qfa.at[x, y], qfa.at[x, y], a_ss.at[0], a_rs.at[0], dev(4 * step))
+            remote(qfb.at[x, y], qfb.at[x, y], a_ss.at[1], a_rs.at[1], dev(step))
+
+    def query_spread():
+        settle(qfa.at[pl.ds(0, 3), 0], a_rs.at[0])
+        settle(qfb.at[pl.ds(0, 3), 0], a_rs.at[1])
+        for step in (2, 1, 3):
+            remote(qfa.at[:, y], qfa.at[:, y], a_ss.at[2], a_rs.at[2], dev(step))
+            remote(qfb.at[x], qfb.at[x], a_ss.at[3], a_rs.at[3], dev(4 * step))
+
+    xy_start(0)
+    query_second()
+    xy_start(1)
+    xy_start(2)
+    z_start(0)
     query_done()
     xy_start(3)
-    z_start(0)
-    xy_start(4)
     z_start(1)
     finish(0)
-    xy_start(5)
+    query_spread()
+    xy_start(4)
     z_start(2)
     finish(1)
-    xy_start(6)
+    xy_start(5)
     z_start(3)
     finish(2)
-    xy_start(7)
+    xy_start(6)
     tok_load.wait()
     own_key, own_value = tok[:, 0, :].astype(f32), tok[:, 1, :].astype(f32)
     lane8 = lax.broadcasted_iota(i32, (8, 128), 1)
@@ -223,13 +247,16 @@
     for p in range(24):
         slot_row = jnp.where(lane8 == p, meta[48 + p] if p < 8 else meta[56 + p], slot_row)
     slot_row = jnp.where(lane8 >= 24, kv * 8 + lane8 - 24, slot_row)
-    settle(qfull.at[pl.ds(0, 120)], a_rs.at[0])
+    settle(qfa.at[:, pl.ds(0, 3)], a_rs.at[2])
+    settle(qfb.at[pl.ds(0, 3)], a_rs.at[3])
     kept_load.wait()
     table = jnp.zeros((32, 128), f32)
     for p in range(8):
         table = note(table, p, *page_scores(p, kept[p, 0], meta[48 + p], meta[56 + p]))
     z_start(4)
     finish(3)
+    xy_start(7)
+    xy_start(8)
     for p in range(16):
         table = note(table, 8 + p, *page_scores(8 + p, fsk[p], meta[64 + p], meta[80 + p]))
     own_lane = lanes >= 24
@@ -253,6 +280,7 @@
     z_start(6)
     finish(5)
     z_start(7)
+    z_start(8)
     settle(stats.at[pl.ds(0, 15)], s_rs.at[0])
     every = jnp.concatenate(
         [stats[4 * i] + stats[4 * i + 1] + stats[4 * i + 2] + stats[4 * i + 3] for i in range(4)], axis=1
@@ -279,9 +307,9 @@
         place(p, weighted(p, kept[p, 1], 0, 128))
 
     def gather_values(c):
-        row = (c % (nc // 2)) * CROWS
+        _, row, tokens = PIECES[c]
         for p in range(16):
-            part = weighted(8 + p, fsv[p, row : row + CROWS, :], row, row + CROWS)
+            part = weighted(8 + p, fsv[p, row : row + tokens, :], row, row + tokens)
             if row == 0:
                 pvacc[p] = part
             else:
@@ -292,9 +320,11 @@
     finish(6)
     gather_values(6)
     finish(7)
+    gather_values(7)
+    finish(8)
+    _, row, tokens = PIECES[8]
     for p in range(16):
-        row = 3 * CROWS
-        place(8 + p, pvacc[p] + weighted(8 + p, fsv[p, row : row + CROWS, :], row, row + CROWS))
+        place(8 + p, pvacc[p] + weighted(8 + p, fsv[p, row : row + tokens, :], row, row + tokens))
 
     tiles = [accs[h] for h in range(16)]
     group = lane32 // 8
@@ -405,8 +435,14 @@
     for c in range(nc):
         settle(xs[c], x_ss.at[c])
         settle(zs[c], z_ss.at[c])
-    settle(qs_send.at[pl.ds(0, 15)], q_ss.at[0])
-    settle(qfull.at[pl.ds(0, 120)], a_ss.at[0])
+    settle(qa1s.at[pl.ds(0, 3)], q_ss.at[0])
+    settle(qb1s.at[pl.ds(0, 3)], q_ss.at[1])
+    settle(qa2s.at[pl.ds(0, 3)], q_ss.at[2])
+    settle(qb2s.at[pl.ds(0, 3)], q_ss.at[3])
+    settle(qfa.at[pl.ds(0, 3), 0], a_ss.at[0])
+    settle(qfb.at[pl.ds(0, 3), 0], a_ss.at[1])
+    settle(qfa.at[:, pl.ds(0, 3)], a_ss.at[2])
+    settle(qfb.at[pl.ds(0, 3)], a_ss.at[3])
     settle(stats.at[pl.ds(0, 15)], s_ss.at[0])
     settle(msend.at[pl.ds(0, 15)], m_ss.at[0])
     settle(pair_send, pair_ss.at[0])
@@ -437,10 +473,10 @@
     vmem = pl.BlockSpec(memory_space=pltpu.VMEM)
     hbm = pl.BlockSpec(memory_space=pl.ANY)
     dma = pltpu.SemaphoreType.DMA
-    nc = CHUNKS
+    nc = len(PIECES)
 
     def chunk(*lead):
-        return [pltpu.VMEM((*lead, CROWS, 512), bf16)] * nc
+        return [pltpu.VMEM((*lead, tokens, 512), bf16) for _, _, tokens in PIECES]
 
     return pl.pallas_call(
         step_kernel,
@@ -455,9 +491,16 @@
             pltpu.VMEM((256, 2048), bf16),
             pltpu.VMEM((8, 2, 512), bf16),
             pltpu.VMEM((8, 2, 128, 512), bf16),
-            pltpu.VMEM((16, 8, 2176), f32),
-            pltpu.VMEM((16, 8, 2176), f32),
-            pltpu.VMEM((128, 16, 128), f32),
+            pltpu.VMEM((4, 32, 1152), f32),
+            pltpu.VMEM((4, 32, 1152), f32),
+            pltpu.VMEM((4, 8, 1152), f32),
+            pltpu.VMEM((4, 8, 1152), f32),
+            pltpu.VMEM((4, 4, 8, 1024), f32),
+            pltpu.VMEM((4, 4, 8, 1024), f32),
+            pltpu.VMEM((4, 8, 1024), f32),
+            pltpu.VMEM((4, 8, 1024), f32),
+            pltpu.VMEM((4, 4, 8, 8, 128), f32),
+            pltpu.VMEM((4, 4, 8, 8, 128), f32),
             pltpu.VMEM((8, 2048), f32),
             pltpu.VMEM((16, 128, 512), bf16),
             pltpu.VMEM((16, 128, 512), bf16),
@@ -487,7 +530,7 @@
             pltpu.VMEM((8, 4096), f32),
             *chunk(16), *chunk(15), *chunk(16), *chunk(3, 4), *chunk(4, 4),
             dma((2,)), dma((nc,)), dma((1,)), dma((2,)),
-            dma((1,)), dma((1,)), dma((1,)), dma((1,)),
+            dma((4,)), dma((4,)), dma((4,)), dma((4,)),
             dma((nc,)), dma((nc,)), dma((nc,)), dma((nc,)),
             dma((1,)), dma((1,)), dma((1,)), dma((1,)),
             dma((4,)), dma((1,)), dma((4,)), dma((1,)), dma((1,)), dma((1,)), dma((16,)),

time: 142 us -> 132 us (0.930)
  Pallas kernels: 131 us -> 121 us
    pallas_call x1, Pallas kernels: 131 us -> 121 us  [step(): pl.pallas_call(step_kernel, name='step', out_shape=(jax.ShapeDtypeStruct(...]
where the time goes in v6:
time: 132 us
  Pallas kernels  121 us (92%)
  local copies, waits for them, and re-layouts  7.5 us (6%)
  other arithmetic  2.75 us (2%)
    pallas_call x1, Pallas kernels, step(): pl.pallas_call(step_kernel, name='step', out_shape=(jax.ShapeDtypeStruct(...  121 us
    unnamed x2, local copies, waits for them, and re-layouts  6.02 us

profile of v6, /device:TPU:1, one launch (start us, length us, event | category | flops | bytes accessed | tf_op | source)
XLA Modules:
  0.0 131.9 jit_solution(3436115164661903224)
XLA Ops:
  0.6 0.7 select_reduce_fusion.1
  1.4 0.8 add_select_fusion
  2.1 0.8 broadcast_compare_fusion
  2.9 0.2 convert_reduce_fusion
  3.1 0.2 select_reduce_fusion
  3.3 0.1 reshape.40
  3.4 0.1 reshape.39
  3.5 0.1 reduce_sum.37
  3.6 1.3 concatenate.3.meta
  4.9 121.0 %step.1 = (bf16[4,4096]{1,0:T(4,128)(2,1)}, bf16[16,2,128,512]{3,2,1,0:T(8,128)(2,1)}) custom-call(s32[96]{0:T(128)} %concatenate.3.meta, bf16[128,256]{1,0:T(8,128)(2,1)} %hid_ref.1, f32[1,256]{1,0:T(1,128)} %bitcast.21, f32[1,4096]{1,0:T(1,128)} %bitcast.20, bf16[128,2,512]{2,1,0:T(2,128)(2,1)} %tok_hbm.1, bf16[256,2048]{1,0:T(8,128)(2,1)} %wq_hbm.1, ...), custom_call_target="tpu_custom_call" | custom-call | tf_op jit(solution)/shard_map/step/pallas_call | solution.py:481
  125.9 1.4 %copy.21 = bf16[4,4096]{1,0:T(4,128)(2,1)} copy(bf16[4,4096]{1,0:T(4,128)(2,1)} %get-tuple-element.10) | data formatting | bytes 65536
  127.3 4.6 %copy.22 = bf16[1,16,2,128,512]{4,3,2,1,0:T(8,128)(2,1)} copy(bf16[1,16,2,128,512]{4,3,2,1,0:T(8,128)(2,1)} %bitcast.15) | data formatting | bytes 8388608
  (3 shorter events, 0.0 us)

commit v7 on v6

--- a/solution.py
+++ b/solution.py
@@ -34,11 +34,11 @@
 
 
 def step_kernel(
-    meta, hid_ref, again_ref, gain_ref, tok_hbm, wq_hbm, pool_hbm, res_hbm, wout_hbm, wg_hbm, wu_hbm, wd_hbm,
+    res_slot, res_len, arr_slot, arr_len, own_ref, loc_ref, hid_ref, again_ref, gain_ref, tok_hbm, wq_hbm, pool_hbm, res_hbm, wout_hbm, wg_hbm, wu_hbm, wd_hbm,
     out_ref, cache_hbm,
     wq, tok, kept, qa1s, qa1r, qa2s, qa2r, qb1s, qb1r, qb2s, qb2r, qfa, qfb, qflat, fsk, fsv, scores, probs, pvacc, accs, stats, msend, mrecv,
     wout, wg, wu, wd, pair_send, pair_recv, own_part, rs_send, rs_recv, ag, hunits,
-    dp_send, dp_recv, dsum, d_send, d_recv, resrow, *rest,
+    dp_send, dp_recv, dsum, d_send, d_recv, resrow, picks, *rest,
 ):
     f32, bf16, i32 = jnp.float32, jnp.bfloat16, jnp.int32
     nc = len(PIECES)
@@ -114,11 +114,38 @@
         remote(qa1s.at[lax.rem(x + step, 4)], qa1r.at[step], q_ss.at[0], q_rs.at[0], dev(4 * step))
         remote(qb1s.at[lax.rem(y + step, 4)], qb1r.at[step], q_ss.at[1], q_rs.at[1], dev(step))
 
+    owners = own_ref[...]
+    spot = lax.broadcasted_iota(i32, (4, 256), 1)
+    group_row = lax.broadcasted_iota(i32, (4, 256), 0)
+    mine = jnp.where(owners == grp * 16 + kv, loc_ref[...], 0)
+    pick = [jnp.sum(jnp.where(spot // 16 == j, mine, 0)) for j in range(16)]
+    from_grp = owners // 16
+    rank = jnp.zeros((4, 256), i32)
+    for back in range(1, 16):
+        earlier = pltpu.roll(from_grp, back, 1) == from_grp
+        rank = rank + jnp.where(earlier & (lax.rem(spot, 16) >= back), 1, 0)
+    here = spot // 16 == kv
+    leaving = here & (from_grp == grp)
+    sender = lax.rem(owners, 16)
+    onward = [
+        [jnp.sum(jnp.where(leaving & (group_row == g) & (rank == r), sender, 0)) for r in range(4)]
+        for g in range(4)
+    ]
+    landed = jnp.where(here & (group_row == grp), from_grp * 4 + rank, 0)
+    landing = [jnp.sum(jnp.where(lax.rem(spot, 16) == i, landed, 0)) for i in range(16)]
+    del mine
+    for j in range(16):
+        picks[j] = pick[j]
+        picks[32 + j] = landing[j]
+    for g in range(4):
+        for r in range(4):
+            picks[16 + 4 * g + r] = onward[g][r]
+
     def xy_start(c):
         pool_loads[c].wait()
-        xr[c][kv] = pool[c][meta[kv]]
+        xr[c][kv] = pool[c][picks[kv]]
         for k in range(1, 16):
-            xs[c][k - 1] = pool[c][meta[peer_of(x, y, k)]]
+            xs[c][k - 1] = pool[c][picks[peer_of(x, y, k)]]
         for k in ORDER[::-1]:
             remote(xs[c].at[k - 1], xr[c].at[kv], x_ss.at[c], x_rs.at[c], dev(k))
 
@@ -127,7 +154,7 @@
         for dz in range(4):
             g = lax.rem(grp + dz, 4)
             for r in range(4):
-                page = xr[c][meta[16 + g * 4 + r]]
+                page = xr[c][picks[16 + g * 4 + r]]
                 if dz == 0:
                     zr[c][grp, r] = page
                 else:
@@ -140,7 +167,7 @@
         half, row, tokens = PIECES[c]
         final = (fsk, fsv)[half]
         for i in range(16):
-            where = meta[32 + i]
+            where = picks[32 + i]
             final[i, row : row + tokens, :] = zr[c][where // 4, lax.rem(where, 4)]
         pltpu.make_async_copy(
             final.at[:, pl.ds(row, tokens), :], cache_hbm.at[:, half, pl.ds(row, tokens), :], out_sem.at[half]
@@ -245,20 +272,20 @@
     own_tops = jnp.concatenate([jnp.zeros((24, 128), f32), own_rows, jnp.zeros((96, 128), f32)], axis=0).T[:16]
     slot_row = jnp.zeros((8, 128), i32)
     for p in range(24):
-        slot_row = jnp.where(lane8 == p, meta[48 + p] if p < 8 else meta[56 + p], slot_row)
+        slot_row = jnp.where(lane8 == p, res_slot[0, p] if p < 8 else arr_slot[0, p - 8], slot_row)
     slot_row = jnp.where(lane8 >= 24, kv * 8 + lane8 - 24, slot_row)
     settle(qfa.at[:, pl.ds(0, 3)], a_rs.at[2])
     settle(qfb.at[pl.ds(0, 3)], a_rs.at[3])
     kept_load.wait()
     table = jnp.zeros((32, 128), f32)
     for p in range(8):
-        table = note(table, p, *page_scores(p, kept[p, 0], meta[48 + p], meta[56 + p]))
+        table = note(table, p, *page_scores(p, kept[p, 0], res_slot[0, p], res_len[0, p]))
     z_start(4)
     finish(3)
     xy_start(7)
     xy_start(8)
     for p in range(16):
-        table = note(table, 8 + p, *page_scores(8 + p, fsk[p], meta[64 + p], meta[80 + p]))
+        table = note(table, 8 + p, *page_scores(8 + p, fsk[p], arr_slot[0, p], arr_len[0, p]))
     own_lane = lanes >= 24
     mine = jnp.concatenate(
         [
@@ -288,7 +315,7 @@
     tops, sums, every_slot = every[:16], every[16:32], every[32:33].astype(i32)
     own_w = jnp.zeros((16, 128), f32)
     for p in range(32):
-        slot = meta[48 + p] if p < 8 else (meta[56 + p] if p < 24 else kv * 8 + p - 24)
+        slot = res_slot[0, p] if p < 8 else (arr_slot[0, p - 8] if p < 24 else kv * 8 + p - 24)
         same = jnp.broadcast_to(every_slot == slot, (16, 512))
         top = jnp.max(jnp.where(same, tops, neg_fill), axis=1, keepdims=True)
         total = jnp.sum(jnp.where(same, jnp.exp(tops - top) * sums, 0.0), axis=1, keepdims=True)
@@ -468,8 +495,9 @@
     settle(d_send.at[pl.ds(0, 15)], d_ss.at[0])
 
 
-def step(meta, hidden, again, gain, token_kv, w_query, pool, resident, w_out, w_gate, w_up, w_down):
+def step(*operands):
     bf16, f32 = jnp.bfloat16, jnp.float32
+    smem = pl.BlockSpec(memory_space=pltpu.SMEM)
     vmem = pl.BlockSpec(memory_space=pltpu.VMEM)
     hbm = pl.BlockSpec(memory_space=pl.ANY)
     dma = pltpu.SemaphoreType.DMA
@@ -485,7 +513,7 @@
             jax.ShapeDtypeStruct((4, 4096), bf16),
             jax.ShapeDtypeStruct((16, 2, 128, 512), bf16),
         ),
-        in_specs=[pl.BlockSpec(memory_space=pltpu.SMEM), vmem, vmem, vmem] + [hbm] * 8,
+        in_specs=[smem] * 4 + [vmem] * 5 + [hbm] * 8,
         out_specs=(vmem, hbm),
         scratch_shapes=[
             pltpu.VMEM((256, 2048), bf16),
@@ -528,6 +556,7 @@
             pltpu.VMEM((16, 4, 4096), bf16),
             pltpu.VMEM((16, 4, 4096), bf16),
             pltpu.VMEM((8, 4096), f32),
+            pltpu.SMEM((48,), jnp.int32),
             *chunk(16), *chunk(15), *chunk(16), *chunk(3, 4), *chunk(4, 4),
             dma((2,)), dma((nc,)), dma((1,)), dma((2,)),
             dma((4,)), dma((4,)), dma((4,)), dma((4,)),
@@ -539,25 +568,7 @@
         compiler_params=pltpu.CompilerParams(
             collective_id=0, has_side_effects=True, vmem_limit_bytes=62 * 1024 * 1024
         ),
-    )(meta, hidden, again, gain, token_kv, w_query, pool, resident, w_out, w_gate, w_up, w_down)
-
-
-def routing(new_owner, new_local, resident_slot, resident_len, new_slot, new_len):
-    i32 = jnp.int32
-    grp, kv = lax.axis_index("grp"), lax.axis_index("kv")
-    mine = jnp.where(new_owner == grp * 16 + kv, new_local, 0)
-    pick = jnp.sum(jnp.sum(mine, axis=0).reshape(16, 16), axis=1)
-    column = lax.dynamic_slice(new_owner, (0, kv * 16), (4, 16))
-    from_grp = column // 16
-    earlier = jnp.arange(16)[None, :] < jnp.arange(16)[:, None]
-    same = (from_grp[:, :, None] == from_grp[:, None, :]) & earlier[None]
-    rank = jnp.sum(same.astype(i32), axis=2)
-    hit = (from_grp == grp)[:, None, :] & (rank[:, None, :] == jnp.arange(4)[None, :, None])
-    onward = jnp.sum(jnp.where(hit, (column % 16)[:, None, :], 0), axis=2).reshape(16)
-    final = lax.dynamic_index_in_dim(from_grp * 4 + rank, grp, 0, keepdims=False)
-    return jnp.concatenate(
-        [pick, onward, final, resident_slot[0], resident_len[0], new_slot[0], new_len[0]]
-    ).astype(i32)
+    )(*operands)
 
 
 def per_device(
@@ -579,9 +590,13 @@
     new_len,
     token_kv,
 ):
-    meta = routing(new_owner, new_local, resident_slot, resident_len, new_slot, new_len)
     mixed, new_pages = step(
-        meta,
+        resident_slot,
+        resident_len,
+        new_slot,
+        new_len,
+        new_owner,
+        new_local,
         hidden_states,
         attn_gain.reshape(1, 256),
         mlp_gain.reshape(1, 4096),

time: 132 us -> 128 us (0.970)
  other arithmetic: 2.75 us -> 0 us
  local copies, waits for them, and re-layouts: 7.5 us -> 6.02 us
where the time goes in v7:
time: 128 us
  Pallas kernels  121 us (95%)
  local copies, waits for them, and re-layouts  6.02 us (5%)
    pallas_call x1, Pallas kernels, step(): pl.pallas_call(step_kernel, name='step', out_shape=(jax.ShapeDtypeStruct(...  121 us
    unnamed x2, local copies, waits for them, and re-layouts  6.02 us

profile of v7, /device:TPU:1, one launch (start us, length us, event | category | flops | bytes accessed | tf_op | source)
XLA Modules:
  0.0 127.9 jit_solution(2498161408231443818)
XLA Ops:
  0.6 121.2 %step.1 = (bf16[4,4096]{1,0:T(4,128)(2,1)}, bf16[16,2,128,512]{3,2,1,0:T(8,128)(2,1)}) custom-call(s32[1,8]{1,0:T(1,128)} %res_slot.1, s32[1,8]{1,0:T(1,128)} %res_len.1, s32[1,16]{1,0:T(1,128)} %arr_slot.1, s32[1,16]{1,0:T(1,128)} %arr_len.1, s32[4,256]{1,0:T(4,128)} %own_ref.1, s32[4,256]{1,0:T(4,128)} %loc_ref.1, bf16[128,256]{1,0:T(8,128)(2,1)} %hid_ref.1, ...), custom_call_target="tpu_custom_call" | custom-call | tf_op jit(solution)/shard_map/step/pallas_call | solution.py:509
  121.9 1.4 %copy.21 = bf16[4,4096]{1,0:T(4,128)(2,1)} copy(bf16[4,4096]{1,0:T(4,128)(2,1)} %get-tuple-element.8) | data formatting | bytes 65536
  123.3 4.6 %copy.22 = bf16[1,16,2,128,512]{4,3,2,1,0:T(8,128)(2,1)} copy(bf16[1,16,2,128,512]{4,3,2,1,0:T(8,128)(2,1)} %bitcast.8) | data formatting | bytes 8388608

commit v8 on v7

--- a/solution.py
+++ b/solution.py
@@ -37,14 +37,14 @@
     res_slot, res_len, arr_slot, arr_len, own_ref, loc_ref, hid_ref, again_ref, gain_ref, tok_hbm, wq_hbm, pool_hbm, res_hbm, wout_hbm, wg_hbm, wu_hbm, wd_hbm,
     out_ref, cache_hbm,
     wq, tok, kept, qa1s, qa1r, qa2s, qa2r, qb1s, qb1r, qb2s, qb2r, qfa, qfb, qflat, fsk, fsv, scores, probs, pvacc, accs, stats, msend, mrecv,
-    wout, wg, wu, wd, pair_send, pair_recv, own_part, rs_send, rs_recv, ag, hunits,
+    wout, wpart, wg, wu, wd, rs_send, rs_recv, ag, hunits,
     dp_send, dp_recv, dsum, d_send, d_recv, resrow, picks, *rest,
 ):
     f32, bf16, i32 = jnp.float32, jnp.bfloat16, jnp.int32
     nc = len(PIECES)
     pool, xs, xr, zs, zr = (rest[i * nc : (i + 1) * nc] for i in range(5))
     (ld_sem, pool_sem, kept_sem, out_sem, q_ss, q_rs, a_ss, a_rs, x_ss, x_rs, z_ss, z_rs, s_ss, s_rs,
-     m_ss, m_rs, w_sem, pair_ss, pair_rs, rs_ss, rs_rs, ag_ss, ag_rs, fw_ss, fw_rs, dp_ss, dp_rs, d_ss,
+     m_ss, m_rs, w_sem, wp_ss, wp_rs, rs_ss, rs_rs, ag_ss, ag_rs, fw_ss, fw_rs, dp_ss, dp_rs, d_ss,
      d_rs) = rest[5 * nc :]
     grp, kv, tp = lax.axis_index("grp"), lax.axis_index("kv"), lax.axis_index("tp")
     x, y = kv // 4, lax.rem(kv, 4)
@@ -93,6 +93,9 @@
     pl.semaphore_signal(barrier, inc=1, device_id=partner, device_id_type=MESH)
     for k in range(1, 16):
         pl.semaphore_signal(barrier, inc=1, device_id=dev(k), device_id_type=MESH)
+        pl.semaphore_signal(
+            barrier, inc=1, device_id=(grp, peer_of(x, y, k), other), device_id_type=MESH
+        )
     for dz in range(1, 4):
         pl.semaphore_signal(barrier, inc=1, device_id=zdev(dz), device_id_type=MESH)
 
@@ -108,7 +111,7 @@
         part = jnp.dot(normed, wq[:, 1024 + h * 512 : 1536 + h * 512], preferred_element_type=f32)
         for i in range(16):
             qb1s[i % 4, i // 4, :, h * 512 : h * 512 + 512] = part[8 * i : 8 * i + 8]
-    pl.semaphore_wait(barrier, 19)
+    pl.semaphore_wait(barrier, 34)
 
     for step in (2, 1, 3):
         remote(qa1s.at[lax.rem(x + step, 4)], qa1r.at[step], q_ss.at[0], q_rs.at[0], dev(4 * step))
@@ -244,6 +247,10 @@
 
     xy_start(0)
     query_second()
+    loads[0].wait()
+    for j in range(16):
+        cols = pl.ds(pl.multiple_of(j * 256 + other * 128, 128), 128)
+        remote(wout.at[:, cols], wpart.at[j], wp_ss.at[0], wp_rs.at[0], partner)
     xy_start(1)
     xy_start(2)
     z_start(0)
@@ -365,46 +372,34 @@
     for j in range(16):
         msend[j] = tiles[j].astype(bf16)
     for k in ORDER[::-1]:
-        remote(msend.at[peer_of(x, y, k)], mrecv.at[kv], m_ss.at[0], m_rs.at[0], dev(k))
-    mrecv[kv] = msend[kv]
-    settle(msend.at[pl.ds(0, 15)], m_rs.at[0])
-    attn = jnp.dot(
-        member, mrecv[...].reshape(512, 128), preferred_element_type=f32
-    ).astype(bf16)
+        piece = msend.at[peer_of(x, y, k)]
+        remote(piece, mrecv.at[tp, kv], m_ss.at[0], m_rs.at[0], dev(k))
+        remote(piece, mrecv.at[tp, kv], m_ss.at[1], m_rs.at[1], (grp, peer_of(x, y, k), other))
+    remote(msend.at[kv], mrecv.at[tp, kv], m_ss.at[1], m_rs.at[1], partner)
+    mrecv[tp, kv] = msend[kv]
 
     rho = lax.broadcasted_iota(jnp.int32, (128, 128), 0)
     col = lax.broadcasted_iota(jnp.int32, (128, 128), 1)
     slot = (lax.rem(rho, 64) // 4) * 8 + (rho // 64) * 4 + lax.rem(rho, 4)
     perm = jnp.where(col == slot, 1.0, 0.0).astype(bf16)
-    hid = jnp.dot(
+    block = jnp.dot(
         perm, hid_ref[:, pl.ds(pl.multiple_of(tp * 128, 128), 128)], preferred_element_type=f32
     )
-
-    loads[0].wait()
-
-    order = ORDER[::-1] + [0]
-    for g in range(4):
-        for i in range(4):
-            k = order[4 * g + i]
-            dest = peer_of(x, y, k)
-            part = jnp.dot(
-                attn, wout[:, pl.ds(pl.multiple_of(dest * 256, 256), 256)], preferred_element_type=f32
-            )
-            low, high = part[:, :128], part[:, 128:]
-            own_part[g, i] = jnp.where(tp == 0, low, high)
-            pair_send[g, i] = jnp.where(tp == 0, high, low).astype(bf16)
-        remote(pair_send.at[g], pair_recv.at[g], pair_ss.at[0], pair_rs.at[g], partner)
-    block = None
-    for g in range(4):
-        settle(pair_recv.at[g], pair_rs.at[g])
-        for i in range(4):
-            k = order[4 * g + i]
-            total = own_part[g, i] + pair_recv[g, i].astype(f32)
-            if k == 0:
-                block = total + hid
-            else:
-                rs_send[k] = total.astype(bf16)
-                remote(rs_send.at[k], rs_recv.at[k], rs_ss.at[0], rs_rs.at[0], dev(k))
+    settle(wpart, wp_rs.at[0])
+    settle(msend.at[pl.ds(0, 15)], m_rs.at[0])
+    near = jnp.dot(member, mrecv[tp].reshape(512, 128), preferred_element_type=f32).astype(bf16)
+    settle(msend, m_rs.at[1])
+    far = jnp.dot(member, mrecv[other].reshape(512, 128), preferred_element_type=f32).astype(bf16)
+    for k in ORDER[::-1] + [0]:
+        dest = peer_of(x, y, k)
+        cols = pl.ds(pl.multiple_of(dest * 256 + tp * 128, 128), 128)
+        total = jnp.dot(near, wout[:, cols], preferred_element_type=f32)
+        total = total + jnp.dot(far, wpart[dest], preferred_element_type=f32)
+        if k == 0:
+            block = block + total
+        else:
+            rs_send[k] = total.astype(bf16)
+            remote(rs_send.at[k], rs_recv.at[k], rs_ss.at[0], rs_rs.at[0], dev(k))
     settle(rs_recv.at[pl.ds(1, 15)], rs_rs.at[0])
     for k in ORDER:
         block = block + rs_recv[k].astype(f32)
@@ -426,7 +421,7 @@
     mine = lax.broadcasted_iota(jnp.int32, (8, 128), 0) + tp * 64 + kv * 4
     pick = jnp.where(lax.broadcasted_iota(jnp.int32, (8, 128), 1) == mine, 1.0, 0.0).astype(bf16)
     for n, k in enumerate(seq):
-        for later in seq[n + 1 : n + 7] if n == 0 else seq[n + 6 : n + 7]:
+        for later in seq[n + 1 : n + 4] if n == 0 else seq[n + 3 : n + 4]:
             settle(ag.at[later, tp], ag_rs.at[later])
             forward(later)
         settle(ag.at[k, other], fw_rs.at[k])
@@ -472,7 +467,8 @@
     settle(qfb.at[pl.ds(0, 3)], a_ss.at[3])
     settle(stats.at[pl.ds(0, 15)], s_ss.at[0])
     settle(msend.at[pl.ds(0, 15)], m_ss.at[0])
-    settle(pair_send, pair_ss.at[0])
+    settle(wpart, wp_ss.at[0])
+    settle(msend, m_ss.at[1])
     settle(rs_send.at[pl.ds(1, 15)], rs_ss.at[0])
     settle(rs_send.at[pl.ds(1, 15)], ag_ss.at[0])
     settle(rs_send, fw_ss.at[0])
@@ -538,14 +534,12 @@
             pltpu.VMEM((16, 32, 128), f32),
             pltpu.VMEM((16, 40, 128), f32),
             pltpu.VMEM((16, 32, 128), bf16),
-            pltpu.VMEM((16, 32, 128), bf16),
+            pltpu.VMEM((2, 16, 32, 128), bf16),
             pltpu.VMEM((128, 4096), bf16),
+            pltpu.VMEM((16, 128, 128), bf16),
             pltpu.VMEM((448, 4096), bf16),
             pltpu.VMEM((448, 4096), bf16),
             pltpu.VMEM((448, 4096), bf16),
-            pltpu.VMEM((4, 4, 128, 128), bf16),
-            pltpu.VMEM((4, 4, 128, 128), bf16),
-            pltpu.VMEM((4, 4, 128, 128), f32),
             pltpu.VMEM((16, 128, 128), bf16),
             pltpu.VMEM((16, 128, 128), bf16),
             pltpu.VMEM((16, 2, 128, 128), bf16),
@@ -561,14 +555,45 @@
             dma((2,)), dma((nc,)), dma((1,)), dma((2,)),
             dma((4,)), dma((4,)), dma((4,)), dma((4,)),
             dma((nc,)), dma((nc,)), dma((nc,)), dma((nc,)),
-            dma((1,)), dma((1,)), dma((1,)), dma((1,)),
-            dma((4,)), dma((1,)), dma((4,)), dma((1,)), dma((1,)), dma((1,)), dma((16,)),
+            dma((1,)), dma((1,)), dma((2,)), dma((2,)),
+            dma((4,)), dma((1,)), dma((1,)), dma((1,)), dma((1,)), dma((1,)), dma((16,)),
             dma((1,)), dma((16,)), dma((1,)), dma((4,)), dma((1,)), dma((1,)),
         ],
         compiler_params=pltpu.CompilerParams(
             collective_id=0, has_side_effects=True, vmem_limit_bytes=62 * 1024 * 1024
         ),
     )(*operands)
+
+
+def deliver_kernel(mixed_ref, cache_hbm, out_ref, final_hbm, pages, in_sem, out_sem):
+    loads = [pltpu.make_async_copy(cache_hbm.at[i], pages.at[i], in_sem.at[i]) for i in range(16)]
+    stores = [pltpu.make_async_copy(pages.at[i], final_hbm.at[i], out_sem.at[i]) for i in range(16)]
+    for load in loads:
+        load.start()
+    out_ref[...] = mixed_ref[...]
+    for load, store in zip(loads, stores):
+        load.wait()
+        store.start()
+    for store in stores:
+        store.wait()
+
+
+def deliver(mixed, cache):
+    vmem = pl.BlockSpec(memory_space=pltpu.VMEM)
+    hbm = pl.BlockSpec(memory_space=pl.ANY)
+    dma = pltpu.SemaphoreType.DMA
+    return pl.pallas_call(
+        deliver_kernel,
+        name="deliver",
+        out_shape=(
+            jax.ShapeDtypeStruct(mixed.shape, mixed.dtype),
+            jax.ShapeDtypeStruct(cache.shape, cache.dtype),
+        ),
+        in_specs=[vmem, hbm],
+        out_specs=(vmem, hbm),
+        scratch_shapes=[pltpu.VMEM(cache.shape, cache.dtype), dma((16,)), dma((16,))],
+        compiler_params=pltpu.CompilerParams(vmem_limit_bytes=62 * 1024 * 1024),
+    )(mixed, cache)
 
 
 def per_device(
@@ -609,6 +634,7 @@
         w_up.T,
         w_down,
     )
+    mixed, new_pages = deliver(mixed, new_pages)
     return (mixed, new_pages[None])
 
 

time: 128 us -> 127 us (level)
  local copies, waits for them, and re-layouts: 6.02 us -> 0 us
  Pallas kernels: 121 us -> 126 us
    unnamed x2 -> x0, local copies, waits for them, and re-layouts: 6.02 us -> none
    pallas_call x0 -> x1, Pallas kernels: none -> 5.22 us  [deliver(): pl.pallas_call(deliver_kernel, name='deliver', out_shape=(jax.ShapeDtypeS...]
where the time goes in v8:
time: 127 us
  Pallas kernels  126 us (99%)
    pallas_call x1, Pallas kernels, step(): pl.pallas_call(step_kernel, name='step', out_shape=(jax.ShapeDtypeStruct(...  121 us
    pallas_call x1, Pallas kernels, deliver(): pl.pallas_call(deliver_kernel, name='deliver', out_shape=(jax.ShapeDtypeS...  5.22 us

profile of v8, /device:TPU:1, one launch (start us, length us, event | category | flops | bytes accessed | tf_op | source)
XLA Modules:
  0.0 126.8 jit_solution(1046385310069255458)
XLA Ops:
  0.6 120.9 %step.1 = (bf16[4,4096]{1,0:T(4,128)(2,1)}, bf16[16,2,128,512]{3,2,1,0:T(8,128)(2,1)}) custom-call(s32[1,8]{1,0:T(1,128)} %res_slot.1, s32[1,8]{1,0:T(1,128)} %res_len.1, s32[1,16]{1,0:T(1,128)} %arr_slot.1, s32[1,16]{1,0:T(1,128)} %arr_len.1, s32[4,256]{1,0:T(4,128)} %own_ref.1, s32[4,256]{1,0:T(4,128)} %loc_ref.1, bf16[128,256]{1,0:T(8,128)(2,1)} %hid_ref.1, ...), custom_call_target="tpu_custom_call" | custom-call | tf_op jit(solution)/shard_map/step/pallas_call | solution.py:505
  121.5 5.2 %deliver.1 = (bf16[4,4096]{1,0:T(4,128)(2,1)}, bf16[16,2,128,512]{3,2,1,0:T(8,128)(2,1)}) custom-call(bf16[4,4096]{1,0:T(4,128)(2,1)} %get-tuple-element.6.mixed_ref, bf16[16,2,128,512]{3,2,1,0:T(8,128)(2,1)} %get-tuple-element.7.cache_hbm), custom_call_target="tpu_custom_call" | custom-call | tf_op jit(solution)/shard_map/deliver/pallas_call | solution.py:585

commit v9 on v8

--- a/solution.py
+++ b/solution.py
@@ -30,14 +30,15 @@
 ORDER = sorted(range(1, 16), key=lambda k: (min(k // 4, 4 - k // 4) + min(k % 4, 4 - k % 4), k))
 
 
-PIECES = [(0, 0, 32), (0, 32, 32), (0, 64, 32), (0, 96, 32), (1, 0, 32), (1, 32, 32), (1, 64, 32), (1, 96, 16), (1, 112, 16)]
+PIECES = [(0, 0, 32), (0, 32, 32), (0, 64, 32), (0, 96, 16), (0, 112, 16)]
+PIECES += [(1, 16 * i, 16) for i in range(8)]
 
 
 def step_kernel(
     res_slot, res_len, arr_slot, arr_len, own_ref, loc_ref, hid_ref, again_ref, gain_ref, tok_hbm, wq_hbm, pool_hbm, res_hbm, wout_hbm, wg_hbm, wu_hbm, wd_hbm,
     out_ref, cache_hbm,
-    wq, tok, kept, qa1s, qa1r, qa2s, qa2r, qb1s, qb1r, qb2s, qb2r, qfa, qfb, qflat, fsk, fsv, scores, probs, pvacc, accs, stats, msend, mrecv,
-    wout, wpart, wg, wu, wd, rs_send, rs_recv, ag, hunits,
+    wq, tok, kept, qa1s, qa1r, qa2s, qa2r, qb1s, qb1r, qb2s, qb2r, qfa, qfb, qflat, fsk, fsv, scores, probs, pvacc, accs, eaccs, stats, msend, esend, mrecv,
+    w2, wg, wu, wd, rs_send, rs_recv, ag, hunits,
     dp_send, dp_recv, dsum, d_send, d_recv, resrow, picks, *rest,
 ):
     f32, bf16, i32 = jnp.float32, jnp.bfloat16, jnp.int32
@@ -84,7 +85,7 @@
 
     loads = [
         pltpu.make_async_copy(src, dst, w_sem.at[i])
-        for i, (src, dst) in enumerate([(wout_hbm, wout), (wg_hbm, wg), (wu_hbm, wu), (wd_hbm, wd)])
+        for i, (src, dst) in enumerate([(wg_hbm, wg), (wu_hbm, wu), (wd_hbm, wd)])
     ]
     for load in loads:
         load.start()
@@ -205,7 +206,7 @@
         out = jnp.dot(jnp.concatenate([high, low], axis=0), values, preferred_element_type=f32)
         return out[:16] + out[16:]
 
-    def place(p, acc):
+    def place(accs, p, acc):
         for h in range(16):
             accs[h, p : p + 1, :] = acc[h : h + 1, (h // 4) * 128 : (h // 4) * 128 + 128]
 
@@ -247,25 +248,28 @@
 
     xy_start(0)
     query_second()
-    loads[0].wait()
     for j in range(16):
-        cols = pl.ds(pl.multiple_of(j * 256 + other * 128, 128), 128)
-        remote(wout.at[:, cols], wpart.at[j], wp_ss.at[0], wp_rs.at[0], partner)
+        near_cols = pl.ds(pl.multiple_of(j * 256 + tp * 128, 128), 128)
+        far_cols = pl.ds(pl.multiple_of(j * 256 + other * 128, 128), 128)
+        here = pl.ds(j * 128, 128)
+        pltpu.make_async_copy(wout_hbm.at[:, near_cols], w2.at[pl.ds(0, 128), here], w_sem.at[3]).start()
+        remote(wout_hbm.at[:, far_cols], w2.at[pl.ds(128, 128), here], wp_ss.at[0], wp_rs.at[0], partner)
     xy_start(1)
     xy_start(2)
     z_start(0)
     query_done()
     xy_start(3)
     z_start(1)
-    finish(0)
     query_spread()
     xy_start(4)
+    xy_start(5)
     z_start(2)
+    finish(0)
+    xy_start(6)
+    xy_start(7)
+    z_start(3)
     finish(1)
-    xy_start(5)
-    z_start(3)
-    finish(2)
-    xy_start(6)
+    xy_start(8)
     tok_load.wait()
     own_key, own_value = tok[:, 0, :].astype(f32), tok[:, 1, :].astype(f32)
     lane8 = lax.broadcasted_iota(i32, (8, 128), 1)
@@ -279,20 +283,24 @@
     own_tops = jnp.concatenate([jnp.zeros((24, 128), f32), own_rows, jnp.zeros((96, 128), f32)], axis=0).T[:16]
     slot_row = jnp.zeros((8, 128), i32)
     for p in range(24):
-        slot_row = jnp.where(lane8 == p, res_slot[0, p] if p < 8 else arr_slot[0, p - 8], slot_row)
+        slot_row = jnp.where(lane8 == p, arr_slot[0, p] if p < 16 else res_slot[0, p - 16], slot_row)
     slot_row = jnp.where(lane8 >= 24, kv * 8 + lane8 - 24, slot_row)
+    z_start(4)
+    finish(2)
+    xy_start(9)
     settle(qfa.at[:, pl.ds(0, 3)], a_rs.at[2])
     settle(qfb.at[pl.ds(0, 3)], a_rs.at[3])
     kept_load.wait()
     table = jnp.zeros((32, 128), f32)
     for p in range(8):
-        table = note(table, p, *page_scores(p, kept[p, 0], res_slot[0, p], res_len[0, p]))
-    z_start(4)
+        table = note(table, 16 + p, *page_scores(16 + p, kept[p, 0], res_slot[0, p], res_len[0, p]))
+    z_start(5)
     finish(3)
-    xy_start(7)
-    xy_start(8)
+    xy_start(10)
+    z_start(6)
+    finish(4)
     for p in range(16):
-        table = note(table, 8 + p, *page_scores(8 + p, fsk[p], arr_slot[0, p], arr_len[0, p]))
+        table = note(table, p, *page_scores(p, fsk[p], arr_slot[0, p], arr_len[0, p]))
     own_lane = lanes >= 24
     mine = jnp.concatenate(
         [
@@ -309,12 +317,11 @@
     stats[kv] = mine
     for k in ORDER[::-1]:
         remote(stats.at[kv], stats.at[kv], s_ss.at[0], s_rs.at[0], dev(k))
-    z_start(5)
-    finish(4)
-    z_start(6)
-    finish(5)
-    z_start(7)
-    z_start(8)
+    xy_start(11)
+    xy_start(12)
+    for c in range(7, nc):
+        z_start(c)
+        finish(c - 2)
     settle(stats.at[pl.ds(0, 15)], s_rs.at[0])
     every = jnp.concatenate(
         [stats[4 * i] + stats[4 * i + 1] + stats[4 * i + 2] + stats[4 * i + 3] for i in range(4)], axis=1
@@ -322,7 +329,7 @@
     tops, sums, every_slot = every[:16], every[16:32], every[32:33].astype(i32)
     own_w = jnp.zeros((16, 128), f32)
     for p in range(32):
-        slot = res_slot[0, p] if p < 8 else (arr_slot[0, p - 8] if p < 24 else kv * 8 + p - 24)
+        slot = arr_slot[0, p] if p < 16 else (res_slot[0, p - 16] if p < 24 else kv * 8 + p - 24)
         same = jnp.broadcast_to(every_slot == slot, (16, 512))
         top = jnp.max(jnp.where(same, tops, neg_fill), axis=1, keepdims=True)
         total = jnp.sum(jnp.where(same, jnp.exp(tops - top) * sums, 0.0), axis=1, keepdims=True)
@@ -333,50 +340,45 @@
     own_weight = jnp.concatenate([own_w, jnp.zeros((112, 128), f32)], axis=0).T[24:32]
     for h in range(16):
         g = (h // 4) * 128
-        accs[h, 24:32, :] = own_weight[:, h : h + 1] * own_value[:, g : g + 128]
+        eaccs[h, 8:16, :] = own_weight[:, h : h + 1] * own_value[:, g : g + 128]
     rho = lax.broadcasted_iota(i32, (128, 512), 0)
     member = (lax.rem(rho, 64) // 4) * 8 + (rho // 64) * 4 + lax.rem(rho, 4) == every_slot
     member = jnp.where(member, 1.0, 0.0).astype(bf16)
+
+    def swap(accs, msend):
+        tiles = [accs[h] for h in range(16)]
+        group = lanes // 8
+        for bit in (1, 2, 4, 8):
+            upper = (group & bit) != 0
+            for h in range(16):
+                if h & bit == 0:
+                    a, b = tiles[h], tiles[h + bit]
+                    tiles[h] = jnp.where(upper, pltpu.roll(b, 8 * bit, 1), a)
+                    tiles[h + bit] = jnp.where(upper, b, pltpu.roll(a, 128 - 8 * bit, 1))
+        for j in range(16):
+            msend[j] = tiles[j].astype(bf16)
+
+    def spread(msend, row, n):
+        rows = pl.ds(row, 16)
+        for k in ORDER[::-1]:
+            piece = msend.at[peer_of(x, y, k)]
+            remote(piece, mrecv.at[tp, kv, rows], m_ss.at[n], m_rs.at[n], dev(k))
+            remote(piece, mrecv.at[tp, kv, rows], m_ss.at[n + 1], m_rs.at[n + 1], (grp, peer_of(x, y, k), other))
+        remote(msend.at[kv], mrecv.at[tp, kv, rows], m_ss.at[n + 1], m_rs.at[n + 1], partner)
+        mrecv[tp, kv, rows, :] = msend[kv]
+
     for p in range(8):
-        place(p, weighted(p, kept[p, 1], 0, 128))
-
-    def gather_values(c):
-        _, row, tokens = PIECES[c]
-        for p in range(16):
-            part = weighted(8 + p, fsv[p, row : row + tokens, :], row, row + tokens)
-            if row == 0:
-                pvacc[p] = part
-            else:
-                pvacc[p] = pvacc[p] + part
-
-    gather_values(4)
-    gather_values(5)
-    finish(6)
-    gather_values(6)
-    finish(7)
-    gather_values(7)
-    finish(8)
-    _, row, tokens = PIECES[8]
+        place(eaccs, p, weighted(16 + p, kept[p, 1], 0, 128))
+    swap(eaccs, esend)
+    spread(esend, 16, 2)
     for p in range(16):
-        place(8 + p, pvacc[p] + weighted(8 + p, fsv[p, row : row + tokens, :], row, row + tokens))
-
-    tiles = [accs[h] for h in range(16)]
-    group = lane32 // 8
-    for bit in (1, 2, 4, 8):
-        upper = (group & bit) != 0
-        for h in range(16):
-            if h & bit == 0:
-                a, b = tiles[h], tiles[h + bit]
-                tiles[h] = jnp.where(upper, pltpu.roll(b, 8 * bit, 1), a)
-                tiles[h + bit] = jnp.where(upper, b, pltpu.roll(a, 128 - 8 * bit, 1))
-    for j in range(16):
-        msend[j] = tiles[j].astype(bf16)
-    for k in ORDER[::-1]:
-        piece = msend.at[peer_of(x, y, k)]
-        remote(piece, mrecv.at[tp, kv], m_ss.at[0], m_rs.at[0], dev(k))
-        remote(piece, mrecv.at[tp, kv], m_ss.at[1], m_rs.at[1], (grp, peer_of(x, y, k), other))
-    remote(msend.at[kv], mrecv.at[tp, kv], m_ss.at[1], m_rs.at[1], partner)
-    mrecv[tp, kv] = msend[kv]
+        pvacc[p] = weighted(p, fsv[p, :96, :], 0, 96)
+    finish(nc - 2)
+    finish(nc - 1)
+    for p in range(16):
+        place(accs, p, pvacc[p] + weighted(p, fsv[p, 96:, :], 96, 128))
+    swap(accs, msend)
+    spread(msend, 0, 0)
 
     rho = lax.broadcasted_iota(jnp.int32, (128, 128), 0)
     col = lax.broadcasted_iota(jnp.int32, (128, 128), 1)
@@ -385,24 +387,37 @@
     block = jnp.dot(
         perm, hid_ref[:, pl.ds(pl.multiple_of(tp * 128, 128), 128)], preferred_element_type=f32
     )
-    settle(wpart, wp_rs.at[0])
+    settle(w2.at[pl.ds(0, 128)], w_sem.at[3])
+    settle(w2.at[pl.ds(128, 128)], wp_rs.at[0])
+    settle(esend.at[pl.ds(0, 15)], m_rs.at[2])
+    settle(esend, m_rs.at[3])
     settle(msend.at[pl.ds(0, 15)], m_rs.at[0])
     near = jnp.dot(member, mrecv[tp].reshape(512, 128), preferred_element_type=f32).astype(bf16)
     settle(msend, m_rs.at[1])
     far = jnp.dot(member, mrecv[other].reshape(512, 128), preferred_element_type=f32).astype(bf16)
-    for k in ORDER[::-1] + [0]:
-        dest = peer_of(x, y, k)
-        cols = pl.ds(pl.multiple_of(dest * 256 + tp * 128, 128), 128)
-        total = jnp.dot(near, wout[:, cols], preferred_element_type=f32)
-        total = total + jnp.dot(far, wpart[dest], preferred_element_type=f32)
-        if k == 0:
-            block = block + total
+    slices = jnp.concatenate([near, far], axis=1)
+
+    def share(j, part):
+        rs_send[j] = part.astype(bf16)
+        remote(rs_send.at[j], rs_recv.at[kv], rs_ss.at[0], rs_rs.at[0], (grp, j, tp))
+
+    for dx in (2, 1, 3):
+        row = lax.rem(x + dx, 4)
+        for half in range(2):
+            cols = pl.ds(pl.multiple_of(row * 512 + half * 256, 256), 256)
+            part = jnp.dot(slices, w2[:, cols], preferred_element_type=f32)
+            share(row * 4 + 2 * half, part[:, :128])
+            share(row * 4 + 2 * half + 1, part[:, 128:])
+    for dy in (2, 1, 3, 0):
+        j = x * 4 + lax.rem(y + dy, 4)
+        part = jnp.dot(slices, w2[:, pl.ds(pl.multiple_of(j * 128, 128), 128)], preferred_element_type=f32)
+        if dy:
+            share(j, part)
         else:
-            rs_send[k] = total.astype(bf16)
-            remote(rs_send.at[k], rs_recv.at[k], rs_ss.at[0], rs_rs.at[0], dev(k))
-    settle(rs_recv.at[pl.ds(1, 15)], rs_rs.at[0])
+            block = block + part
+    settle(rs_recv.at[pl.ds(0, 15)], rs_rs.at[0])
     for k in ORDER:
-        block = block + rs_recv[k].astype(f32)
+        block = block + rs_recv[source_of(x, y, k)].astype(f32)
     ag[0, tp] = block.astype(bf16)
 
     def forward(k):
@@ -411,8 +426,8 @@
     forward(0)
     for k in ORDER:
         remote(ag.at[0, tp], ag.at[k, tp], ag_ss.at[0], ag_rs.at[k], dev(k))
+    loads[0].wait()
     loads[1].wait()
-    loads[2].wait()
     seq = [0] + ORDER
     nt = (((1,), (1,)), ((), ()))
     gate = jnp.zeros((128, 448), f32)
@@ -438,7 +453,7 @@
     upward = upward * scale
     hunits[...] = (gate / (1.0 + jnp.exp(-gate)) * upward).astype(bf16)
 
-    loads[3].wait()
+    loads[2].wait()
     for c in range(4):
         cols = pl.ds(c * 1024, 1024)
         part = jnp.dot(hunits[...], wd[:, cols], preferred_element_type=f32)
@@ -467,8 +482,10 @@
     settle(qfb.at[pl.ds(0, 3)], a_ss.at[3])
     settle(stats.at[pl.ds(0, 15)], s_ss.at[0])
     settle(msend.at[pl.ds(0, 15)], m_ss.at[0])
-    settle(wpart, wp_ss.at[0])
+    settle(w2.at[pl.ds(0, 128)], wp_ss.at[0])
     settle(msend, m_ss.at[1])
+    settle(esend.at[pl.ds(0, 15)], m_ss.at[2])
+    settle(esend, m_ss.at[3])
     settle(rs_send.at[pl.ds(1, 15)], rs_ss.at[0])
     settle(rs_send.at[pl.ds(1, 15)], ag_ss.at[0])
     settle(rs_send, fw_ss.at[0])
@@ -531,12 +548,13 @@
             pltpu.VMEM((24, 16, 128), f32),
             pltpu.VMEM((24, 16, 128), f32),
             pltpu.VMEM((16, 16, 512), f32),
-            pltpu.VMEM((16, 32, 128), f32),
+            pltpu.VMEM((16, 16, 128), f32),
+            pltpu.VMEM((16, 16, 128), f32),
             pltpu.VMEM((16, 40, 128), f32),
-            pltpu.VMEM((16, 32, 128), bf16),
+            pltpu.VMEM((16, 16, 128), bf16),
+            pltpu.VMEM((16, 16, 128), bf16),
             pltpu.VMEM((2, 16, 32, 128), bf16),
-            pltpu.VMEM((128, 4096), bf16),
-            pltpu.VMEM((16, 128, 128), bf16),
+            pltpu.VMEM((256, 2048), bf16),
             pltpu.VMEM((448, 4096), bf16),
             pltpu.VMEM((448, 4096), bf16),
             pltpu.VMEM((448, 4096), bf16),
@@ -555,7 +573,7 @@
             dma((2,)), dma((nc,)), dma((1,)), dma((2,)),
             dma((4,)), dma((4,)), dma((4,)), dma((4,)),
             dma((nc,)), dma((nc,)), dma((nc,)), dma((nc,)),
-            dma((1,)), dma((1,)), dma((2,)), dma((2,)),
+            dma((1,)), dma((1,)), dma((4,)), dma((4,)),
             dma((4,)), dma((1,)), dma((1,)), dma((1,)), dma((1,)), dma((1,)), dma((16,)),
             dma((1,)), dma((16,)), dma((1,)), dma((4,)), dma((1,)), dma((1,)),
         ],
@@ -566,16 +584,15 @@
 
 
 def deliver_kernel(mixed_ref, cache_hbm, out_ref, final_hbm, pages, in_sem, out_sem):
-    loads = [pltpu.make_async_copy(cache_hbm.at[i], pages.at[i], in_sem.at[i]) for i in range(16)]
-    stores = [pltpu.make_async_copy(pages.at[i], final_hbm.at[i], out_sem.at[i]) for i in range(16)]
+    loads = [pltpu.make_async_copy(cache_hbm.at[i // 2, i % 2], pages.at[i // 2, i % 2], in_sem.at[i]) for i in range(32)]
+    stores = [pltpu.make_async_copy(pages.at[i // 2, i % 2], final_hbm.at[i // 2, i % 2], out_sem.at[0]) for i in range(32)]
     for load in loads:
         load.start()
     out_ref[...] = mixed_ref[...]
     for load, store in zip(loads, stores):
         load.wait()
         store.start()
-    for store in stores:
-        store.wait()
+    pltpu.make_async_copy(pages, pages, out_sem.at[0]).wait()
 
 
 def deliver(mixed, cache):
@@ -591,7 +608,7 @@
         ),
         in_specs=[vmem, hbm],
         out_specs=(vmem, hbm),
-        scratch_shapes=[pltpu.VMEM(cache.shape, cache.dtype), dma((16,)), dma((16,))],
+        scratch_shapes=[pltpu.VMEM(cache.shape, cache.dtype), dma((32,)), dma((1,))],
         compiler_params=pltpu.CompilerParams(vmem_limit_bytes=62 * 1024 * 1024),
     )(mixed, cache)
 

time: 127 us -> 128 us (level)
  no operation moved by 1% of the time
where the time goes in v9:
time: 128 us
  Pallas kernels  127 us (99%)
    pallas_call x1, Pallas kernels, step(): pl.pallas_call(step_kernel, name='step', out_shape=(jax.ShapeDtypeStruct(...  121 us
    pallas_call x1, Pallas kernels, deliver(): pl.pallas_call(deliver_kernel, name='deliver', out_shape=(jax.ShapeDtypeS...  5.61 us

profile of v9, /device:TPU:1, one launch (start us, length us, event | category | flops | bytes accessed | tf_op | source)
XLA Modules:
  0.0 127.6 jit_solution(15969665593892845567)
XLA Ops:
  0.6 121.4 %step.1 = (bf16[4,4096]{1,0:T(4,128)(2,1)}, bf16[16,2,128,512]{3,2,1,0:T(8,128)(2,1)}) custom-call(s32[1,8]{1,0:T(1,128)} %res_slot.1, s32[1,8]{1,0:T(1,128)} %res_len.1, s32[1,16]{1,0:T(1,128)} %arr_slot.1, s32[1,16]{1,0:T(1,128)} %arr_len.1, s32[4,256]{1,0:T(4,128)} %own_ref.1, s32[4,256]{1,0:T(4,128)} %loc_ref.1, bf16[128,256]{1,0:T(8,128)(2,1)} %hid_ref.1, ...), custom_call_target="tpu_custom_call" | custom-call | tf_op jit(solution)/shard_map/step/pallas_call | solution.py:522
  122.0 5.6 %deliver.1 = (bf16[4,4096]{1,0:T(4,128)(2,1)}, bf16[16,2,128,512]{3,2,1,0:T(8,128)(2,1)}) custom-call(bf16[4,4096]{1,0:T(4,128)(2,1)} %get-tuple-element.6.mixed_ref, bf16[16,2,128,512]{3,2,1,0:T(8,128)(2,1)} %get-tuple-element.7.cache_hbm), custom_call_target="tpu_custom_call" | custom-call | tf_op jit(solution)/shard_map/deliver/pallas_call | solution.py:602

commit v10 on v9

--- a/solution.py
+++ b/solution.py
@@ -30,8 +30,7 @@
 ORDER = sorted(range(1, 16), key=lambda k: (min(k // 4, 4 - k // 4) + min(k % 4, 4 - k % 4), k))
 
 
-PIECES = [(0, 0, 32), (0, 32, 32), (0, 64, 32), (0, 96, 16), (0, 112, 16)]
-PIECES += [(1, 16 * i, 16) for i in range(8)]
+PIECES = [(0, 0, 32), (0, 32, 32), (0, 64, 32), (0, 96, 32), (1, 0, 32), (1, 32, 32), (1, 64, 32), (1, 96, 16), (1, 112, 16)]
 
 
 def step_kernel(
@@ -260,16 +259,15 @@
     query_done()
     xy_start(3)
     z_start(1)
+    finish(0)
     query_spread()
     xy_start(4)
+    z_start(2)
+    finish(1)
     xy_start(5)
-    z_start(2)
-    finish(0)
+    z_start(3)
+    finish(2)
     xy_start(6)
-    xy_start(7)
-    z_start(3)
-    finish(1)
-    xy_start(8)
     tok_load.wait()
     own_key, own_value = tok[:, 0, :].astype(f32), tok[:, 1, :].astype(f32)
     lane8 = lax.broadcasted_iota(i32, (8, 128), 1)
@@ -285,20 +283,16 @@
     for p in range(24):
         slot_row = jnp.where(lane8 == p, arr_slot[0, p] if p < 16 else res_slot[0, p - 16], slot_row)
     slot_row = jnp.where(lane8 >= 24, kv * 8 + lane8 - 24, slot_row)
-    z_start(4)
-    finish(2)
-    xy_start(9)
     settle(qfa.at[:, pl.ds(0, 3)], a_rs.at[2])
     settle(qfb.at[pl.ds(0, 3)], a_rs.at[3])
     kept_load.wait()
     table = jnp.zeros((32, 128), f32)
     for p in range(8):
         table = note(table, 16 + p, *page_scores(16 + p, kept[p, 0], res_slot[0, p], res_len[0, p]))
-    z_start(5)
+    z_start(4)
     finish(3)
-    xy_start(10)
-    z_start(6)
-    finish(4)
+    xy_start(7)
+    xy_start(8)
     for p in range(16):
         table = note(table, p, *page_scores(p, fsk[p], arr_slot[0, p], arr_len[0, p]))
     own_lane = lanes >= 24
@@ -317,11 +311,12 @@
     stats[kv] = mine
     for k in ORDER[::-1]:
         remote(stats.at[kv], stats.at[kv], s_ss.at[0], s_rs.at[0], dev(k))
-    xy_start(11)
-    xy_start(12)
-    for c in range(7, nc):
-        z_start(c)
-        finish(c - 2)
+    z_start(5)
+    finish(4)
+    z_start(6)
+    finish(5)
+    z_start(7)
+    z_start(8)
     settle(stats.at[pl.ds(0, 15)], s_rs.at[0])
     every = jnp.concatenate(
         [stats[4 * i] + stats[4 * i + 1] + stats[4 * i + 2] + stats[4 * i + 3] for i in range(4)], axis=1
@@ -372,9 +367,12 @@
     swap(eaccs, esend)
     spread(esend, 16, 2)
     for p in range(16):
-        pvacc[p] = weighted(p, fsv[p, :96, :], 0, 96)
-    finish(nc - 2)
-    finish(nc - 1)
+        pvacc[p] = weighted(p, fsv[p, :64, :], 0, 64)
+    finish(6)
+    for p in range(16):
+        pvacc[p] = pvacc[p] + weighted(p, fsv[p, 64:96, :], 64, 96)
+    finish(7)
+    finish(8)
     for p in range(16):
         place(accs, p, pvacc[p] + weighted(p, fsv[p, 96:, :], 96, 128))
     swap(accs, msend)
@@ -401,9 +399,9 @@
         rs_send[j] = part.astype(bf16)
         remote(rs_send.at[j], rs_recv.at[kv], rs_ss.at[0], rs_rs.at[0], (grp, j, tp))
 
-    for dx in (2, 1, 3):
-        row = lax.rem(x + dx, 4)
-        for half in range(2):
+    for half in range(2):
+        for dx in (2, 1, 3):
+            row = lax.rem(x + dx, 4)
             cols = pl.ds(pl.multiple_of(row * 512 + half * 256, 256), 256)
             part = jnp.dot(slices, w2[:, cols], preferred_element_type=f32)
             share(row * 4 + 2 * half, part[:, :128])
@@ -584,8 +582,8 @@
 
 
 def deliver_kernel(mixed_ref, cache_hbm, out_ref, final_hbm, pages, in_sem, out_sem):
-    loads = [pltpu.make_async_copy(cache_hbm.at[i // 2, i % 2], pages.at[i // 2, i % 2], in_sem.at[i]) for i in range(32)]
-    stores = [pltpu.make_async_copy(pages.at[i // 2, i % 2], final_hbm.at[i // 2, i % 2], out_sem.at[0]) for i in range(32)]
+    loads = [pltpu.make_async_copy(cache_hbm.at[i], pages.at[i], in_sem.at[i]) for i in range(16)]
+    stores = [pltpu.make_async_copy(pages.at[i], final_hbm.at[i], out_sem.at[0]) for i in range(16)]
     for load in loads:
         load.start()
     out_ref[...] = mixed_ref[...]
@@ -608,7 +606,7 @@
         ),
         in_specs=[vmem, hbm],
         out_specs=(vmem, hbm),
-        scratch_shapes=[pltpu.VMEM(cache.shape, cache.dtype), dma((32,)), dma((1,))],
+        scratch_shapes=[pltpu.VMEM(cache.shape, cache.dtype), dma((16,)), dma((1,))],
         compiler_params=pltpu.CompilerParams(vmem_limit_bytes=62 * 1024 * 1024),
     )(mixed, cache)
 

time: 128 us -> 127 us (level)
  no operation moved by 1% of the time
where the time goes in v10:
time: 127 us
  Pallas kernels  126 us (99%)
    pallas_call x1, Pallas kernels, step(): pl.pallas_call(step_kernel, name='step', out_shape=(jax.ShapeDtypeStruct(...  121 us
    pallas_call x1, Pallas kernels, deliver(): pl.pallas_call(deliver_kernel, name='deliver', out_shape=(jax.ShapeDtypeS...  5.09 us

profile of v10, /device:TPU:1, one launch (start us, length us, event | category | flops | bytes accessed | tf_op | source)
XLA Modules:
  0.0 126.6 jit_solution(6492593332764106613)
XLA Ops:
  0.6 120.8 %step.1 = (bf16[4,4096]{1,0:T(4,128)(2,1)}, bf16[16,2,128,512]{3,2,1,0:T(8,128)(2,1)}) custom-call(s32[1,8]{1,0:T(1,128)} %res_slot.1, s32[1,8]{1,0:T(1,128)} %res_len.1, s32[1,16]{1,0:T(1,128)} %arr_slot.1, s32[1,16]{1,0:T(1,128)} %arr_len.1, s32[4,256]{1,0:T(4,128)} %own_ref.1, s32[4,256]{1,0:T(4,128)} %loc_ref.1, bf16[128,256]{1,0:T(8,128)(2,1)} %hid_ref.1, ...), custom_call_target="tpu_custom_call" | custom-call | tf_op jit(solution)/shard_map/step/pallas_call | solution.py:520
  121.5 5.1 %deliver.1 = (bf16[4,4096]{1,0:T(4,128)(2,1)}, bf16[16,2,128,512]{3,2,1,0:T(8,128)(2,1)}) custom-call(bf16[4,4096]{1,0:T(4,128)(2,1)} %get-tuple-element.6.mixed_ref, bf16[16,2,128,512]{3,2,1,0:T(8,128)(2,1)} %get-tuple-element.7.cache_hbm), custom_call_target="tpu_custom_call" | custom-call | tf_op jit(solution)/shard_map/deliver/pallas_call | solution.py:600

commit v11 on v10

--- a/solution.py
+++ b/solution.py
@@ -35,15 +35,15 @@
 
 def step_kernel(
     res_slot, res_len, arr_slot, arr_len, own_ref, loc_ref, hid_ref, again_ref, gain_ref, tok_hbm, wq_hbm, pool_hbm, res_hbm, wout_hbm, wg_hbm, wu_hbm, wd_hbm,
-    out_ref, cache_hbm,
-    wq, tok, kept, qa1s, qa1r, qa2s, qa2r, qb1s, qb1r, qb2s, qb2r, qfa, qfb, qflat, fsk, fsv, scores, probs, pvacc, accs, eaccs, stats, msend, esend, mrecv,
+    out_ref, cache_ref,
+    wq, tok, kept, qa1s, qa1r, qa2s, qa2r, qb1s, qb1r, qb2s, qb2r, qfa, qfb, qflat, scores, probs, pvacc, accs, eaccs, stats, msend, esend, mrecv,
     w2, wg, wu, wd, rs_send, rs_recv, ag, hunits,
     dp_send, dp_recv, dsum, d_send, d_recv, resrow, picks, *rest,
 ):
     f32, bf16, i32 = jnp.float32, jnp.bfloat16, jnp.int32
     nc = len(PIECES)
     pool, xs, xr, zs, zr = (rest[i * nc : (i + 1) * nc] for i in range(5))
-    (ld_sem, pool_sem, kept_sem, out_sem, q_ss, q_rs, a_ss, a_rs, x_ss, x_rs, z_ss, z_rs, s_ss, s_rs,
+    (ld_sem, pool_sem, kept_sem, q_ss, q_rs, a_ss, a_rs, x_ss, x_rs, z_ss, z_rs, s_ss, s_rs,
      m_ss, m_rs, w_sem, wp_ss, wp_rs, rs_ss, rs_rs, ag_ss, ag_rs, fw_ss, fw_rs, dp_ss, dp_rs, d_ss,
      d_rs) = rest[5 * nc :]
     grp, kv, tp = lax.axis_index("grp"), lax.axis_index("kv"), lax.axis_index("tp")
@@ -168,13 +168,9 @@
     def finish(c):
         settle(zs[c], z_rs.at[c])
         half, row, tokens = PIECES[c]
-        final = (fsk, fsv)[half]
         for i in range(16):
             where = picks[32 + i]
-            final[i, row : row + tokens, :] = zr[c][where // 4, lax.rem(where, 4)]
-        pltpu.make_async_copy(
-            final.at[:, pl.ds(row, tokens), :], cache_hbm.at[:, half, pl.ds(row, tokens), :], out_sem.at[half]
-        ).start()
+            cache_ref[i, half, row : row + tokens, :] = zr[c][where // 4, lax.rem(where, 4)]
 
     head_of = lax.broadcasted_iota(i32, (16, 512), 0) // 4
     block_of = lax.broadcasted_iota(i32, (16, 512), 1) // 128
@@ -294,7 +290,7 @@
     xy_start(7)
     xy_start(8)
     for p in range(16):
-        table = note(table, p, *page_scores(p, fsk[p], arr_slot[0, p], arr_len[0, p]))
+        table = note(table, p, *page_scores(p, cache_ref[p, 0], arr_slot[0, p], arr_len[0, p]))
     own_lane = lanes >= 24
     mine = jnp.concatenate(
         [
@@ -367,14 +363,14 @@
     swap(eaccs, esend)
     spread(esend, 16, 2)
     for p in range(16):
-        pvacc[p] = weighted(p, fsv[p, :64, :], 0, 64)
+        pvacc[p] = weighted(p, cache_ref[p, 1, :64, :], 0, 64)
     finish(6)
     for p in range(16):
-        pvacc[p] = pvacc[p] + weighted(p, fsv[p, 64:96, :], 64, 96)
+        pvacc[p] = pvacc[p] + weighted(p, cache_ref[p, 1, 64:96, :], 64, 96)
     finish(7)
     finish(8)
     for p in range(16):
-        place(accs, p, pvacc[p] + weighted(p, fsv[p, 96:, :], 96, 128))
+        place(accs, p, pvacc[p] + weighted(p, cache_ref[p, 1, 96:, :], 96, 128))
     swap(accs, msend)
     spread(msend, 0, 0)
 
@@ -399,17 +395,10 @@
         rs_send[j] = part.astype(bf16)
         remote(rs_send.at[j], rs_recv.at[kv], rs_ss.at[0], rs_rs.at[0], (grp, j, tp))
 
-    for half in range(2):
-        for dx in (2, 1, 3):
-            row = lax.rem(x + dx, 4)
-            cols = pl.ds(pl.multiple_of(row * 512 + half * 256, 256), 256)
-            part = jnp.dot(slices, w2[:, cols], preferred_element_type=f32)
-            share(row * 4 + 2 * half, part[:, :128])
-            share(row * 4 + 2 * half + 1, part[:, 128:])
-    for dy in (2, 1, 3, 0):
-        j = x * 4 + lax.rem(y + dy, 4)
+    for k in ORDER[::-1] + [0]:
+        j = peer_of(x, y, k)
         part = jnp.dot(slices, w2[:, pl.ds(pl.multiple_of(j * 128, 128), 128)], preferred_element_type=f32)
-        if dy:
+        if k:
             share(j, part)
         else:
             block = block + part
@@ -488,8 +477,6 @@
     settle(rs_send.at[pl.ds(1, 15)], ag_ss.at[0])
     settle(rs_send, fw_ss.at[0])
     settle(dp_send, dp_ss.at[0])
-    settle(fsk, out_sem.at[0])
-    settle(fsv, out_sem.at[1])
     for k in range(16):
         for t in range(2):
             cols = pl.ds(pl.multiple_of((source_of(x, y, k) * 2 + t) * 128, 128), 128)
@@ -521,11 +508,11 @@
         step_kernel,
         name="step",
         out_shape=(
-            jax.ShapeDtypeStruct((4, 4096), bf16),
-            jax.ShapeDtypeStruct((16, 2, 128, 512), bf16),
+            pltpu.VMEM((4, 4096), bf16),
+            pltpu.VMEM((16, 2, 128, 512), bf16),
         ),
         in_specs=[smem] * 4 + [vmem] * 5 + [hbm] * 8,
-        out_specs=(vmem, hbm),
+        out_specs=(vmem, vmem),
         scratch_shapes=[
             pltpu.VMEM((256, 2048), bf16),
             pltpu.VMEM((8, 2, 512), bf16),
@@ -541,8 +528,6 @@
             pltpu.VMEM((4, 4, 8, 8, 128), f32),
             pltpu.VMEM((4, 4, 8, 8, 128), f32),
             pltpu.VMEM((8, 2048), f32),
-            pltpu.VMEM((16, 128, 512), bf16),
-            pltpu.VMEM((16, 128, 512), bf16),
             pltpu.VMEM((24, 16, 128), f32),
             pltpu.VMEM((24, 16, 128), f32),
             pltpu.VMEM((16, 16, 512), f32),
@@ -568,7 +553,7 @@
             pltpu.VMEM((8, 4096), f32),
             pltpu.SMEM((48,), jnp.int32),
             *chunk(16), *chunk(15), *chunk(16), *chunk(3, 4), *chunk(4, 4),
-            dma((2,)), dma((nc,)), dma((1,)), dma((2,)),
+            dma((2,)), dma((nc,)), dma((1,)),
             dma((4,)), dma((4,)), dma((4,)), dma((4,)),
             dma((nc,)), dma((nc,)), dma((nc,)), dma((nc,)),
             dma((1,)), dma((1,)), dma((4,)), dma((4,)),
@@ -576,39 +561,9 @@
             dma((1,)), dma((16,)), dma((1,)), dma((4,)), dma((1,)), dma((1,)),
         ],
         compiler_params=pltpu.CompilerParams(
-            collective_id=0, has_side_effects=True, vmem_limit_bytes=62 * 1024 * 1024
+            collective_id=0, has_side_effects=True, vmem_limit_bytes=58 * 1024 * 1024
         ),
     )(*operands)
-
-
-def deliver_kernel(mixed_ref, cache_hbm, out_ref, final_hbm, pages, in_sem, out_sem):
-    loads = [pltpu.make_async_copy(cache_hbm.at[i], pages.at[i], in_sem.at[i]) for i in range(16)]
-    stores = [pltpu.make_async_copy(pages.at[i], final_hbm.at[i], out_sem.at[0]) for i in range(16)]
-    for load in loads:
-        load.start()
-    out_ref[...] = mixed_ref[...]
-    for load, store in zip(loads, stores):
-        load.wait()
-        store.start()
-    pltpu.make_async_copy(pages, pages, out_sem.at[0]).wait()
-
-
-def deliver(mixed, cache):
-    vmem = pl.BlockSpec(memory_space=pltpu.VMEM)
-    hbm = pl.BlockSpec(memory_space=pl.ANY)
-    dma = pltpu.SemaphoreType.DMA
-    return pl.pallas_call(
-        deliver_kernel,
-        name="deliver",
-        out_shape=(
-            jax.ShapeDtypeStruct(mixed.shape, mixed.dtype),
-            jax.ShapeDtypeStruct(cache.shape, cache.dtype),
-        ),
-        in_specs=[vmem, hbm],
-        out_specs=(vmem, hbm),
-        scratch_shapes=[pltpu.VMEM(cache.shape, cache.dtype), dma((16,)), dma((1,))],
-        compiler_params=pltpu.CompilerParams(vmem_limit_bytes=62 * 1024 * 1024),
-    )(mixed, cache)
 
 
 def per_device(
@@ -649,7 +604,6 @@
         w_up.T,
         w_down,
     )
-    mixed, new_pages = deliver(mixed, new_pages)
     return (mixed, new_pages[None])
 
 

time: 127 us -> 123 us (0.969)
  Pallas kernels: 126 us -> 120 us
  local copies, waits for them, and re-layouts: 0 us -> 2.63 us
    pallas_call x2 -> x1, Pallas kernels: 126 us -> 120 us  [step(): pl.pallas_call(step_kernel, name='step', out_shape=(pltpu.VMEM((4, 4096),...]
    unnamed x0 -> x2, local copies, waits for them, and re-layouts: none -> 2.63 us
where the time goes in v11:
time: 123 us
  Pallas kernels  120 us (98%)
  local copies, waits for them, and re-layouts  2.63 us (2%)
    pallas_call x1, Pallas kernels, step(): pl.pallas_call(step_kernel, name='step', out_shape=(pltpu.VMEM((4, 4096),...  120 us
    unnamed x2, local copies, waits for them, and re-layouts  2.63 us

profile of v11, /device:TPU:1, one launch (start us, length us, event | category | flops | bytes accessed | tf_op | source)
XLA Modules:
  0.0 122.8 jit_solution(10527202407491028334)
XLA Ops:
  0.6 119.5 %step.1 = (bf16[4,4096]{1,0:T(4,128)(2,1)S(1)}, bf16[16,2,128,512]{3,2,1,0:T(8,128)(2,1)S(1)}) custom-call(s32[1,8]{1,0:T(1,128)} %res_slot.1, s32[1,8]{1,0:T(1,128)} %res_len.1, s32[1,16]{1,0:T(1,128)} %arr_slot.1, s32[1,16]{1,0:T(1,128)} %arr_len.1, s32[4,256]{1,0:T(4,128)} %own_ref.1, s32[4,256]{1,0:T(4,128)} %loc_ref.1, bf16[128,256]{1,0:T(8,128)(2,1)} %hid_ref.1, ...), custom_call_target="tpu_custom_call" | custom-call | tf_op jit(solution)/shard_map/step/pallas_call | solution.py:507
  120.2 0.6 copy.21
  120.8 2.0 %copy.22 = bf16[1,16,2,128,512]{4,3,2,1,0:T(8,128)(2,1)} copy(bf16[1,16,2,128,512]{4,3,2,1,0:T(8,128)(2,1)S(1)} %bitcast.8) | data formatting | bytes 8388608
